TPU v7x, 512 devices: a whole 4x8x8 slice. The times are simulated.
512 devices in a mesh: seq: 64 (over z, y), head: 8 (over x, core).
Axes of the slice: x: 4, y: 8, z: 8, core: 2. Of those that a mesh axis runs over, the one named last changes fastest.
Arguments:
- queries: bfloat16 [16384, 32, 128], P('seq', 'head'), may hold values from -8 to 8
- keys: bfloat16 [16384, 8, 128], P('seq', 'head'), may hold values from -8 to 8
- values: bfloat16 [16384, 8, 128], P('seq', 'head'), may hold values from -6 to 6
- out_weight: bfloat16 [4096, 4096], P('head', 'seq'), may hold values from -0.25 to 0.25
- doc_lengths: int32 [64], replicated, may hold values from 1 to 8448, 16384 in all
Outputs:
- projected: bfloat16 [16384, 4096], P('seq', 'head')
Inputs may be any that keep to these rules, and one draw needn't show every extreme that they name: `doc_lengths`: every document is at most 8448 tokens long and the longest is exactly that; the lengths sum to 16384.
All inputs are finite; a program needn't handle non-finite values.
Results may differ from a plain program's by a relative error of at most 0.014.
Values may be sent and summed in bfloat16 or wider, within the bound.
No kernel may reach another device: no remote copies, remote signals or barrier semaphores. Data moves between devices by JAX's collectives and lax.ppermute only.
A program may use at most 64 MiB of HBM per device.

v0:
```python
import math

import jax
import jax.numpy as jnp
from jax import lax
from jax.experimental import pallas as pl
from jax.experimental.pallas import tpu as pltpu
from jax.sharding import PartitionSpec as P


NEG = -1e30


def visit(where_ref, q_ref, starts_ref, block_ref, offsets, accum, top):
    heads, tok, width = q_ref.shape
    factor = math.log2(math.e) / math.sqrt(width)
    span = len(offsets) * tok
    me, first, last_start = where_ref[0], where_ref[1], where_ref[2]

    def process(masked):
        keys = block_ref[:, :tok, :].reshape(span, width)
        vals = block_ref[:, tok:, :].reshape(span, width)
        vals = jnp.concatenate([vals, jnp.ones((span, width), jnp.bfloat16)], axis=1)
        if masked:
            lane = lax.broadcasted_iota(jnp.int32, (1, tok), 1)
            key_pos = jnp.concatenate([lane + (me + offset) * tok for offset in offsets], axis=1)
            query_pos = me * tok + lax.broadcasted_iota(jnp.int32, (tok, 1), 0)
            allowed = (key_pos >= starts_ref[:, :1]) & (key_pos <= query_pos)

        def one_head(h):
            scores = lax.dot_general(
                q_ref[h], keys, (((1,), (1,)), ((), ())), preferred_element_type=jnp.float32
            )
            if masked:
                scores = jnp.where(allowed, scores, NEG)
            old = top[h][:, :1]
            new = jnp.maximum(old, jnp.max(scores, axis=1, keepdims=True))
            weights = jnp.exp2((scores - new) * factor).astype(jnp.bfloat16)
            rescale = jnp.exp2((old - new) * factor)
            accum[h] = accum[h] * rescale + jnp.dot(weights, vals, preferred_element_type=jnp.float32)
            top[h] = jnp.broadcast_to(new, (tok, width))

        if masked:
            pl.loop(0, heads)(one_head)
        else:
            for h in range(heads):
                one_head(h)

    needed = me + max(offsets) >= first
    full = ((me + min(offsets)) * tok >= last_start) & (max(offsets) < 0)
    pl.when(needed & full)(lambda: process(False))
    pl.when(needed & jnp.logical_not(full))(lambda: process(True))


def attend(where, queries, starts, sets, state, weight=None):
    heads, tok, width = queries.shape
    arrays = [array for array, _ in sets]
    offsets = [offset for _, offset in sets]
    count = len(sets)
    state_shapes = [
        jax.ShapeDtypeStruct((heads, tok, 2 * width), jnp.float32),
        jax.ShapeDtypeStruct((heads, tok, width), jnp.float32),
    ]
    vmem = pl.BlockSpec(memory_space=pltpu.VMEM)
    specs = [pl.BlockSpec(memory_space=pltpu.SMEM)] + [vmem] * (2 + count)
    keys_seen = sum(map(len, offsets)) * tok
    cost = pl.CostEstimate(
        flops=4 * heads * tok * keys_seen * width,
        bytes_accessed=4 * keys_seen * width,
        transcendentals=heads * tok * keys_seen,
    )
    limit = pltpu.CompilerParams(vmem_limit_bytes=32 * 1024 * 1024)

    if weight is None:

        def kernel(where_ref, q_ref, starts_ref, *refs):
            blocks = refs[:count]
            accum, top = refs[-2:]
            if state is None:
                accum[...] = jnp.zeros_like(accum)
                top[...] = jnp.full_like(top, NEG)
            for block, offset in zip(blocks, offsets):
                visit(where_ref, q_ref, starts_ref, block, offset, accum, top)

        given = [] if state is None else list(state)
        return pl.pallas_call(
            kernel,
            out_shape=state_shapes,
            in_specs=specs + [vmem] * len(given),
            out_specs=[vmem, vmem],
            input_output_aliases={} if state is None else {3 + count: 0, 4 + count: 1},
            compiler_params=limit,
            cost_estimate=cost,
            name="attend",
        )(where, queries, starts, *arrays, *given)

    cols = weight.shape[0] // 8

    def last(where_ref, q_ref, starts_ref, *refs):
        blocks = refs[:count]
        accum_in, top_in, weight_ref, out_ref, accum, top, wbuf, sem = refs[count:]
        copy = pltpu.make_async_copy(weight_ref, wbuf, sem)
        copy.start()
        accum[...] = accum_in[...]
        top[...] = top_in[...]
        for block, offset in zip(blocks, offsets):
            visit(where_ref, q_ref, starts_ref, block, offset, accum, top)
        attended = jnp.concatenate(
            [(accum[h][:, :width] / accum[h][:, width:]).astype(jnp.bfloat16) for h in range(heads)], axis=1
        )
        copy.wait()
        core = where_ref[3]
        for kept in range(2):
            for x in range(4):
                owner = 2 * x + (core if kept == 0 else 1 - core)
                part = wbuf[pl.ds(pl.multiple_of(owner * cols, cols), cols), :]
                out_ref[kept, x] = lax.dot_general(
                    attended, part, (((1,), (1,)), ((), ())), preferred_element_type=jnp.float32
                ).astype(jnp.bfloat16)

    return pl.pallas_call(
        last,
        out_shape=jax.ShapeDtypeStruct((2, 4, tok, cols), jnp.bfloat16),
        in_specs=specs + [vmem, vmem, pl.BlockSpec(memory_space=pltpu.HBM)],
        out_specs=vmem,
        scratch_shapes=[
            pltpu.VMEM((heads, tok, 2 * width), jnp.float32),
            pltpu.VMEM((heads, tok, width), jnp.float32),
            pltpu.VMEM(weight.shape, jnp.bfloat16),
            pltpu.SemaphoreType.DMA,
        ],
        compiler_params=limit,
        cost_estimate=cost,
        name="finish",
    )(where, queries, starts, *arrays, *state, weight)


def moved(array, steps):
    count = lax.axis_size("seq")
    return lax.ppermute(array, "seq", [(i, (i + steps) % count) for i in range(count)])


def layer(queries, keys, values, out_weight, doc_lengths):
    tok, _, width = queries.shape
    me = lax.axis_index("seq")
    core = lax.axis_index("head") % 2
    weight = lax.all_gather(out_weight.T, "seq", axis=0, tiled=True)

    own = jnp.concatenate([keys.reshape(1, tok, width), values.reshape(1, tok, width)], axis=1)
    column = jnp.concatenate([own] + [moved(own, 8 * a) for a in (1, 2, 3, 4)], axis=0)

    ends = jnp.cumsum(doc_lengths)
    position = me * tok + jnp.arange(tok, dtype=jnp.int32)
    starts = jnp.max(jnp.where(ends[None, :] <= position[:, None], ends[None, :], 0), axis=1)
    where = jnp.stack([me, starts[0] // tok, starts[-1], core]).astype(jnp.int32)
    starts = jnp.broadcast_to(starts[:, None], (tok, 128))
    turned = jnp.transpose(queries, (1, 0, 2))

    sets, state = [(column, [-8 * a for a in range(5)])], None
    up, down = column, column[1:]
    for turn in range(1, 5):
        up = moved(up if turn == 1 else up[:4] if turn < 4 else up[:2], 1)
        down = moved(down if turn < 4 else down[2:], -1)
        state = attend(where, turned, starts, sets, state)
        below = [-turn - 8 * a for a in range(up.shape[0])]
        above = [turn - 8 * a for a in range(5 - down.shape[0], 5)]
        sets = [(up, below), (down, above)]
    partial = attend(where, turned, starts, sets, state, weight)

    other = lax.ppermute(partial[1], "head", [(h, h ^ 1) for h in range(8)])
    both = (partial[0].astype(jnp.float32) + other.astype(jnp.float32)).astype(jnp.bfloat16)
    parts = lax.all_to_all(
        both, "head", 0, 0, axis_index_groups=[[0, 2, 4, 6], [1, 3, 5, 7]], tiled=True
    )
    return jnp.sum(parts.astype(jnp.float32), axis=0).astype(jnp.bfloat16)


def solution(mesh):
    placed = (
        P("seq", "head", None),
        P("seq", "head", None),
        P("seq", "head", None),
        P("head", "seq"),
        P(),
    )
    return jax.shard_map(layer, mesh=mesh, in_specs=placed, out_specs=P("seq", "head"), check_vma=False)
```

profile of v0, /device:TPU:248, one launch (start us, length us, event | category | flops | bytes accessed | tf_op | source)
XLA Modules:
  0.0 190.3 jit_solution(4513593649207485067)
XLA Ops:
  8.2 5.5 %collective-permute-start = (bf16[1,512,128]{2,1,0:T(8,128)(2,1)S(1)}, bf16[1,512,128]{2,1,0:T(8,128)(2,1)S(1)}, u32[]{:S(2)}, u32[]{:S(2)}) collective-permute-start(bf16[1,512,128]{2,1,0:T(8,128)(2,1)S(1)} %get-tuple-element.21), channel_id=1, source_target_pairs={{0,64},{8,72},{16,80},{24,88},{32,96},{40,104},{48,112},{56,120},{... | collective-permute-start | bytes 393224 | tf_op jit(solution)/shard_map/ppermute | solution.py:140
  13.7 4.3 %collective-permute-start.1 = (bf16[1,512,128]{2,1,0:T(8,128)(2,1)S(1)}, bf16[1,512,128]{2,1,0:T(8,128)(2,1)S(1)}, u32[]{:S(2)}, u32[]{:S(2)}) collective-permute-start(bf16[1,512,128]{2,1,0:T(8,128)(2,1)S(1)} %get-tuple-element.21), channel_id=1, source_target_pairs={{0,128},{8,136},{16,144},{24,152},{32,160},{40,168},{48,176},{56,1... | collective-permute-start | bytes 393224 | tf_op jit(solution)/shard_map/ppermute | solution.py:140
  18.0 2.8 %collective-permute-start.2 = (bf16[1,512,128]{2,1,0:T(8,128)(2,1)S(1)}, bf16[1,512,128]{2,1,0:T(8,128)(2,1)S(1)}, u32[]{:S(2)}, u32[]{:S(2)}) collective-permute-start(bf16[1,512,128]{2,1,0:T(8,128)(2,1)S(1)} %get-tuple-element.21), channel_id=1, source_target_pairs={{0,192},{8,200},{16,208},{24,216},{32,224},{40,232},{48,240},{56,2... | collective-permute-start | bytes 393224 | tf_op jit(solution)/shard_map/ppermute | solution.py:140
  20.8 6.0 %collective-permute-start.3 = (bf16[1,512,128]{2,1,0:T(8,128)(2,1)S(1)}, bf16[1,512,128]{2,1,0:T(8,128)(2,1)S(1)}, u32[]{:S(2)}, u32[]{:S(2)}) collective-permute-start(bf16[1,512,128]{2,1,0:T(8,128)(2,1)S(1)} %get-tuple-element.21), channel_id=1, source_target_pairs={{0,256},{8,264},{16,272},{24,280},{32,288},{40,296},{48,304},{56,3... | collective-permute-start | bytes 393224 | tf_op jit(solution)/shard_map/ppermute | solution.py:140
  26.9 6.1 %collective-permute-done.2 = bf16[1,512,128]{2,1,0:T(8,128)(2,1)S(1)} collective-permute-done((bf16[1,512,128]{2,1,0:T(8,128)(2,1)S(1)}, bf16[1,512,128]{2,1,0:T(8,128)(2,1)S(1)}, u32[]{:S(2)}, u32[]{:S(2)}) %collective-permute-start.2) | collective-permute-done | bytes 131104 | tf_op jit(solution)/shard_map/ppermute | solution.py:140
  34.5 5.2 %collective-permute-start.4 = (bf16[5,512,128]{2,1,0:T(8,128)(2,1)S(1)}, bf16[5,512,128]{2,1,0:T(8,128)(2,1)S(1)}, u32[]{:S(2)}, u32[]{:S(2)}) collective-permute-start(bf16[5,512,128]{2,1,0:T(8,128)(2,1)S(1)} %constant_dynamic-update-slice_fusion.refs_0_), channel_id=1, source_target_pairs={{0,8},{8,16},{16,24},{24,32},{32,40},{40,48},{48,56},{56,64},{64,7... | collective-permute-start | bytes 1966088 | tf_op jit(solution)/shard_map/ppermute | solution.py:140
  39.8 1.9 %collective-permute-start.8 = (bf16[4,512,128]{2,1,0:T(8,128)(2,1)S(1)}, bf16[4,512,128]{2,1,0:T(8,128)(2,1)S(1)}, u32[]{:S(2)}, u32[]{:S(2)}) collective-permute-start(bf16[4,512,128]{2,1,0:T(8,128)(2,1)S(1)} %pad_maximum_fusion), channel_id=1, source_target_pairs={{0,504},{8,0},{16,8},{24,16},{32,24},{40,32},{48,40},{56,48},{64,5... | collective-permute-start | bytes 1572872 | tf_op jit(solution)/shard_map/ppermute | solution.py:140
  41.7 17.4 %collective-permute-done.8.refs_1_ = bf16[4,512,128]{2,1,0:T(8,128)(2,1)S(1)} collective-permute-done((bf16[4,512,128]{2,1,0:T(8,128)(2,1)S(1)}, bf16[4,512,128]{2,1,0:T(8,128)(2,1)S(1)}, u32[]{:S(2)}, u32[]{:S(2)}) %collective-permute-start.8) | collective-permute-done | bytes 524320 | tf_op jit(solution)/shard_map/ppermute | solution.py:140
  59.2 1.9 %collective-permute-start.9 = (bf16[4,512,128]{2,1,0:T(8,128)(2,1)S(1)}, bf16[4,512,128]{2,1,0:T(8,128)(2,1)}, u32[]{:S(2)}, u32[]{:S(2)}) collective-permute-start(bf16[4,512,128]{2,1,0:T(8,128)(2,1)S(1)} %collective-permute-done.8.refs_1_), channel_id=1, source_target_pairs={{0,504},{8,0},{16,8},{24,16},{32,24},{40,32},{48,40},{56,48},{64,5... | collective-permute-start | bytes 1572872 | tf_op jit(solution)/shard_map/ppermute | solution.py:140
  61.1 7.2 %collective-permute-start.5 = (bf16[4,512,128]{2,1,0:T(8,128)(2,1)S(1)}, bf16[4,512,128]{2,1,0:T(8,128)(2,1)}, u32[]{:S(2)}, u32[]{:S(2)}) collective-permute-start(bf16[4,512,128]{2,1,0:T(8,128)(2,1)S(1)} %slice.30), channel_id=1, source_target_pairs={{0,8},{8,16},{16,24},{24,32},{32,40},{40,48},{48,56},{56,64},{64,7... | collective-permute-start | bytes 1572872 | tf_op jit(solution)/shard_map/ppermute | solution.py:140
  68.4 11.5 %collective-permute-done.9.refs_1_ = bf16[4,512,128]{2,1,0:T(8,128)(2,1)} collective-permute-done((bf16[4,512,128]{2,1,0:T(8,128)(2,1)S(1)}, bf16[4,512,128]{2,1,0:T(8,128)(2,1)}, u32[]{:S(2)}, u32[]{:S(2)}) %collective-permute-start.9) | collective-permute-done | bytes 524320 | tf_op jit(solution)/shard_map/ppermute | solution.py:140
  81.8 4.9 %collective-permute-done.5.refs_0_ = bf16[4,512,128]{2,1,0:T(8,128)(2,1)} collective-permute-done((bf16[4,512,128]{2,1,0:T(8,128)(2,1)S(1)}, bf16[4,512,128]{2,1,0:T(8,128)(2,1)}, u32[]{:S(2)}, u32[]{:S(2)}) %collective-permute-start.5) | collective-permute-done | bytes 524320 | tf_op jit(solution)/shard_map/ppermute | solution.py:140
  86.7 7.8 %collective-permute-start.6 = (bf16[4,512,128]{2,1,0:T(8,128)(2,1)}, bf16[4,512,128]{2,1,0:T(8,128)(2,1)}, u32[]{:S(2)}, u32[]{:S(2)}) collective-permute-start(bf16[4,512,128]{2,1,0:T(8,128)(2,1)} %collective-permute-done.5.refs_0_), channel_id=1, source_target_pairs={{0,8},{8,16},{16,24},{24,32},{32,40},{40,48},{48,56},{56,64},{64,7... | collective-permute-start | bytes 1572872 | tf_op jit(solution)/shard_map/ppermute | solution.py:140
  100.2 5.5 %attend.4 = (f32[4,256,256]{2,1,0:T(8,128)S(1)}, f32[4,256,128]{2,1,0:T(8,128)S(1)}) custom-call(s32[4]{0:T(128)S(1)} %pad_add_fusion.where_ref, bf16[4,256,128]{2,1,0:T(8,128)(2,1)S(1)} %bitcast.18, s32[256,128]{1,0:T(8,128)S(1)} %broadcast_in_dim.13.starts_ref, bf16[5,512,128]{2,1,0:T(8,128)(2,1)S(1)} %copy-done.4), custom_call_target="tpu_custom_call" | custom-call | flops 671088640 | bytes 655360 | tf_op jit(solution)/shard_map/attend/pallas_call | solution.py:86
  105.7 2.3 %collective-permute-done.10.refs_1_ = bf16[4,512,128]{2,1,0:T(8,128)(2,1)S(1)} collective-permute-done((bf16[4,512,128]{2,1,0:T(8,128)(2,1)}, bf16[4,512,128]{2,1,0:T(8,128)(2,1)S(1)}, u32[]{:S(2)}, u32[]{:S(2)}) %collective-permute-start.10) | collective-permute-done | bytes 524320 | tf_op jit(solution)/shard_map/ppermute | solution.py:140
  111.7 7.2 %collective-permute-start.7 = (bf16[2,512,128]{2,1,0:T(8,128)(2,1)S(1)}, bf16[2,512,128]{2,1,0:T(8,128)(2,1)S(1)}, u32[]{:S(2)}, u32[]{:S(2)}) collective-permute-start(bf16[2,512,128]{2,1,0:T(8,128)(2,1)S(1)} %slice.31), channel_id=1, source_target_pairs={{0,8},{8,16},{16,24},{24,32},{32,40},{40,48},{48,56},{56,64},{64,7... | collective-permute-start | bytes 786440 | tf_op jit(solution)/shard_map/ppermute | solution.py:140
  120.0 9.7 %attend.5 = (f32[4,256,256]{2,1,0:T(8,128)S(1)}, f32[4,256,128]{2,1,0:T(8,128)S(1)}) custom-call(s32[4]{0:T(128)S(1)} %pad_add_fusion.where_ref, bf16[4,256,128]{2,1,0:T(8,128)(2,1)S(1)} %bitcast.19, s32[256,128]{1,0:T(8,128)S(1)} %broadcast_in_dim.13.starts_ref, ...), custom_call_target="tpu_custom_call", output_to_operand_aliasing={{0}: (5, {}), {1}: (6, {})} | custom-call | flops 1207959552 | bytes 1179648 | tf_op jit(solution)/shard_map/attend/pallas_call | solution.py:86
  129.7 9.9 %attend.6 = (f32[4,256,256]{2,1,0:T(8,128)S(1)}, f32[4,256,128]{2,1,0:T(8,128)S(1)}) custom-call(s32[4]{0:T(128)S(1)} %pad_add_fusion.where_ref, bf16[4,256,128]{2,1,0:T(8,128)(2,1)S(1)} %bitcast.20, s32[256,128]{1,0:T(8,128)S(1)} %broadcast_in_dim.13.starts_ref, ...), custom_call_target="tpu_custom_call", output_to_operand_aliasing={{0}: (5, {}), {1}: (6, {})} | custom-call | flops 1073741824 | bytes 1048576 | tf_op jit(solution)/shard_map/attend/pallas_call | solution.py:86
  139.7 9.6 %attend.7 = (f32[4,256,256]{2,1,0:T(8,128)S(1)}, f32[4,256,128]{2,1,0:T(8,128)S(1)}) custom-call(s32[4]{0:T(128)S(1)} %pad_add_fusion.where_ref, bf16[4,256,128]{2,1,0:T(8,128)(2,1)S(1)} %bitcast.21, s32[256,128]{1,0:T(8,128)S(1)} %broadcast_in_dim.13.starts_ref, ...), custom_call_target="tpu_custom_call", output_to_operand_aliasing={{0}: (5, {}), {1}: (6, {})} | custom-call | flops 1073741824 | bytes 1048576 | tf_op jit(solution)/shard_map/attend/pallas_call | solution.py:86
  149.3 2.2 %copy-done = bf16[4096,512]{1,0:T(8,128)(2,1)S(1)} copy-done((bf16[4096,512]{1,0:T(8,128)(2,1)S(1)}, bf16[4096,512]{1,0:T(8,128)(2,1)}, u32[]{:S(2)}) %copy-start) | copy-done | bytes 4194328
  151.5 6.6 %finish.1 = bf16[2,4,256,512]{3,2,1,0:T(8,128)(2,1)S(1)} custom-call(s32[4]{0:T(128)S(1)} %pad_add_fusion.where_ref, bf16[4,256,128]{2,1,0:T(8,128)(2,1)S(1)} %bitcast.22, s32[256,128]{1,0:T(8,128)S(1)} %broadcast_in_dim.13.starts_ref, bf16[2,512,128]{2,1,0:T(8,128)(2,1)S(1)} %collective-permute-done.7.refs_0_, ...), custom_call_target="tpu_custom_call" | custom-call | flops 536870912 | bytes 524288 | tf_op jit(solution)/shard_map/finish/pallas_call | solution.py:121
  158.2 1.9 %collective-permute-start.12 = (bf16[4,256,512]{2,1,0:T(8,128)(2,1)S(1)}, bf16[4,256,512]{2,1,0:T(8,128)(2,1)S(1)}, u32[]{:S(2)}, u32[]{:S(2)}) collective-permute-start(bf16[4,256,512]{2,1,0:T(8,128)(2,1)S(1)} %slice_bitcast_fusion), channel_id=1, source_target_pairs={{0,1},{1,0},{2,3},{3,2},{4,5},{5,4},{6,7},{7,6},{8,9},{9,8},{10,11... | collective-permute-start | bytes 3145736 | tf_op jit(solution)/shard_map/ppermute | solution.py:170
  160.1 2.6 %collective-permute-done.12 = bf16[4,256,512]{2,1,0:T(8,128)(2,1)S(1)} collective-permute-done((bf16[4,256,512]{2,1,0:T(8,128)(2,1)S(1)}, bf16[4,256,512]{2,1,0:T(8,128)(2,1)S(1)}, u32[]{:S(2)}, u32[]{:S(2)}) %collective-permute-start.12) | collective-permute-done | bytes 1048608 | tf_op jit(solution)/shard_map/ppermute | solution.py:170
  163.1 19.5 %all_to_all.5 = bf16[4,256,512]{2,1,0:T(8,128)(2,1)S(1)} all-to-all(bf16[4,256,512]{2,1,0:T(8,128)(2,1)S(1)} %fusion), channel_id=1, replica_groups={{0,2,4,6},{1,3,5,7},{8,10,12,14},{9,11,13,15},{16,18,20,22},{17,19,21,2..., dimensions={0} | all-to-all | bytes 2097152 | tf_op jit(solution)/shard_map/all_to_all | solution.py:172
  (50 shorter events, 14.2 us)
Async XLA Ops:
  6.5 88.0 %copy-start.8 = (s32[64]{0:T(128)S(1)}, s32[64]{0:T(128)}, u32[]{:S(2)}) copy-start(s32[64]{0:T(128)} %param.9) | copy-start | bytes 772
  6.5 91.7 %copy-start.7 = (bf16[256,4,128]{2,1,0:T(4,128)(2,1)S(1)}, bf16[256,4,128]{2,1,0:T(4,128)(2,1)}, u32[]{:S(2)}) copy-start(bf16[256,4,128]{2,1,0:T(4,128)(2,1)} %param.5) | copy-start | bytes 786436
  6.5 142.7 %all-gather.2.cloned.1.call-start = ((), (), s32[]{:S(2)}) async-start(), calls=%async_computation.1 | async-start | bytes 4259840 | tf_op jit(solution)/shard_map/all_gather | solution.py:147
  8.2 18.7 %collective-permute-start = (bf16[1,512,128]{2,1,0:T(8,128)(2,1)S(1)}, bf16[1,512,128]{2,1,0:T(8,128)(2,1)S(1)}, u32[]{:S(2)}, u32[]{:S(2)}) collective-permute-start(bf16[1,512,128]{2,1,0:T(8,128)(2,1)S(1)} %get-tuple-element.21), channel_id=1, source_target_pairs={{0,64},{8,72},{16,80},{24,88},{32,96},{40,104},{48,112},{56,120},{... | collective-permute-start | bytes 393224 | tf_op jit(solution)/shard_map/ppermute | solution.py:140
  13.7 13.2 %collective-permute-start.1 = (bf16[1,512,128]{2,1,0:T(8,128)(2,1)S(1)}, bf16[1,512,128]{2,1,0:T(8,128)(2,1)S(1)}, u32[]{:S(2)}, u32[]{:S(2)}) collective-permute-start(bf16[1,512,128]{2,1,0:T(8,128)(2,1)S(1)} %get-tuple-element.21), channel_id=1, source_target_pairs={{0,128},{8,136},{16,144},{24,152},{32,160},{40,168},{48,176},{56,1... | collective-permute-start | bytes 393224 | tf_op jit(solution)/shard_map/ppermute | solution.py:140
  18.0 15.0 %collective-permute-start.2 = (bf16[1,512,128]{2,1,0:T(8,128)(2,1)S(1)}, bf16[1,512,128]{2,1,0:T(8,128)(2,1)S(1)}, u32[]{:S(2)}, u32[]{:S(2)}) collective-permute-start(bf16[1,512,128]{2,1,0:T(8,128)(2,1)S(1)} %get-tuple-element.21), channel_id=1, source_target_pairs={{0,192},{8,200},{16,208},{24,216},{32,224},{40,232},{48,240},{56,2... | collective-permute-start | bytes 393224 | tf_op jit(solution)/shard_map/ppermute | solution.py:140
  20.8 13.6 %collective-permute-start.3 = (bf16[1,512,128]{2,1,0:T(8,128)(2,1)S(1)}, bf16[1,512,128]{2,1,0:T(8,128)(2,1)S(1)}, u32[]{:S(2)}, u32[]{:S(2)}) collective-permute-start(bf16[1,512,128]{2,1,0:T(8,128)(2,1)S(1)} %get-tuple-element.21), channel_id=1, source_target_pairs={{0,256},{8,264},{16,272},{24,280},{32,288},{40,296},{48,304},{56,3... | collective-permute-start | bytes 393224 | tf_op jit(solution)/shard_map/ppermute | solution.py:140
  34.5 33.9 %copy-start.3 = (bf16[5,512,128]{2,1,0:T(8,128)(2,1)}, bf16[5,512,128]{2,1,0:T(8,128)(2,1)S(1)}, u32[]{:S(2)}) copy-start(bf16[5,512,128]{2,1,0:T(8,128)(2,1)S(1)} %constant_dynamic-update-slice_fusion.refs_0_) | copy-start | bytes 1966084
  34.5 26.6 %collective-permute-start.4 = (bf16[5,512,128]{2,1,0:T(8,128)(2,1)S(1)}, bf16[5,512,128]{2,1,0:T(8,128)(2,1)S(1)}, u32[]{:S(2)}, u32[]{:S(2)}) collective-permute-start(bf16[5,512,128]{2,1,0:T(8,128)(2,1)S(1)} %constant_dynamic-update-slice_fusion.refs_0_), channel_id=1, source_target_pairs={{0,8},{8,16},{16,24},{24,32},{32,40},{40,48},{48,56},{56,64},{64,7... | collective-permute-start | bytes 1966088 | tf_op jit(solution)/shard_map/ppermute | solution.py:140
  39.8 19.4 %collective-permute-start.8 = (bf16[4,512,128]{2,1,0:T(8,128)(2,1)S(1)}, bf16[4,512,128]{2,1,0:T(8,128)(2,1)S(1)}, u32[]{:S(2)}, u32[]{:S(2)}) collective-permute-start(bf16[4,512,128]{2,1,0:T(8,128)(2,1)S(1)} %pad_maximum_fusion), channel_id=1, source_target_pairs={{0,504},{8,0},{16,8},{24,16},{32,24},{40,32},{48,40},{56,48},{64,5... | collective-permute-start | bytes 1572872 | tf_op jit(solution)/shard_map/ppermute | solution.py:140
  59.2 20.8 %copy-start.5 = (bf16[4,512,128]{2,1,0:T(8,128)(2,1)}, bf16[4,512,128]{2,1,0:T(8,128)(2,1)S(1)}, u32[]{:S(2)}) copy-start(bf16[4,512,128]{2,1,0:T(8,128)(2,1)S(1)} %collective-permute-done.8.refs_1_) | copy-start | bytes 1572868
  59.2 20.7 %collective-permute-start.9 = (bf16[4,512,128]{2,1,0:T(8,128)(2,1)S(1)}, bf16[4,512,128]{2,1,0:T(8,128)(2,1)}, u32[]{:S(2)}, u32[]{:S(2)}) collective-permute-start(bf16[4,512,128]{2,1,0:T(8,128)(2,1)S(1)} %collective-permute-done.8.refs_1_), channel_id=1, source_target_pairs={{0,504},{8,0},{16,8},{24,16},{32,24},{40,32},{48,40},{56,48},{64,5... | collective-permute-start | bytes 1572872 | tf_op jit(solution)/shard_map/ppermute | solution.py:140
  61.1 25.6 %collective-permute-start.5 = (bf16[4,512,128]{2,1,0:T(8,128)(2,1)S(1)}, bf16[4,512,128]{2,1,0:T(8,128)(2,1)}, u32[]{:S(2)}, u32[]{:S(2)}) collective-permute-start(bf16[4,512,128]{2,1,0:T(8,128)(2,1)S(1)} %slice.30), channel_id=1, source_target_pairs={{0,8},{8,16},{16,24},{24,32},{32,40},{40,48},{48,56},{56,64},{64,7... | collective-permute-start | bytes 1572872 | tf_op jit(solution)/shard_map/ppermute | solution.py:140
  79.9 28.1 %collective-permute-start.10 = (bf16[4,512,128]{2,1,0:T(8,128)(2,1)}, bf16[4,512,128]{2,1,0:T(8,128)(2,1)S(1)}, u32[]{:S(2)}, u32[]{:S(2)}) collective-permute-start(bf16[4,512,128]{2,1,0:T(8,128)(2,1)} %collective-permute-done.9.refs_1_), channel_id=1, source_target_pairs={{0,504},{8,0},{16,8},{24,16},{32,24},{40,32},{48,40},{56,48},{64,5... | collective-permute-start | bytes 1572872 | tf_op jit(solution)/shard_map/ppermute | solution.py:140
  86.7 24.1 %collective-permute-start.6 = (bf16[4,512,128]{2,1,0:T(8,128)(2,1)}, bf16[4,512,128]{2,1,0:T(8,128)(2,1)}, u32[]{:S(2)}, u32[]{:S(2)}) collective-permute-start(bf16[4,512,128]{2,1,0:T(8,128)(2,1)} %collective-permute-done.5.refs_0_), channel_id=1, source_target_pairs={{0,8},{8,16},{16,24},{24,32},{32,40},{40,48},{48,56},{56,64},{64,7... | collective-permute-start | bytes 1572872 | tf_op jit(solution)/shard_map/ppermute | solution.py:140
  99.1 1.1 copy-start.4
  108.1 0.8 copy-start.1
  108.8 40.4 %collective-permute-start.11 = (bf16[2,512,128]{2,1,0:T(8,128)(2,1)S(1)}, bf16[2,512,128]{2,1,0:T(8,128)(2,1)S(1)}, u32[]{:S(2)}, u32[]{:S(2)}) collective-permute-start(bf16[2,512,128]{2,1,0:T(8,128)(2,1)S(1)} %slice.32), channel_id=1, source_target_pairs={{0,504},{8,0},{16,8},{24,16},{32,24},{40,32},{48,40},{56,48},{64,5... | collective-permute-start | bytes 786440 | tf_op jit(solution)/shard_map/ppermute | solution.py:140
  111.7 37.5 %collective-permute-start.7 = (bf16[2,512,128]{2,1,0:T(8,128)(2,1)S(1)}, bf16[2,512,128]{2,1,0:T(8,128)(2,1)S(1)}, u32[]{:S(2)}, u32[]{:S(2)}) collective-permute-start(bf16[2,512,128]{2,1,0:T(8,128)(2,1)S(1)} %slice.31), channel_id=1, source_target_pairs={{0,8},{8,16},{16,24},{24,32},{32,40},{40,48},{48,56},{56,64},{64,7... | collective-permute-start | bytes 786440 | tf_op jit(solution)/shard_map/ppermute | solution.py:140
  119.0 1.0 copy-start.6
  129.7 10.0 %copy-start.2 = (bf16[4,512,128]{2,1,0:T(8,128)(2,1)S(1)}, bf16[4,512,128]{2,1,0:T(8,128)(2,1)}, u32[]{:S(2)}) copy-start(bf16[4,512,128]{2,1,0:T(8,128)(2,1)} %copy-done.1) | copy-start | bytes 1572868
  149.3 2.2 %copy-start = (bf16[4096,512]{1,0:T(8,128)(2,1)S(1)}, bf16[4096,512]{1,0:T(8,128)(2,1)}, u32[]{:S(2)}) copy-start(bf16[4096,512]{1,0:T(8,128)(2,1)} %all-gather.2.cloned.1.call-done.refs_4_) | copy-start | bytes 12582916
  158.2 4.6 %collective-permute-start.12 = (bf16[4,256,512]{2,1,0:T(8,128)(2,1)S(1)}, bf16[4,256,512]{2,1,0:T(8,128)(2,1)S(1)}, u32[]{:S(2)}, u32[]{:S(2)}) collective-permute-start(bf16[4,256,512]{2,1,0:T(8,128)(2,1)S(1)} %slice_bitcast_fusion), channel_id=1, source_target_pairs={{0,1},{1,0},{2,3},{3,2},{4,5},{5,4},{6,7},{7,6},{8,9},{9,8},{10,11... | collective-permute-start | bytes 3145736 | tf_op jit(solution)/shard_map/ppermute | solution.py:170
Sparse Core Ops, SparseCore 0:
  10.4 100.4 all-gather.1
where the time goes:
time: 191 us; the launch traced here: 190 us
  starting transfers between devices  55.7 us (29%)
  waiting for transfers between devices  47 us (25%)
  Pallas kernels  41.2 us (22%)
  blocking collectives  19.5 us (10%)
  between operations  16.4 us (9%)
  local copies, waits for them, and re-layouts  7.15 us (4%)
  other arithmetic  3.25 us (2%)
    ppermute x12, starting transfers between devices, moved(): lax.ppermute(array, 'seq', [(i, (i + steps) % count) for i in range(count)])  53.8 us
    ppermute x12, waiting for transfers between devices, moved(): lax.ppermute(array, 'seq', [(i, (i + steps) % count) for i in range(count)])  43.7 us
    pallas_call x4, Pallas kernels, attend(): pl.pallas_call(kernel, out_shape=state_shapes, in_specs=specs + [vmem] *...  34.6 us
    all_to_all x1, blocking collectives, layer(): lax.all_to_all(both, 'head', 0, 0, axis_index_groups=[[0, 2, 4, 6], [1, 3...  19.5 us
    pallas_call x1, Pallas kernels, attend(): pl.pallas_call(last, out_shape=jax.ShapeDtypeStruct((2, 4, tok, cols), jn...  6.6 us
    unnamed x22, local copies, waits for them, and re-layouts  5.2 us
  transfers between devices with their start and end apart: 14, of which 7 were waited for; matrix products, arithmetic and copies ran while one was open for 2% of the time, Pallas kernels for 18%

commit v1 on v0

v1 whole, which is shorter than its diff:
```python
import math

import jax
import jax.numpy as jnp
from jax import lax
from jax.experimental import pallas as pl
from jax.experimental.pallas import tpu as pltpu
from jax.sharding import PartitionSpec as P


NEG = -1e30
WIDE = 4


def visit(where_ref, q_ref, starts_ref, block_ref, nearest, accum, top):
    heads, tok, width = q_ref.shape
    factor = math.log2(math.e) / math.sqrt(width)
    count = block_ref.shape[0]
    me, first, last_start = where_ref[0], where_ref[1], where_ref[2]

    def add(keys, vals, allowed):
        vals = jnp.concatenate([vals, jnp.ones(vals.shape, jnp.bfloat16)], axis=1)
        for h in range(heads):
            scores = lax.dot_general(
                q_ref[h], keys, (((1,), (1,)), ((), ())), preferred_element_type=jnp.float32
            )
            if allowed is not None:
                scores = jnp.where(allowed, scores, NEG)
            old = top[h][:, :1]
            new = jnp.maximum(old, jnp.max(scores, axis=1, keepdims=True))
            weights = jnp.exp2((scores - new) * factor).astype(jnp.bfloat16)
            rescale = jnp.exp2((old - new) * factor)
            accum[h] = accum[h] * rescale + jnp.dot(weights, vals, preferred_element_type=jnp.float32)
            top[h] = jnp.broadcast_to(new, (tok, width))

    begin = 0
    if nearest < 0 and count >= WIDE:
        full = (me + nearest - 8 * (WIDE - 1)) * tok >= last_start
        begin = jnp.where(full, WIDE, 0)

        @pl.when(full)
        def _():
            span = WIDE * tok
            keys = block_ref[:WIDE, :tok, :].reshape(span, width)
            add(keys, block_ref[:WIDE, tok:, :].reshape(span, width), None)

    @pl.loop(begin, count)
    def _(k):
        place = me + nearest - 8 * k

        @pl.when((place >= first) & (place >= 0))
        def _():
            key_pos = place * tok + lax.broadcasted_iota(jnp.int32, (1, tok), 1)
            query_pos = me * tok + lax.broadcasted_iota(jnp.int32, (tok, 1), 0)
            allowed = (key_pos >= starts_ref[:, :1]) & (key_pos <= query_pos)
            block = block_ref[k]
            add(block[:tok], block[tok:], allowed)


def attend(where, queries, starts, sets, state, weights=None):
    heads, tok, width = queries.shape
    arrays = [array for array, _ in sets]
    count = len(sets)
    state_shapes = [
        jax.ShapeDtypeStruct((heads, tok, 2 * width), jnp.float32),
        jax.ShapeDtypeStruct((heads, tok, width), jnp.float32),
    ]
    vmem = pl.BlockSpec(memory_space=pltpu.VMEM)
    specs = [pl.BlockSpec(memory_space=pltpu.SMEM)] + [vmem] * (2 + count)
    keys_seen = sum(array.shape[0] for array in arrays) * tok
    cost = pl.CostEstimate(
        flops=4 * heads * tok * keys_seen * width,
        bytes_accessed=4 * keys_seen * width,
        transcendentals=heads * tok * keys_seen,
    )
    limit = pltpu.CompilerParams(vmem_limit_bytes=32 * 1024 * 1024)

    def visit_all(where_ref, q_ref, starts_ref, blocks, accum, top):
        for block, (_, nearest) in zip(blocks, sets):
            visit(where_ref, q_ref, starts_ref, block, nearest, accum, top)

    if weights is None:

        def kernel(where_ref, q_ref, starts_ref, *refs):
            accum, top = refs[-2:]
            if state is None:
                accum[...] = jnp.zeros_like(accum)
                top[...] = jnp.full_like(top, NEG)
            visit_all(where_ref, q_ref, starts_ref, refs[:count], accum, top)

        given = [] if state is None else list(state)
        return pl.pallas_call(
            kernel,
            out_shape=state_shapes,
            in_specs=specs + [vmem] * len(given),
            out_specs=[vmem, vmem],
            input_output_aliases={} if state is None else {3 + count: 0, 4 + count: 1},
            compiler_params=limit,
            cost_estimate=cost,
            name="attend",
        )(where, queries, starts, *arrays, *given)

    cols = weights[0][0].shape[0]

    def last(where_ref, q_ref, starts_ref, *refs):
        accum_in, top_in, *weight_refs = refs[count:-3]
        out_ref, accum, top = refs[-3:]
        accum[...] = accum_in[...]
        top[...] = top_in[...]
        visit_all(where_ref, q_ref, starts_ref, refs[:count], accum, top)
        attended = jnp.concatenate(
            [(accum[h][:, :width] / accum[h][:, width:]).astype(jnp.bfloat16) for h in range(heads)], axis=1
        )
        core, plane = where_ref[3], where_ref[4]
        for weight_ref, (_, distance) in zip(weight_refs, weights):
            owner = lax.rem(plane + 8 - distance, 8)
            sent = jnp.bitwise_xor(owner & 1, core)
            out_ref[sent, owner >> 1] = lax.dot_general(
                attended, weight_ref[...], (((1,), (1,)), ((), ())), preferred_element_type=jnp.float32
            ).astype(jnp.bfloat16)

    return pl.pallas_call(
        last,
        out_shape=jax.ShapeDtypeStruct((2, 4, tok, cols), jnp.bfloat16),
        in_specs=specs + [vmem] * (2 + len(weights)),
        out_specs=vmem,
        scratch_shapes=[pltpu.VMEM(shape.shape, jnp.float32) for shape in state_shapes],
        compiler_params=limit,
        cost_estimate=cost,
        name="finish",
    )(where, queries, starts, *arrays, *state, *[weight for weight, _ in weights])


def moved(array, steps):
    count = lax.axis_size("seq")
    return lax.ppermute(array, "seq", [(i, (i + steps) % count) for i in range(count)])


def layer(queries, keys, values, out_weight, doc_lengths):
    tok, _, width = queries.shape
    me = lax.axis_index("seq")
    core = lax.axis_index("head") % 2

    own = jnp.concatenate([keys.reshape(1, tok, width), values.reshape(1, tok, width)], axis=1)
    near = moved(own, 8)
    far = moved(own, 32)
    two = jnp.concatenate([own, near], axis=0)
    double = moved(two, 16)
    turned = out_weight.T
    weight = lax.all_to_all(
        jnp.broadcast_to(turned[None], (8,) + turned.shape),
        "seq",
        0,
        0,
        axis_index_groups=[[8 * z + y for y in range(8)] for z in range(8)],
        tiled=True,
    ).reshape(8 * turned.shape[0], turned.shape[1])
    column = jnp.concatenate([two, double, far], axis=0)

    ends = jnp.cumsum(doc_lengths)
    position = me * tok + jnp.arange(tok, dtype=jnp.int32)
    starts = jnp.max(jnp.where(ends[None, :] <= position[:, None], ends[None, :], 0), axis=1)
    where = jnp.stack([me, starts[0] // tok, starts[-1], core, me // 8]).astype(jnp.int32)
    starts = jnp.broadcast_to(starts[:, None], (tok, 128))
    queries = jnp.transpose(queries, (1, 0, 2))

    weights = [(weight, 0)]
    ahead = behind = weight
    sets, state = [(column, 0)], None
    up, down = column, column[1:]
    for turn in range(1, 5):
        up = moved(up if turn == 1 else up[:4] if turn < 4 else up[:2], 1)
        down = moved(down if turn < 4 else down[2:], -1)
        ahead = moved(ahead, 8)
        weights.append((ahead, turn))
        if turn < 4:
            behind = moved(behind, -8)
            weights.append((behind, 8 - turn))
        state = attend(where, queries, starts, sets, state)
        sets = [(up, -turn), (down, turn - 8 * (5 - down.shape[0]))]
    partial = attend(where, queries, starts, sets, state, weights)

    other = lax.ppermute(partial[1], "head", [(h, h ^ 1) for h in range(8)])
    both = (partial[0].astype(jnp.float32) + other.astype(jnp.float32)).astype(jnp.bfloat16)
    parts = lax.all_to_all(
        both, "head", 0, 0, axis_index_groups=[[0, 2, 4, 6], [1, 3, 5, 7]], tiled=True
    )
    return jnp.sum(parts.astype(jnp.float32), axis=0).astype(jnp.bfloat16)


def solution(mesh):
    placed = (
        P("seq", "head", None),
        P("seq", "head", None),
        P("seq", "head", None),
        P("head", "seq"),
        P(),
    )
    return jax.shard_map(layer, mesh=mesh, in_specs=placed, out_specs=P("seq", "head"), check_vma=False)
```

time: 191 us -> 218 us (1.14)
  the two profiles are of different devices: /device:TPU:248 before, /device:TPU:320 now
where the time goes in v1:
time: 218 us; the launch traced here: 217 us
  starting transfers between devices  65.6 us (30%)
  Pallas kernels  61.8 us (28%)
  waiting for transfers between devices  58.6 us (27%)
  blocking collectives  19.5 us (9%)
  local copies, waits for them, and re-layouts  7.12 us (3%)
  between operations  3 us (1%)
    ppermute x18, starting transfers between devices, moved(): lax.ppermute(array, 'seq', [(i, (i + steps) % count) for i in range(count)])  56.6 us
    pallas_call x4, Pallas kernels, attend(): pl.pallas_call(kernel, out_shape=state_shapes, in_specs=specs + [vmem] *...  52.5 us
    ppermute x18, waiting for transfers between devices, moved(): lax.ppermute(array, 'seq', [(i, (i + steps) % count) for i in range(count)])  52.4 us
    all_to_all x1, blocking collectives, layer(): lax.all_to_all(both, 'head', 0, 0, axis_index_groups=[[0, 2, 4, 6], [1, 3...  19.5 us
    pallas_call x1, Pallas kernels, attend(): pl.pallas_call(last, out_shape=jax.ShapeDtypeStruct((2, 4, tok, cols), jn...  9.24 us
    all_to_all x1, starting transfers between devices, layer(): lax.all_to_all(jnp.broadcast_to(turned[None], (8,) + turned.shape), 'seq'...  7.1 us
  transfers between devices with their start and end apart: 20, of which 8 were waited for; matrix products, arithmetic and copies ran while one was open for 2% of the time, Pallas kernels for 24%

profile of v1, /device:TPU:320, one launch (start us, length us, event | category | flops | bytes accessed | tf_op | source)
XLA Modules:
  0.0 217.3 jit_solution(10667023253814028382)
XLA Ops:
  1.7 7.1 %all-to-all-start = ((bf16[8,64,512]{2,1,0:T(8,128)(2,1)}), bf16[8,64,512]{2,1,0:T(8,128)(2,1)S(1)}, u32[]{:S(2)}, u32[]{:S(2)}) async-start(bf16[8,64,512]{2,1,0:T(8,128)(2,1)} %broadcast_in_dim.16), calls=%async_computation | async-start | bytes 1048576 | tf_op jit(solution)/shard_map/all_to_all | solution.py:150
  8.9 3.4 %collective-permute-start = (bf16[1,512,128]{2,1,0:T(8,128)(2,1)S(1)}, bf16[1,512,128]{2,1,0:T(8,128)(2,1)S(1)}, u32[]{:S(2)}, u32[]{:S(2)}) collective-permute-start(bf16[1,512,128]{2,1,0:T(8,128)(2,1)S(1)} %pad_maximum_fusion.3), channel_id=1, source_target_pairs={{0,64},{8,72},{16,80},{24,88},{32,96},{40,104},{48,112},{56,120},{... | collective-permute-start | bytes 393224 | tf_op jit(solution)/shard_map/ppermute | solution.py:136
  12.3 3.5 %collective-permute-done = bf16[1,512,128]{2,1,0:T(8,128)(2,1)S(1)} collective-permute-done((bf16[1,512,128]{2,1,0:T(8,128)(2,1)S(1)}, bf16[1,512,128]{2,1,0:T(8,128)(2,1)S(1)}, u32[]{:S(2)}, u32[]{:S(2)}) %collective-permute-start) | collective-permute-done | bytes 131104 | tf_op jit(solution)/shard_map/ppermute | solution.py:136
  15.7 4.3 %collective-permute-start.1 = (bf16[2,512,128]{2,1,0:T(8,128)(2,1)S(1)}, bf16[2,512,128]{2,1,0:T(8,128)(2,1)S(1)}, u32[]{:S(2)}, u32[]{:S(2)}) collective-permute-start(bf16[2,512,128]{2,1,0:T(8,128)(2,1)S(1)} %pad_maximum_fusion.2), channel_id=1, source_target_pairs={{0,128},{8,136},{16,144},{24,152},{32,160},{40,168},{48,176},{56,1... | collective-permute-start | bytes 786440 | tf_op jit(solution)/shard_map/ppermute | solution.py:136
  22.7 3.6 %all-to-all-done = bf16[8,64,512]{2,1,0:T(8,128)(2,1)S(1)} async-done(((bf16[8,64,512]{2,1,0:T(8,128)(2,1)}), bf16[8,64,512]{2,1,0:T(8,128)(2,1)S(1)}, u32[]{:S(2)}, u32[]{:S(2)}) %all-to-all-start) | async-done | bytes 524320 | tf_op jit(solution)/shard_map/all_to_all | solution.py:150
  26.3 3.4 %collective-permute-start.11 = (bf16[512,512]{1,0:T(8,128)(2,1)S(1)}, bf16[512,512]{1,0:T(8,128)(2,1)S(1)}, u32[]{:S(2)}, u32[]{:S(2)}) collective-permute-start(bf16[512,512]{1,0:T(8,128)(2,1)S(1)} %bitcast.20), channel_id=1, source_target_pairs={{0,64},{8,72},{16,80},{24,88},{32,96},{40,104},{48,112},{56,120},{... | collective-permute-start | bytes 1572872 | tf_op jit(solution)/shard_map/ppermute | solution.py:136
  32.2 6.6 %collective-permute-done.1 = bf16[2,512,128]{2,1,0:T(8,128)(2,1)S(1)} collective-permute-done((bf16[2,512,128]{2,1,0:T(8,128)(2,1)S(1)}, bf16[2,512,128]{2,1,0:T(8,128)(2,1)S(1)}, u32[]{:S(2)}, u32[]{:S(2)}) %collective-permute-start.1) | collective-permute-done | bytes 262176 | tf_op jit(solution)/shard_map/ppermute | solution.py:136
  38.8 3.6 %collective-permute-start.3 = (bf16[5,512,128]{2,1,0:T(8,128)(2,1)S(1)}, bf16[5,512,128]{2,1,0:T(8,128)(2,1)S(1)}, u32[]{:S(2)}, u32[]{:S(2)}) collective-permute-start(bf16[5,512,128]{2,1,0:T(8,128)(2,1)S(1)} %pad_maximum_fusion.refs_0_), channel_id=1, source_target_pairs={{0,8},{8,16},{16,24},{24,32},{32,40},{40,48},{48,56},{56,64},{64,7... | collective-permute-start | bytes 1966088 | tf_op jit(solution)/shard_map/ppermute | solution.py:136
  42.5 4.4 %collective-permute-start.7 = (bf16[4,512,128]{2,1,0:T(8,128)(2,1)S(1)}, bf16[4,512,128]{2,1,0:T(8,128)(2,1)S(1)}, u32[]{:S(2)}, u32[]{:S(2)}) collective-permute-start(bf16[4,512,128]{2,1,0:T(8,128)(2,1)S(1)} %pad_maximum_fusion.1), channel_id=1, source_target_pairs={{0,504},{8,0},{16,8},{24,16},{32,24},{40,32},{48,40},{56,48},{64,5... | collective-permute-start | bytes 1572872 | tf_op jit(solution)/shard_map/ppermute | solution.py:136
  49.5 12.5 %collective-permute-done.11.refs_5_ = bf16[512,512]{1,0:T(8,128)(2,1)S(1)} collective-permute-done((bf16[512,512]{1,0:T(8,128)(2,1)S(1)}, bf16[512,512]{1,0:T(8,128)(2,1)S(1)}, u32[]{:S(2)}, u32[]{:S(2)}) %collective-permute-start.11) | collective-permute-done | bytes 524320 | tf_op jit(solution)/shard_map/ppermute | solution.py:136
  62.0 3.4 %collective-permute-start.13 = (bf16[512,512]{1,0:T(8,128)(2,1)S(1)}, bf16[512,512]{1,0:T(8,128)(2,1)S(1)}, u32[]{:S(2)}, u32[]{:S(2)}) collective-permute-start(bf16[512,512]{1,0:T(8,128)(2,1)S(1)} %collective-permute-done.11.refs_5_), channel_id=1, source_target_pairs={{0,64},{8,72},{16,80},{24,88},{32,96},{40,104},{48,112},{56,120},{... | collective-permute-start | bytes 1572872 | tf_op jit(solution)/shard_map/ppermute | solution.py:136
  68.2 3.9 %collective-permute-start.4 = (bf16[4,512,128]{2,1,0:T(8,128)(2,1)S(1)}, bf16[4,512,128]{2,1,0:T(8,128)(2,1)}, u32[]{:S(2)}, u32[]{:S(2)}) collective-permute-start(bf16[4,512,128]{2,1,0:T(8,128)(2,1)S(1)} %slice.30), channel_id=1, source_target_pairs={{0,8},{8,16},{16,24},{24,32},{32,40},{40,48},{48,56},{56,64},{64,7... | collective-permute-start | bytes 1572872 | tf_op jit(solution)/shard_map/ppermute | solution.py:136
  74.6 13.7 %collective-permute-done.13.refs_7_ = bf16[512,512]{1,0:T(8,128)(2,1)S(1)} collective-permute-done((bf16[512,512]{1,0:T(8,128)(2,1)S(1)}, bf16[512,512]{1,0:T(8,128)(2,1)S(1)}, u32[]{:S(2)}, u32[]{:S(2)}) %collective-permute-start.13) | collective-permute-done | bytes 524320 | tf_op jit(solution)/shard_map/ppermute | solution.py:136
  88.3 3.3 %collective-permute-start.15 = (bf16[512,512]{1,0:T(8,128)(2,1)S(1)}, bf16[512,512]{1,0:T(8,128)(2,1)}, u32[]{:S(2)}, u32[]{:S(2)}) collective-permute-start(bf16[512,512]{1,0:T(8,128)(2,1)S(1)} %collective-permute-done.13.refs_7_), channel_id=1, source_target_pairs={{0,64},{8,72},{16,80},{24,88},{32,96},{40,104},{48,112},{56,120},{... | collective-permute-start | bytes 1572872 | tf_op jit(solution)/shard_map/ppermute | solution.py:136
  93.6 3.9 %collective-permute-start.5 = (bf16[4,512,128]{2,1,0:T(8,128)(2,1)}, bf16[4,512,128]{2,1,0:T(8,128)(2,1)}, u32[]{:S(2)}, u32[]{:S(2)}) collective-permute-start(bf16[4,512,128]{2,1,0:T(8,128)(2,1)} %collective-permute-done.4.refs_0_), channel_id=1, source_target_pairs={{0,8},{8,16},{16,24},{24,32},{32,40},{40,48},{48,56},{56,64},{64,7... | collective-permute-start | bytes 1572872 | tf_op jit(solution)/shard_map/ppermute | solution.py:136
  97.8 3.4 %collective-permute-start.16 = (bf16[512,512]{1,0:T(8,128)(2,1)S(1)}, bf16[512,512]{1,0:T(8,128)(2,1)}, u32[]{:S(2)}, u32[]{:S(2)}) collective-permute-start(bf16[512,512]{1,0:T(8,128)(2,1)S(1)} %collective-permute-done.14.refs_8_), channel_id=1, source_target_pairs={{0,448},{8,456},{16,464},{24,472},{32,480},{40,488},{48,496},{56,5... | collective-permute-start | bytes 1572872 | tf_op jit(solution)/shard_map/ppermute | solution.py:136
  101.3 13.7 %collective-permute-done.15.refs_9_ = bf16[512,512]{1,0:T(8,128)(2,1)} collective-permute-done((bf16[512,512]{1,0:T(8,128)(2,1)S(1)}, bf16[512,512]{1,0:T(8,128)(2,1)}, u32[]{:S(2)}, u32[]{:S(2)}) %collective-permute-start.15) | collective-permute-done | bytes 524320 | tf_op jit(solution)/shard_map/ppermute | solution.py:136
  122.3 8.7 %attend.4 = (f32[4,256,256]{2,1,0:T(8,128)S(1)}, f32[4,256,128]{2,1,0:T(8,128)S(1)}) custom-call(s32[5]{0:T(128)S(1)} %stack.19.where_ref, bf16[4,256,128]{2,1,0:T(8,128)(2,1)S(1)} %bitcast.23, s32[256,128]{1,0:T(8,128)S(1)} %broadcast_in_dim.15.starts_ref, bf16[5,512,128]{2,1,0:T(8,128)(2,1)S(1)} %pad_maximum_fusion.refs_0_), custom_call_target="tpu_custom_call" | custom-call | flops 671088640 | bytes 655360 | tf_op jit(solution)/shard_map/attend/pallas_call | solution.py:92
  134.9 3.9 %collective-permute-start.6 = (bf16[2,512,128]{2,1,0:T(8,128)(2,1)S(1)}, bf16[2,512,128]{2,1,0:T(8,128)(2,1)S(1)}, u32[]{:S(2)}, u32[]{:S(2)}) collective-permute-start(bf16[2,512,128]{2,1,0:T(8,128)(2,1)S(1)} %slice.31), channel_id=1, source_target_pairs={{0,8},{8,16},{16,24},{24,32},{32,40},{40,48},{48,56},{56,64},{64,7... | collective-permute-start | bytes 786440 | tf_op jit(solution)/shard_map/ppermute | solution.py:136
  138.8 15.1 %attend.5 = (f32[4,256,256]{2,1,0:T(8,128)S(1)}, f32[4,256,128]{2,1,0:T(8,128)S(1)}) custom-call(s32[5]{0:T(128)S(1)} %stack.19.where_ref, bf16[4,256,128]{2,1,0:T(8,128)(2,1)S(1)} %bitcast.24, s32[256,128]{1,0:T(8,128)S(1)} %broadcast_in_dim.15.starts_ref, bf16[5,512,128]{2,1,0:T(8,128)(2,1)S(1)} %copy-done.1, ...), custom_call_target="tpu_custom_call", output_to_operand_aliasing={{0}: (5, {}), {1}: (6, {})} | custom-call | flops 1207959552 | bytes 1179648 | tf_op jit(solution)/shard_map/attend/pallas_call | solution.py:92
  153.9 14.3 %attend.6 = (f32[4,256,256]{2,1,0:T(8,128)S(1)}, f32[4,256,128]{2,1,0:T(8,128)S(1)}) custom-call(s32[5]{0:T(128)S(1)} %stack.19.where_ref, bf16[4,256,128]{2,1,0:T(8,128)(2,1)S(1)} %bitcast.25, s32[256,128]{1,0:T(8,128)S(1)} %broadcast_in_dim.15.starts_ref, ...), custom_call_target="tpu_custom_call", output_to_operand_aliasing={{0}: (5, {}), {1}: (6, {})} | custom-call | flops 1073741824 | bytes 1048576 | tf_op jit(solution)/shard_map/attend/pallas_call | solution.py:92
  168.3 14.4 %attend.7 = (f32[4,256,256]{2,1,0:T(8,128)S(1)}, f32[4,256,128]{2,1,0:T(8,128)S(1)}) custom-call(s32[5]{0:T(128)S(1)} %stack.19.where_ref, bf16[4,256,128]{2,1,0:T(8,128)(2,1)S(1)} %bitcast.26, s32[256,128]{1,0:T(8,128)S(1)} %broadcast_in_dim.15.starts_ref, ...), custom_call_target="tpu_custom_call", output_to_operand_aliasing={{0}: (5, {}), {1}: (6, {})} | custom-call | flops 1073741824 | bytes 1048576 | tf_op jit(solution)/shard_map/attend/pallas_call | solution.py:92
  182.7 9.2 %finish.1 = bf16[2,4,256,512]{3,2,1,0:T(8,128)(2,1)S(1)} custom-call(s32[5]{0:T(128)S(1)} %stack.19.where_ref, bf16[4,256,128]{2,1,0:T(8,128)(2,1)S(1)} %bitcast.27, s32[256,128]{1,0:T(8,128)S(1)} %broadcast_in_dim.15.starts_ref, bf16[2,512,128]{2,1,0:T(8,128)(2,1)S(1)} %collective-permute-done.6.refs_0_, ...), custom_call_target="tpu_custom_call" | custom-call | flops 536870912 | bytes 524288 | tf_op jit(solution)/shard_map/finish/pallas_call | solution.py:122
  196.9 19.5 %all_to_all.10 = bf16[4,256,512]{2,1,0:T(8,128)(2,1)S(1)} all-to-all(bf16[4,256,512]{2,1,0:T(8,128)(2,1)S(1)} %fusion), channel_id=1, replica_groups={{0,2,4,6},{1,3,5,7},{8,10,12,14},{9,11,13,15},{16,18,20,22},{17,19,21,2..., dimensions={0} | all-to-all | bytes 2097152 | tf_op jit(solution)/shard_map/all_to_all | solution.py:185
  (56 shorter events, 31.5 us)
Async XLA Ops:
  1.7 24.6 %all-to-all-start = ((bf16[8,64,512]{2,1,0:T(8,128)(2,1)}), bf16[8,64,512]{2,1,0:T(8,128)(2,1)S(1)}, u32[]{:S(2)}, u32[]{:S(2)}) async-start(bf16[8,64,512]{2,1,0:T(8,128)(2,1)} %broadcast_in_dim.16), calls=%async_computation | async-start | bytes 1048576 | tf_op jit(solution)/shard_map/all_to_all | solution.py:150
  8.9 6.9 %collective-permute-start = (bf16[1,512,128]{2,1,0:T(8,128)(2,1)S(1)}, bf16[1,512,128]{2,1,0:T(8,128)(2,1)S(1)}, u32[]{:S(2)}, u32[]{:S(2)}) collective-permute-start(bf16[1,512,128]{2,1,0:T(8,128)(2,1)S(1)} %pad_maximum_fusion.3), channel_id=1, source_target_pairs={{0,64},{8,72},{16,80},{24,88},{32,96},{40,104},{48,112},{56,120},{... | collective-permute-start | bytes 393224 | tf_op jit(solution)/shard_map/ppermute | solution.py:136
  15.7 23.0 %collective-permute-start.1 = (bf16[2,512,128]{2,1,0:T(8,128)(2,1)S(1)}, bf16[2,512,128]{2,1,0:T(8,128)(2,1)S(1)}, u32[]{:S(2)}, u32[]{:S(2)}) collective-permute-start(bf16[2,512,128]{2,1,0:T(8,128)(2,1)S(1)} %pad_maximum_fusion.2), channel_id=1, source_target_pairs={{0,128},{8,136},{16,144},{24,152},{32,160},{40,168},{48,176},{56,1... | collective-permute-start | bytes 786440 | tf_op jit(solution)/shard_map/ppermute | solution.py:136
  20.0 12.2 %collective-permute-start.2 = (bf16[1,512,128]{2,1,0:T(8,128)(2,1)S(1)}, bf16[1,512,128]{2,1,0:T(8,128)(2,1)S(1)}, u32[]{:S(2)}, u32[]{:S(2)}) collective-permute-start(bf16[1,512,128]{2,1,0:T(8,128)(2,1)S(1)} %pad_maximum_fusion.3), channel_id=1, source_target_pairs={{0,256},{8,264},{16,272},{24,280},{32,288},{40,296},{48,304},{56,3... | collective-permute-start | bytes 393224 | tf_op jit(solution)/shard_map/ppermute | solution.py:136
  26.3 35.7 %collective-permute-start.11 = (bf16[512,512]{1,0:T(8,128)(2,1)S(1)}, bf16[512,512]{1,0:T(8,128)(2,1)S(1)}, u32[]{:S(2)}, u32[]{:S(2)}) collective-permute-start(bf16[512,512]{1,0:T(8,128)(2,1)S(1)} %bitcast.20), channel_id=1, source_target_pairs={{0,64},{8,72},{16,80},{24,88},{32,96},{40,104},{48,112},{56,120},{... | collective-permute-start | bytes 1572872 | tf_op jit(solution)/shard_map/ppermute | solution.py:136
  38.8 58.7 %copy-start.6 = (s32[64]{0:T(128)S(1)}, s32[64]{0:T(128)}, u32[]{:S(2)}) copy-start(s32[64]{0:T(128)} %param.9) | copy-start | bytes 772
  38.8 29.3 %collective-permute-start.3 = (bf16[5,512,128]{2,1,0:T(8,128)(2,1)S(1)}, bf16[5,512,128]{2,1,0:T(8,128)(2,1)S(1)}, u32[]{:S(2)}, u32[]{:S(2)}) collective-permute-start(bf16[5,512,128]{2,1,0:T(8,128)(2,1)S(1)} %pad_maximum_fusion.refs_0_), channel_id=1, source_target_pairs={{0,8},{8,16},{16,24},{24,32},{32,40},{40,48},{48,56},{56,64},{64,7... | collective-permute-start | bytes 1966088 | tf_op jit(solution)/shard_map/ppermute | solution.py:136
  42.5 22.9 %collective-permute-start.7 = (bf16[4,512,128]{2,1,0:T(8,128)(2,1)S(1)}, bf16[4,512,128]{2,1,0:T(8,128)(2,1)S(1)}, u32[]{:S(2)}, u32[]{:S(2)}) collective-permute-start(bf16[4,512,128]{2,1,0:T(8,128)(2,1)S(1)} %pad_maximum_fusion.1), channel_id=1, source_target_pairs={{0,504},{8,0},{16,8},{24,16},{32,24},{40,32},{48,40},{56,48},{64,5... | collective-permute-start | bytes 1572872 | tf_op jit(solution)/shard_map/ppermute | solution.py:136
  46.9 25.2 %collective-permute-start.12 = (bf16[512,512]{1,0:T(8,128)(2,1)S(1)}, bf16[512,512]{1,0:T(8,128)(2,1)S(1)}, u32[]{:S(2)}, u32[]{:S(2)}) collective-permute-start(bf16[512,512]{1,0:T(8,128)(2,1)S(1)} %bitcast.21), channel_id=1, source_target_pairs={{0,448},{8,456},{16,464},{24,472},{32,480},{40,488},{48,496},{56,5... | collective-permute-start | bytes 1572872 | tf_op jit(solution)/shard_map/ppermute | solution.py:136
  62.0 26.3 %collective-permute-start.13 = (bf16[512,512]{1,0:T(8,128)(2,1)S(1)}, bf16[512,512]{1,0:T(8,128)(2,1)S(1)}, u32[]{:S(2)}, u32[]{:S(2)}) collective-permute-start(bf16[512,512]{1,0:T(8,128)(2,1)S(1)} %collective-permute-done.11.refs_5_), channel_id=1, source_target_pairs={{0,64},{8,72},{16,80},{24,88},{32,96},{40,104},{48,112},{56,120},{... | collective-permute-start | bytes 1572872 | tf_op jit(solution)/shard_map/ppermute | solution.py:136
  65.4 26.2 %collective-permute-start.8 = (bf16[4,512,128]{2,1,0:T(8,128)(2,1)S(1)}, bf16[4,512,128]{2,1,0:T(8,128)(2,1)}, u32[]{:S(2)}, u32[]{:S(2)}) collective-permute-start(bf16[4,512,128]{2,1,0:T(8,128)(2,1)S(1)} %collective-permute-done.7.refs_1_), channel_id=1, source_target_pairs={{0,504},{8,0},{16,8},{24,16},{32,24},{40,32},{48,40},{56,48},{64,5... | collective-permute-start | bytes 1572872 | tf_op jit(solution)/shard_map/ppermute | solution.py:136
  68.1 20.1 %copy-start = (bf16[5,512,128]{2,1,0:T(8,128)(2,1)}, bf16[5,512,128]{2,1,0:T(8,128)(2,1)S(1)}, u32[]{:S(2)}) copy-start(bf16[5,512,128]{2,1,0:T(8,128)(2,1)S(1)} %collective-permute-done.3.refs_0_) | copy-start | bytes 1966084
  68.2 25.4 %collective-permute-start.4 = (bf16[4,512,128]{2,1,0:T(8,128)(2,1)S(1)}, bf16[4,512,128]{2,1,0:T(8,128)(2,1)}, u32[]{:S(2)}, u32[]{:S(2)}) collective-permute-start(bf16[4,512,128]{2,1,0:T(8,128)(2,1)S(1)} %slice.30), channel_id=1, source_target_pairs={{0,8},{8,16},{16,24},{24,32},{32,40},{40,48},{48,56},{56,64},{64,7... | collective-permute-start | bytes 1572872 | tf_op jit(solution)/shard_map/ppermute | solution.py:136
  72.1 25.7 %collective-permute-start.14 = (bf16[512,512]{1,0:T(8,128)(2,1)S(1)}, bf16[512,512]{1,0:T(8,128)(2,1)S(1)}, u32[]{:S(2)}, u32[]{:S(2)}) collective-permute-start(bf16[512,512]{1,0:T(8,128)(2,1)S(1)} %collective-permute-done.12.refs_6_), channel_id=1, source_target_pairs={{0,448},{8,456},{16,464},{24,472},{32,480},{40,488},{48,496},{56,5... | collective-permute-start | bytes 1572872 | tf_op jit(solution)/shard_map/ppermute | solution.py:136
  88.3 26.7 %collective-permute-start.15 = (bf16[512,512]{1,0:T(8,128)(2,1)S(1)}, bf16[512,512]{1,0:T(8,128)(2,1)}, u32[]{:S(2)}, u32[]{:S(2)}) collective-permute-start(bf16[512,512]{1,0:T(8,128)(2,1)S(1)} %collective-permute-done.13.refs_7_), channel_id=1, source_target_pairs={{0,64},{8,72},{16,80},{24,88},{32,96},{40,104},{48,112},{56,120},{... | collective-permute-start | bytes 1572872 | tf_op jit(solution)/shard_map/ppermute | solution.py:136
  91.6 39.4 %collective-permute-start.9 = (bf16[4,512,128]{2,1,0:T(8,128)(2,1)}, bf16[4,512,128]{2,1,0:T(8,128)(2,1)}, u32[]{:S(2)}, u32[]{:S(2)}) collective-permute-start(bf16[4,512,128]{2,1,0:T(8,128)(2,1)} %collective-permute-done.8.refs_1_), channel_id=1, source_target_pairs={{0,504},{8,0},{16,8},{24,16},{32,24},{40,32},{48,40},{56,48},{64,5... | collective-permute-start | bytes 1572872 | tf_op jit(solution)/shard_map/ppermute | solution.py:136
  93.6 40.3 %collective-permute-start.5 = (bf16[4,512,128]{2,1,0:T(8,128)(2,1)}, bf16[4,512,128]{2,1,0:T(8,128)(2,1)}, u32[]{:S(2)}, u32[]{:S(2)}) collective-permute-start(bf16[4,512,128]{2,1,0:T(8,128)(2,1)} %collective-permute-done.4.refs_0_), channel_id=1, source_target_pairs={{0,8},{8,16},{16,24},{24,32},{32,40},{40,48},{48,56},{56,64},{64,7... | collective-permute-start | bytes 1572872 | tf_op jit(solution)/shard_map/ppermute | solution.py:136
  97.8 84.8 %collective-permute-start.16 = (bf16[512,512]{1,0:T(8,128)(2,1)S(1)}, bf16[512,512]{1,0:T(8,128)(2,1)}, u32[]{:S(2)}, u32[]{:S(2)}) collective-permute-start(bf16[512,512]{1,0:T(8,128)(2,1)S(1)} %collective-permute-done.14.refs_8_), channel_id=1, source_target_pairs={{0,448},{8,456},{16,464},{24,472},{32,480},{40,488},{48,496},{56,5... | collective-permute-start | bytes 1572872 | tf_op jit(solution)/shard_map/ppermute | solution.py:136
  115.0 67.7 %collective-permute-start.17 = (bf16[512,512]{1,0:T(8,128)(2,1)}, bf16[512,512]{1,0:T(8,128)(2,1)}, u32[]{:S(2)}, u32[]{:S(2)}) collective-permute-start(bf16[512,512]{1,0:T(8,128)(2,1)} %collective-permute-done.15.refs_9_), channel_id=1, source_target_pairs={{0,64},{8,72},{16,80},{24,88},{32,96},{40,104},{48,112},{56,120},{... | collective-permute-start | bytes 1572872 | tf_op jit(solution)/shard_map/ppermute | solution.py:136
  122.2 16.6 %copy-start.1 = (bf16[5,512,128]{2,1,0:T(8,128)(2,1)S(1)}, bf16[5,512,128]{2,1,0:T(8,128)(2,1)}, u32[]{:S(2)}) copy-start(bf16[5,512,128]{2,1,0:T(8,128)(2,1)} %copy-done) | copy-start | bytes 1966084
  122.3 16.6 %copy-start.3 = (bf16[4,512,128]{2,1,0:T(8,128)(2,1)S(1)}, bf16[4,512,128]{2,1,0:T(8,128)(2,1)}, u32[]{:S(2)}) copy-start(bf16[4,512,128]{2,1,0:T(8,128)(2,1)} %copy-done.2) | copy-start | bytes 1572868
  132.0 50.7 %collective-permute-start.10 = (bf16[2,512,128]{2,1,0:T(8,128)(2,1)S(1)}, bf16[2,512,128]{2,1,0:T(8,128)(2,1)S(1)}, u32[]{:S(2)}, u32[]{:S(2)}) collective-permute-start(bf16[2,512,128]{2,1,0:T(8,128)(2,1)S(1)} %slice.32), channel_id=1, source_target_pairs={{0,504},{8,0},{16,8},{24,16},{32,24},{40,32},{48,40},{56,48},{64,5... | collective-permute-start | bytes 786440 | tf_op jit(solution)/shard_map/ppermute | solution.py:136
  134.9 47.8 %collective-permute-start.6 = (bf16[2,512,128]{2,1,0:T(8,128)(2,1)S(1)}, bf16[2,512,128]{2,1,0:T(8,128)(2,1)S(1)}, u32[]{:S(2)}, u32[]{:S(2)}) collective-permute-start(bf16[2,512,128]{2,1,0:T(8,128)(2,1)S(1)} %slice.31), channel_id=1, source_target_pairs={{0,8},{8,16},{16,24},{24,32},{32,40},{40,48},{48,56},{56,64},{64,7... | collective-permute-start | bytes 786440 | tf_op jit(solution)/shard_map/ppermute | solution.py:136
  192.0 4.6 %collective-permute-start.18 = (bf16[4,256,512]{2,1,0:T(8,128)(2,1)S(1)}, bf16[4,256,512]{2,1,0:T(8,128)(2,1)S(1)}, u32[]{:S(2)}, u32[]{:S(2)}) collective-permute-start(bf16[4,256,512]{2,1,0:T(8,128)(2,1)S(1)} %slice_bitcast_fusion), channel_id=1, source_target_pairs={{0,1},{1,0},{2,3},{3,2},{4,5},{5,4},{6,7},{7,6},{8,9},{9,8},{10,11... | collective-permute-start | bytes 3145736 | tf_op jit(solution)/shard_map/ppermute | solution.py:183
  (3 other events, 18.5 us)

commit v2 on v1

v2 whole, which is shorter than its diff:
```python
import math

import jax
import jax.numpy as jnp
from jax import lax
from jax.experimental import pallas as pl
from jax.experimental.pallas import tpu as pltpu
from jax.sharding import PartitionSpec as P


NEG = -1e30


def visit(where_ref, q_ref, starts_ref, blocks, accum, top):
    heads, tok, width = q_ref.shape
    factor = math.log2(math.e) / math.sqrt(width)
    me, first = where_ref[0], where_ref[1]

    def add(chosen):
        keys = jnp.concatenate([ref[k, :tok, :] for ref, k, _ in chosen], axis=0)
        vals = jnp.concatenate([ref[k, tok:, :] for ref, k, _ in chosen], axis=0)
        vals = jnp.concatenate([vals, jnp.ones(vals.shape, jnp.bfloat16)], axis=1)
        lane = lax.broadcasted_iota(jnp.int32, (1, tok), 1)
        key_pos = jnp.concatenate([lane + (me + offset) * tok for _, _, offset in chosen], axis=1)
        allowed = key_pos >= starts_ref[:, :1]
        if chosen[0][2] == 0:
            allowed &= key_pos <= me * tok + lax.broadcasted_iota(jnp.int32, (tok, 1), 0)
        for h in range(heads):
            scores = lax.dot_general(
                q_ref[h], keys, (((1,), (1,)), ((), ())), preferred_element_type=jnp.float32
            )
            scores = jnp.where(allowed, scores, NEG)
            old = top[h][:, :1]
            new = jnp.maximum(old, jnp.max(scores, axis=1, keepdims=True))
            weights = jnp.exp2((scores - new) * factor).astype(jnp.bfloat16)
            rescale = jnp.exp2((old - new) * factor)
            accum[h] = accum[h] * rescale + jnp.dot(weights, vals, preferred_element_type=jnp.float32)
            top[h] = jnp.broadcast_to(new, (tok, width))

    pl.when(me + blocks[0][2] >= first)(lambda: add(blocks))


def attend(where, queries, starts, sets, state, finish=False):
    heads, tok, width = queries.shape
    arrays = [array for array, _, _ in sets]
    count = len(sets)
    state_shapes = [
        jax.ShapeDtypeStruct((heads, tok, 2 * width), jnp.float32),
        jax.ShapeDtypeStruct((heads, tok, width), jnp.float32),
    ]
    out_shape = state_shapes
    if finish:
        out_shape = [jax.ShapeDtypeStruct((4, tok, heads * width), jnp.bfloat16)]
    vmem = pl.BlockSpec(memory_space=pltpu.VMEM)
    given = [] if state is None else list(state)
    keys_seen = sum(array.shape[0] for array in arrays) * tok

    def kernel(where_ref, q_ref, starts_ref, *refs):
        if finish:
            accum_in, top_in, out_ref, accum, top = refs[count:]
            accum[...] = accum_in[...]
            top[...] = top_in[...]
        else:
            accum, top = refs[-2:]
        if state is None:
            accum[...] = jnp.zeros_like(accum)
            top[...] = jnp.full_like(top, NEG)
        groups = {}
        for ref, (_, group, offsets) in zip(refs, sets):
            groups.setdefault(group, []).extend((ref, k, offset) for k, offset in enumerate(offsets))
        for blocks in groups.values():
            visit(where_ref, q_ref, starts_ref, blocks, accum, top)
        if finish:
            for h in range(heads):
                attended = (accum[h][:, :width] / accum[h][:, width:]).astype(jnp.bfloat16)
                for copy in range(4):
                    out_ref[copy, :, h * width : (h + 1) * width] = attended

    return pl.pallas_call(
        kernel,
        out_shape=out_shape,
        in_specs=[pl.BlockSpec(memory_space=pltpu.SMEM)] + [vmem] * (2 + count + len(given)),
        out_specs=[vmem] * len(out_shape),
        input_output_aliases={} if finish or state is None else {3 + count: 0, 4 + count: 1},
        scratch_shapes=[pltpu.VMEM(shape.shape, jnp.float32) for shape in state_shapes] if finish else [],
        compiler_params=pltpu.CompilerParams(vmem_limit_bytes=32 * 1024 * 1024),
        cost_estimate=pl.CostEstimate(
            flops=4 * heads * tok * keys_seen * width,
            bytes_accessed=4 * keys_seen * width,
            transcendentals=heads * tok * keys_seen,
        ),
        name="attend",
    )(where, queries, starts, *arrays, *given)


def project(where, mine, others, weight):
    groups, cols, _ = weight.shape
    tok = mine.shape[1]

    def kernel(where_ref, mine_ref, others_ref, weight_ref, out_ref, held, sems):
        copies = [
            pltpu.make_async_copy(weight_ref.at[group], held.at[group], sems.at[group]) for group in range(groups)
        ]
        for copy in copies:
            copy.start()
        core = where_ref[3]
        total = jnp.zeros((tok, cols), jnp.float32)
        for group in range(groups):
            rows = jnp.where(core == group % 2, mine_ref[group // 2], others_ref[group // 2])
            copies[group].wait()
            total += lax.dot_general(
                rows, held[group], (((1,), (1,)), ((), ())), preferred_element_type=jnp.float32
            )
        out_ref[...] = total.astype(jnp.bfloat16)

    vmem = pl.BlockSpec(memory_space=pltpu.VMEM)
    return pl.pallas_call(
        kernel,
        out_shape=jax.ShapeDtypeStruct((tok, cols), jnp.bfloat16),
        in_specs=[pl.BlockSpec(memory_space=pltpu.SMEM), vmem, vmem, pl.BlockSpec(memory_space=pltpu.HBM)],
        out_specs=vmem,
        scratch_shapes=[pltpu.VMEM(weight.shape, jnp.bfloat16), pltpu.SemaphoreType.DMA((groups,))],
        compiler_params=pltpu.CompilerParams(vmem_limit_bytes=32 * 1024 * 1024),
        name="project",
    )(where, mine, others, pltpu.with_memory_space_constraint(weight, pltpu.HBM))


def moved(array, steps):
    count = lax.axis_size("seq")
    return lax.ppermute(array, "seq", [(i, (i + steps) % count) for i in range(count)])


def layer(queries, keys, values, out_weight, doc_lengths):
    tok, _, width = queries.shape
    me = lax.axis_index("seq")
    core = lax.axis_index("head") % 2

    own = jnp.concatenate([keys.reshape(1, tok, width), values.reshape(1, tok, width)], axis=1)
    near = moved(own, 8)
    two = jnp.concatenate([own, near], axis=0)
    double = moved(two, 16)
    column = jnp.concatenate([two, double], axis=0)
    places = [(z, y, h) for z in range(8) for y in range(8) for h in range(8)]
    block = lax.ppermute(
        out_weight.T,
        ("seq", "head"),
        [(64 * z + 8 * y + h, 64 * h + 8 * y + z) for z, y, h in places],
    )
    weight = lax.all_gather(block, "seq", axis=0, tiled=True).reshape(8, -1, block.shape[1])

    ends = jnp.cumsum(doc_lengths)
    position = me * tok + jnp.arange(tok, dtype=jnp.int32)
    starts = jnp.max(jnp.where(ends[None, :] <= position[:, None], ends[None, :], 0), axis=1)
    where = jnp.stack([me, starts[0] // tok, starts[-1], core]).astype(jnp.int32)
    starts = jnp.broadcast_to(starts[:, None], (tok, 128))
    queries = jnp.transpose(queries, (1, 0, 2))

    sets, state = [(column, 0, [0, -8, -16, -24])], None
    up = down = column
    for turn in range(1, 6):
        if turn < 5:
            up = moved(up if turn < 4 else up[:2], 1)
            down = moved(down, 7) if turn == 1 else moved(down if turn < 4 else down[2:], -1)
        if turn == 1:
            edge = jnp.concatenate([column[3:], up[3:]], axis=0)
        if turn == 2:
            edge = moved(edge, 8)
        state = attend(where, queries, starts, sets, state, turn == 5)
        below = [-turn - 8 * a for a in range(4)]
        above = [turn - 8 - 8 * a for a in range(4)]
        if turn < 4:
            sets = [(up, 0, below), (down, 1, above)]
        else:
            sets = [(up, 0, below[:2]), (down, 0, above[2:]), (edge, 1, [-32, -33])]

    mine = lax.all_to_all(
        state[0], "head", 0, 0, axis_index_groups=[[0, 2, 4, 6], [1, 3, 5, 7]], tiled=True
    )
    others = lax.ppermute(mine, "head", [(h, h ^ 1) for h in range(8)])
    return project(where, mine, others, weight)


def solution(mesh):
    placed = (
        P("seq", "head", None),
        P("seq", "head", None),
        P("seq", "head", None),
        P("head", "seq"),
        P(),
    )
    return jax.shard_map(layer, mesh=mesh, in_specs=placed, out_specs=P("seq", "head"), check_vma=False)
```

time: 218 us -> 167 us (0.77)
  the two profiles are of different devices: /device:TPU:320 before, /device:TPU:1 now
where the time goes in v2:
time: 167 us; the launch traced here: 166 us
  waiting for transfers between devices  58.5 us (35%)
  starting transfers between devices  50.9 us (30%)
  blocking collectives  22 us (13%)
  between operations  15.9 us (10%)
  Pallas kernels  10.3 us (6%)
  local copies, waits for them, and re-layouts  4.78 us (3%)
  other arithmetic  3.78 us (2%)
    ppermute x11, waiting for transfers between devices, moved(): lax.ppermute(array, 'seq', [(i, (i + steps) % count) for i in range(count)])  54.1 us
    ppermute x11, starting transfers between devices, moved(): lax.ppermute(array, 'seq', [(i, (i + steps) % count) for i in range(count)])  32.7 us
    all_to_all x1, blocking collectives, layer(): lax.all_to_all(state[0], 'head', 0, 0, axis_index_groups=[[0, 2, 4, 6], [...  22 us
    ppermute x1, starting transfers between devices, layer(): others = lax.ppermute(mine, 'head', [(h, h ^ 1) for h in range(8)])  12.8 us
    pallas_call x5, Pallas kernels, attend(): pl.pallas_call(kernel, out_shape=out_shape, in_specs=[pl.BlockSpec(memory...  5.91 us
    ppermute x1, starting transfers between devices, layer(): lax.ppermute(out_weight.T, ('seq', 'head'), [(64 * z + 8 * y + h, 64 * h...  5.37 us
    pallas_call x1, Pallas kernels, project(): pl.pallas_call(kernel, out_shape=jax.ShapeDtypeStruct((tok, cols), jnp.bf...  4.43 us
  transfers between devices with their start and end apart: 14, of which 9 were waited for; matrix products, arithmetic and copies ran while one was open for 4% of the time, Pallas kernels for 4%

profile of v2, /device:TPU:1, one launch (start us, length us, event | category | flops | bytes accessed | tf_op | source)
XLA Modules:
  0.0 166.2 jit_solution(15736320271210486560)
XLA Ops:
  6.5 5.4 %collective-permute-start.12 = (bf16[64,512]{1,0:T(8,128)(2,1)}, bf16[64,512]{1,0:T(8,128)(2,1)S(1)}, u32[]{:S(2)}, u32[]{:S(2)}) collective-permute-start(bf16[64,512]{1,0:T(8,128)(2,1)} %bitcast.25), channel_id=1, source_target_pairs={{0,0},{1,64},{2,128},{3,192},{4,256},{5,320},{6,384},{7,448},{8,8}... | collective-permute-start | bytes 196616 | tf_op jit(solution)/shard_map/ppermute | solution.py:144
  11.9 2.1 %collective-permute-done.12 = bf16[64,512]{1,0:T(8,128)(2,1)S(1)} collective-permute-done((bf16[64,512]{1,0:T(8,128)(2,1)}, bf16[64,512]{1,0:T(8,128)(2,1)S(1)}, u32[]{:S(2)}, u32[]{:S(2)}) %collective-permute-start.12) | collective-permute-done | bytes 65568 | tf_op jit(solution)/shard_map/ppermute | solution.py:144
  15.6 1.9 %collective-permute-start = (bf16[1,512,128]{2,1,0:T(8,128)(2,1)S(1)}, bf16[1,512,128]{2,1,0:T(8,128)(2,1)S(1)}, u32[]{:S(2)}, u32[]{:S(2)}) collective-permute-start(bf16[1,512,128]{2,1,0:T(8,128)(2,1)S(1)} %pad_maximum_fusion.3), channel_id=1, source_target_pairs={{0,64},{8,72},{16,80},{24,88},{32,96},{40,104},{48,112},{56,120},{... | collective-permute-start | bytes 393224 | tf_op jit(solution)/shard_map/ppermute | solution.py:130
  17.5 14.1 %collective-permute-done = bf16[1,512,128]{2,1,0:T(8,128)(2,1)S(1)} collective-permute-done((bf16[1,512,128]{2,1,0:T(8,128)(2,1)S(1)}, bf16[1,512,128]{2,1,0:T(8,128)(2,1)S(1)}, u32[]{:S(2)}, u32[]{:S(2)}) %collective-permute-start) | collective-permute-done | bytes 131104 | tf_op jit(solution)/shard_map/ppermute | solution.py:130
  32.5 1.9 %collective-permute-start.1 = (bf16[2,512,128]{2,1,0:T(8,128)(2,1)S(1)}, bf16[2,512,128]{2,1,0:T(8,128)(2,1)S(1)}, u32[]{:S(2)}, u32[]{:S(2)}) collective-permute-start(bf16[2,512,128]{2,1,0:T(8,128)(2,1)S(1)} %pad_maximum_fusion.1), channel_id=1, source_target_pairs={{0,128},{8,136},{16,144},{24,152},{32,160},{40,168},{48,176},{56,1... | collective-permute-start | bytes 786440 | tf_op jit(solution)/shard_map/ppermute | solution.py:130
  34.4 12.5 %collective-permute-done.1 = bf16[2,512,128]{2,1,0:T(8,128)(2,1)S(1)} collective-permute-done((bf16[2,512,128]{2,1,0:T(8,128)(2,1)S(1)}, bf16[2,512,128]{2,1,0:T(8,128)(2,1)S(1)}, u32[]{:S(2)}, u32[]{:S(2)}) %collective-permute-start.1) | collective-permute-done | bytes 262176 | tf_op jit(solution)/shard_map/ppermute | solution.py:130
  48.5 3.2 %collective-permute-start.2 = (bf16[4,512,128]{2,1,0:T(8,128)(2,1)S(1)}, bf16[4,512,128]{2,1,0:T(8,128)(2,1)S(1)}, u32[]{:S(2)}, u32[]{:S(2)}) collective-permute-start(bf16[4,512,128]{2,1,0:T(8,128)(2,1)S(1)} %pad_maximum_fusion.refs_0_), channel_id=1, source_target_pairs={{0,8},{8,16},{16,24},{24,32},{32,40},{40,48},{48,56},{56,64},{64,7... | collective-permute-start | bytes 1572872 | tf_op jit(solution)/shard_map/ppermute | solution.py:130
  51.8 4.0 %collective-permute-start.6 = (bf16[4,512,128]{2,1,0:T(8,128)(2,1)S(1)}, bf16[4,512,128]{2,1,0:T(8,128)(2,1)S(1)}, u32[]{:S(2)}, u32[]{:S(2)}) collective-permute-start(bf16[4,512,128]{2,1,0:T(8,128)(2,1)S(1)} %pad_maximum_fusion.refs_0_), channel_id=1, source_target_pairs={{0,56},{8,64},{16,72},{24,80},{32,88},{40,96},{48,104},{56,112},{6... | collective-permute-start | bytes 1572872 | tf_op jit(solution)/shard_map/ppermute | solution.py:130
  55.8 11.4 %collective-permute-done.2.refs_0_ = bf16[4,512,128]{2,1,0:T(8,128)(2,1)S(1)} collective-permute-done((bf16[4,512,128]{2,1,0:T(8,128)(2,1)S(1)}, bf16[4,512,128]{2,1,0:T(8,128)(2,1)S(1)}, u32[]{:S(2)}, u32[]{:S(2)}) %collective-permute-start.2) | collective-permute-done | bytes 524320 | tf_op jit(solution)/shard_map/ppermute | solution.py:130
  67.1 1.9 %collective-permute-start.3 = (bf16[4,512,128]{2,1,0:T(8,128)(2,1)S(1)}, bf16[4,512,128]{2,1,0:T(8,128)(2,1)S(1)}, u32[]{:S(2)}, u32[]{:S(2)}) collective-permute-start(bf16[4,512,128]{2,1,0:T(8,128)(2,1)S(1)} %collective-permute-done.2.refs_0_), channel_id=1, source_target_pairs={{0,8},{8,16},{16,24},{24,32},{32,40},{40,48},{48,56},{56,64},{64,7... | collective-permute-start | bytes 1572872 | tf_op jit(solution)/shard_map/ppermute | solution.py:130
  69.0 8.1 %collective-permute-done.6.refs_1_ = bf16[4,512,128]{2,1,0:T(8,128)(2,1)S(1)} collective-permute-done((bf16[4,512,128]{2,1,0:T(8,128)(2,1)S(1)}, bf16[4,512,128]{2,1,0:T(8,128)(2,1)S(1)}, u32[]{:S(2)}, u32[]{:S(2)}) %collective-permute-start.6) | collective-permute-done | bytes 524320 | tf_op jit(solution)/shard_map/ppermute | solution.py:130
  77.2 1.9 %collective-permute-start.7 = (bf16[4,512,128]{2,1,0:T(8,128)(2,1)S(1)}, bf16[4,512,128]{2,1,0:T(8,128)(2,1)}, u32[]{:S(2)}, u32[]{:S(2)}) collective-permute-start(bf16[4,512,128]{2,1,0:T(8,128)(2,1)S(1)} %collective-permute-done.6.refs_1_), channel_id=1, source_target_pairs={{0,504},{8,0},{16,8},{24,16},{32,24},{40,32},{48,40},{56,48},{64,5... | collective-permute-start | bytes 1572872 | tf_op jit(solution)/shard_map/ppermute | solution.py:130
  79.1 5.3 %collective-permute-done.3.refs_0_ = bf16[4,512,128]{2,1,0:T(8,128)(2,1)S(1)} collective-permute-done((bf16[4,512,128]{2,1,0:T(8,128)(2,1)S(1)}, bf16[4,512,128]{2,1,0:T(8,128)(2,1)S(1)}, u32[]{:S(2)}, u32[]{:S(2)}) %collective-permute-start.3) | collective-permute-done | bytes 524320 | tf_op jit(solution)/shard_map/ppermute | solution.py:130
  84.4 1.9 %collective-permute-start.4 = (bf16[4,512,128]{2,1,0:T(8,128)(2,1)S(1)}, bf16[4,512,128]{2,1,0:T(8,128)(2,1)S(1)}, u32[]{:S(2)}, u32[]{:S(2)}) collective-permute-start(bf16[4,512,128]{2,1,0:T(8,128)(2,1)S(1)} %collective-permute-done.3.refs_0_), channel_id=1, source_target_pairs={{0,8},{8,16},{16,24},{24,32},{32,40},{40,48},{48,56},{56,64},{64,7... | collective-permute-start | bytes 1572872 | tf_op jit(solution)/shard_map/ppermute | solution.py:130
  87.6 5.4 %collective-permute-start.8 = (bf16[4,512,128]{2,1,0:T(8,128)(2,1)}, bf16[4,512,128]{2,1,0:T(8,128)(2,1)S(1)}, u32[]{:S(2)}, u32[]{:S(2)}) collective-permute-start(bf16[4,512,128]{2,1,0:T(8,128)(2,1)} %collective-permute-done.7.refs_1_), channel_id=1, source_target_pairs={{0,504},{8,0},{16,8},{24,16},{32,24},{40,32},{48,40},{56,48},{64,5... | collective-permute-start | bytes 1572872 | tf_op jit(solution)/shard_map/ppermute | solution.py:130
  99.7 2.7 %attend.5 = (f32[4,256,256]{2,1,0:T(8,128)S(1)}, f32[4,256,128]{2,1,0:T(8,128)S(1)}) custom-call(s32[4]{0:T(128)S(1)} %pad_add_fusion.where_ref, bf16[4,256,128]{2,1,0:T(8,128)(2,1)S(1)} %bitcast.12, s32[256,128]{1,0:T(8,128)S(1)} %broadcast_in_dim.13.starts_ref, bf16[4,512,128]{2,1,0:T(8,128)(2,1)S(1)} %pad_maximum_fusion.refs_0_), custom_call_target="tpu_custom_call" | custom-call | flops 536870912 | bytes 524288 | tf_op jit(solution)/shard_map/attend/pallas_call | solution.py:79
  102.5 1.9 %collective-permute-start.10 = (bf16[2,512,128]{2,1,0:T(8,128)(2,1)S(1)}, bf16[2,512,128]{2,1,0:T(8,128)(2,1)S(1)}, u32[]{:S(2)}, u32[]{:S(2)}) collective-permute-start(bf16[2,512,128]{2,1,0:T(8,128)(2,1)S(1)} %pad_maximum_fusion.2), channel_id=1, source_target_pairs={{0,64},{8,72},{16,80},{24,88},{32,96},{40,104},{48,112},{56,120},{... | collective-permute-start | bytes 786440 | tf_op jit(solution)/shard_map/ppermute | solution.py:130
  104.5 1.9 %collective-permute-start.5 = (bf16[2,512,128]{2,1,0:T(8,128)(2,1)S(1)}, bf16[2,512,128]{2,1,0:T(8,128)(2,1)S(1)}, u32[]{:S(2)}, u32[]{:S(2)}) collective-permute-start(bf16[2,512,128]{2,1,0:T(8,128)(2,1)S(1)} %slice.24), channel_id=1, source_target_pairs={{0,8},{8,16},{16,24},{24,32},{32,40},{40,48},{48,56},{56,64},{64,7... | collective-permute-start | bytes 786440 | tf_op jit(solution)/shard_map/ppermute | solution.py:130
  106.5 6.7 %collective-permute-start.9 = (bf16[2,512,128]{2,1,0:T(8,128)(2,1)S(1)}, bf16[2,512,128]{2,1,0:T(8,128)(2,1)S(1)}, u32[]{:S(2)}, u32[]{:S(2)}) collective-permute-start(bf16[2,512,128]{2,1,0:T(8,128)(2,1)S(1)} %slice.25), channel_id=1, source_target_pairs={{0,504},{8,0},{16,8},{24,16},{32,24},{40,32},{48,40},{56,48},{64,5... | collective-permute-start | bytes 786440 | tf_op jit(solution)/shard_map/ppermute | solution.py:130
  115.6 1.5 collective-permute-done.9.refs_1_
  117.8 22.0 %all_to_all.5.mine_ref = bf16[4,256,512]{2,1,0:T(8,128)(2,1)S(1)} all-to-all(bf16[4,256,512]{2,1,0:T(8,128)(2,1)S(1)} %attend.9), channel_id=1, replica_groups={{0,2,4,6},{1,3,5,7},{8,10,12,14},{9,11,13,15},{16,18,20,22},{17,19,21,2..., dimensions={0} | all-to-all | bytes 2097152 | tf_op jit(solution)/shard_map/all_to_all | solution.py:176
  139.8 12.8 %collective-permute-start.11 = (bf16[4,256,512]{2,1,0:T(8,128)(2,1)S(1)}, bf16[4,256,512]{2,1,0:T(8,128)(2,1)S(1)}, u32[]{:S(2)}, u32[]{:S(2)}) collective-permute-start(bf16[4,256,512]{2,1,0:T(8,128)(2,1)S(1)} %all_to_all.5.mine_ref), channel_id=1, source_target_pairs={{0,1},{1,0},{2,3},{3,2},{4,5},{5,4},{6,7},{7,6},{8,9},{9,8},{10,11... | collective-permute-start | bytes 3145736 | tf_op jit(solution)/shard_map/ppermute | solution.py:179
  152.6 2.3 %collective-permute-done.11.others_ref = bf16[4,256,512]{2,1,0:T(8,128)(2,1)S(1)} collective-permute-done((bf16[4,256,512]{2,1,0:T(8,128)(2,1)S(1)}, bf16[4,256,512]{2,1,0:T(8,128)(2,1)S(1)}, u32[]{:S(2)}, u32[]{:S(2)}) %collective-permute-start.11) | collective-permute-done | bytes 1048608 | tf_op jit(solution)/shard_map/ppermute | solution.py:179
  154.9 4.4 %project.1 = bf16[256,512]{1,0:T(8,128)(2,1)} custom-call(s32[4]{0:T(128)S(1)} %pad_add_fusion.where_ref, bf16[4,256,512]{2,1,0:T(8,128)(2,1)S(1)} %all_to_all.5.mine_ref, bf16[4,256,512]{2,1,0:T(8,128)(2,1)S(1)} %collective-permute-done.11.others_ref, bf16[8,512,512]{2,1,0:T(8,128)(2,1)} %bitcast.17), custom_call_target="tpu_custom_call" | custom-call | tf_op jit(solution)/shard_map/project/pallas_call | solution.py:117
  (33 shorter events, 13.1 us)
Async XLA Ops:
  6.5 148.4 %all-gather.2.cloned.1.call-start = ((), (), s32[]{:S(2)}) async-start(), calls=%async_computation.1 | async-start | bytes 4259840 | tf_op jit(solution)/shard_map/all_gather | solution.py:149
  6.5 7.5 %collective-permute-start.12 = (bf16[64,512]{1,0:T(8,128)(2,1)}, bf16[64,512]{1,0:T(8,128)(2,1)S(1)}, u32[]{:S(2)}, u32[]{:S(2)}) collective-permute-start(bf16[64,512]{1,0:T(8,128)(2,1)} %bitcast.25), channel_id=1, source_target_pairs={{0,0},{1,64},{2,128},{3,192},{4,256},{5,320},{6,384},{7,448},{8,8}... | collective-permute-start | bytes 196616 | tf_op jit(solution)/shard_map/ppermute | solution.py:144
  14.1 0.6 copy-start.1
  15.6 16.0 %collective-permute-start = (bf16[1,512,128]{2,1,0:T(8,128)(2,1)S(1)}, bf16[1,512,128]{2,1,0:T(8,128)(2,1)S(1)}, u32[]{:S(2)}, u32[]{:S(2)}) collective-permute-start(bf16[1,512,128]{2,1,0:T(8,128)(2,1)S(1)} %pad_maximum_fusion.3), channel_id=1, source_target_pairs={{0,64},{8,72},{16,80},{24,88},{32,96},{40,104},{48,112},{56,120},{... | collective-permute-start | bytes 393224 | tf_op jit(solution)/shard_map/ppermute | solution.py:130
  32.5 14.5 %collective-permute-start.1 = (bf16[2,512,128]{2,1,0:T(8,128)(2,1)S(1)}, bf16[2,512,128]{2,1,0:T(8,128)(2,1)S(1)}, u32[]{:S(2)}, u32[]{:S(2)}) collective-permute-start(bf16[2,512,128]{2,1,0:T(8,128)(2,1)S(1)} %pad_maximum_fusion.1), channel_id=1, source_target_pairs={{0,128},{8,136},{16,144},{24,152},{32,160},{40,168},{48,176},{56,1... | collective-permute-start | bytes 786440 | tf_op jit(solution)/shard_map/ppermute | solution.py:130
  46.9 0.7 copy-start
  48.5 18.6 %collective-permute-start.2 = (bf16[4,512,128]{2,1,0:T(8,128)(2,1)S(1)}, bf16[4,512,128]{2,1,0:T(8,128)(2,1)S(1)}, u32[]{:S(2)}, u32[]{:S(2)}) collective-permute-start(bf16[4,512,128]{2,1,0:T(8,128)(2,1)S(1)} %pad_maximum_fusion.refs_0_), channel_id=1, source_target_pairs={{0,8},{8,16},{16,24},{24,32},{32,40},{40,48},{48,56},{56,64},{64,7... | collective-permute-start | bytes 1572872 | tf_op jit(solution)/shard_map/ppermute | solution.py:130
  51.8 25.4 %collective-permute-start.6 = (bf16[4,512,128]{2,1,0:T(8,128)(2,1)S(1)}, bf16[4,512,128]{2,1,0:T(8,128)(2,1)S(1)}, u32[]{:S(2)}, u32[]{:S(2)}) collective-permute-start(bf16[4,512,128]{2,1,0:T(8,128)(2,1)S(1)} %pad_maximum_fusion.refs_0_), channel_id=1, source_target_pairs={{0,56},{8,64},{16,72},{24,80},{32,88},{40,96},{48,104},{56,112},{6... | collective-permute-start | bytes 1572872 | tf_op jit(solution)/shard_map/ppermute | solution.py:130
  67.1 17.3 %collective-permute-start.3 = (bf16[4,512,128]{2,1,0:T(8,128)(2,1)S(1)}, bf16[4,512,128]{2,1,0:T(8,128)(2,1)S(1)}, u32[]{:S(2)}, u32[]{:S(2)}) collective-permute-start(bf16[4,512,128]{2,1,0:T(8,128)(2,1)S(1)} %collective-permute-done.2.refs_0_), channel_id=1, source_target_pairs={{0,8},{8,16},{16,24},{24,32},{32,40},{40,48},{48,56},{56,64},{64,7... | collective-permute-start | bytes 1572872 | tf_op jit(solution)/shard_map/ppermute | solution.py:130
  77.2 10.4 %collective-permute-start.7 = (bf16[4,512,128]{2,1,0:T(8,128)(2,1)S(1)}, bf16[4,512,128]{2,1,0:T(8,128)(2,1)}, u32[]{:S(2)}, u32[]{:S(2)}) collective-permute-start(bf16[4,512,128]{2,1,0:T(8,128)(2,1)S(1)} %collective-permute-done.6.refs_1_), channel_id=1, source_target_pairs={{0,504},{8,0},{16,8},{24,16},{32,24},{40,32},{48,40},{56,48},{64,5... | collective-permute-start | bytes 1572872 | tf_op jit(solution)/shard_map/ppermute | solution.py:130
  84.4 20.1 %collective-permute-start.4 = (bf16[4,512,128]{2,1,0:T(8,128)(2,1)S(1)}, bf16[4,512,128]{2,1,0:T(8,128)(2,1)S(1)}, u32[]{:S(2)}, u32[]{:S(2)}) collective-permute-start(bf16[4,512,128]{2,1,0:T(8,128)(2,1)S(1)} %collective-permute-done.3.refs_0_), channel_id=1, source_target_pairs={{0,8},{8,16},{16,24},{24,32},{32,40},{40,48},{48,56},{56,64},{64,7... | collective-permute-start | bytes 1572872 | tf_op jit(solution)/shard_map/ppermute | solution.py:130
  87.6 18.8 %collective-permute-start.8 = (bf16[4,512,128]{2,1,0:T(8,128)(2,1)}, bf16[4,512,128]{2,1,0:T(8,128)(2,1)S(1)}, u32[]{:S(2)}, u32[]{:S(2)}) collective-permute-start(bf16[4,512,128]{2,1,0:T(8,128)(2,1)} %collective-permute-done.7.refs_1_), channel_id=1, source_target_pairs={{0,504},{8,0},{16,8},{24,16},{32,24},{40,32},{48,40},{56,48},{64,5... | collective-permute-start | bytes 1572872 | tf_op jit(solution)/shard_map/ppermute | solution.py:130
  102.5 13.0 %collective-permute-start.10 = (bf16[2,512,128]{2,1,0:T(8,128)(2,1)S(1)}, bf16[2,512,128]{2,1,0:T(8,128)(2,1)S(1)}, u32[]{:S(2)}, u32[]{:S(2)}) collective-permute-start(bf16[2,512,128]{2,1,0:T(8,128)(2,1)S(1)} %pad_maximum_fusion.2), channel_id=1, source_target_pairs={{0,64},{8,72},{16,80},{24,88},{32,96},{40,104},{48,112},{56,120},{... | collective-permute-start | bytes 786440 | tf_op jit(solution)/shard_map/ppermute | solution.py:130
  104.5 11.1 %collective-permute-start.5 = (bf16[2,512,128]{2,1,0:T(8,128)(2,1)S(1)}, bf16[2,512,128]{2,1,0:T(8,128)(2,1)S(1)}, u32[]{:S(2)}, u32[]{:S(2)}) collective-permute-start(bf16[2,512,128]{2,1,0:T(8,128)(2,1)S(1)} %slice.24), channel_id=1, source_target_pairs={{0,8},{8,16},{16,24},{24,32},{32,40},{40,48},{48,56},{56,64},{64,7... | collective-permute-start | bytes 786440 | tf_op jit(solution)/shard_map/ppermute | solution.py:130
  106.5 10.6 %collective-permute-start.9 = (bf16[2,512,128]{2,1,0:T(8,128)(2,1)S(1)}, bf16[2,512,128]{2,1,0:T(8,128)(2,1)S(1)}, u32[]{:S(2)}, u32[]{:S(2)}) collective-permute-start(bf16[2,512,128]{2,1,0:T(8,128)(2,1)S(1)} %slice.25), channel_id=1, source_target_pairs={{0,504},{8,0},{16,8},{24,16},{32,24},{40,32},{48,40},{56,48},{64,5... | collective-permute-start | bytes 786440 | tf_op jit(solution)/shard_map/ppermute | solution.py:130
  139.8 15.1 %collective-permute-start.11 = (bf16[4,256,512]{2,1,0:T(8,128)(2,1)S(1)}, bf16[4,256,512]{2,1,0:T(8,128)(2,1)S(1)}, u32[]{:S(2)}, u32[]{:S(2)}) collective-permute-start(bf16[4,256,512]{2,1,0:T(8,128)(2,1)S(1)} %all_to_all.5.mine_ref), channel_id=1, source_target_pairs={{0,1},{1,0},{2,3},{3,2},{4,5},{5,4},{6,7},{7,6},{8,9},{9,8},{10,11... | collective-permute-start | bytes 3145736 | tf_op jit(solution)/shard_map/ppermute | solution.py:179
Sparse Core Ops, SparseCore 0:
  14.8 133.6 all-gather.1

commit v3 on v2

v3 whole, which is shorter than its diff:
```python
import math

import jax
import jax.numpy as jnp
from jax import lax
from jax.experimental import pallas as pl
from jax.experimental.pallas import tpu as pltpu
from jax.sharding import PartitionSpec as P


NEG = -1e30


def visit(where_ref, q_ref, starts_ref, blocks, nearest, accum, top, causal=False):
    heads, tok, width = q_ref.shape
    factor = math.log2(math.e) / math.sqrt(width)
    me, first = where_ref[0], where_ref[1]

    def add():
        keys = jnp.concatenate([ref[k, :tok, :] for ref, k, _ in blocks], axis=0)
        vals = jnp.concatenate([ref[k, tok:, :] for ref, k, _ in blocks], axis=0)
        vals = jnp.concatenate([vals, jnp.ones(vals.shape, jnp.bfloat16)], axis=1)
        lane = lax.broadcasted_iota(jnp.int32, (1, tok), 1)
        key_pos = jnp.concatenate([lane + number * tok for _, _, number in blocks], axis=1)
        allowed = key_pos >= starts_ref[:, :1]
        if causal:
            allowed &= key_pos <= me * tok + lax.broadcasted_iota(jnp.int32, (tok, 1), 0)
        for h in range(heads):
            scores = lax.dot_general(
                q_ref[h], keys, (((1,), (1,)), ((), ())), preferred_element_type=jnp.float32
            )
            scores = jnp.where(allowed, scores, NEG)
            old = top[h][:, :1]
            new = jnp.maximum(old, jnp.max(scores, axis=1, keepdims=True))
            weights = jnp.exp2((scores - new) * factor).astype(jnp.bfloat16)
            rescale = jnp.exp2((old - new) * factor)
            accum[h] = accum[h] * rescale + jnp.dot(weights, vals, preferred_element_type=jnp.float32)
            top[h] = jnp.broadcast_to(new, (tok, width))

    pl.when(me + nearest >= first)(add)


def attend(where, queries, starts, arrays, plan, state, finish=False):
    heads, tok, width = queries.shape
    count = len(arrays)
    state_shapes = [
        jax.ShapeDtypeStruct((heads, tok, 2 * width), jnp.float32),
        jax.ShapeDtypeStruct((heads, tok, width), jnp.float32),
    ]
    out_shape = state_shapes
    if finish:
        out_shape = [jax.ShapeDtypeStruct((tok, heads * width), jnp.bfloat16)]
    vmem = pl.BlockSpec(memory_space=pltpu.VMEM)
    given = [] if state is None else list(state)
    keys_seen = 8 * tok

    def kernel(where_ref, q_ref, starts_ref, *refs):
        if finish:
            accum_in, top_in, out_ref, accum, top = refs[count:]
            accum[...] = accum_in[...]
            top[...] = top_in[...]
        else:
            accum, top = refs[-2:]
        if state is None:
            accum[...] = jnp.zeros_like(accum)
            top[...] = jnp.full_like(top, NEG)
        for blocks, nearest, causal in plan(where_ref, refs[:count]):
            visit(where_ref, q_ref, starts_ref, blocks, nearest, accum, top, causal)
        if finish:
            for h in range(heads):
                out_ref[:, h * width : (h + 1) * width] = (
                    accum[h][:, :width] / accum[h][:, width:]
                ).astype(jnp.bfloat16)

    return pl.pallas_call(
        kernel,
        out_shape=out_shape,
        in_specs=[pl.BlockSpec(memory_space=pltpu.SMEM)] + [vmem] * (2 + count + len(given)),
        out_specs=[vmem] * len(out_shape),
        input_output_aliases={} if finish or state is None else {3 + count: 0, 4 + count: 1},
        scratch_shapes=[pltpu.VMEM(shape.shape, jnp.float32) for shape in state_shapes] if finish else [],
        compiler_params=pltpu.CompilerParams(vmem_limit_bytes=16 * 1024 * 1024),
        cost_estimate=pl.CostEstimate(
            flops=4 * heads * tok * keys_seen * width,
            bytes_accessed=4 * keys_seen * width,
            transcendentals=heads * tok * keys_seen,
        ),
        name="attend",
    )(where, queries, starts, *arrays, *given)


def project(where, attended, weight):
    tok, depth = attended.shape
    groups = 8
    weight = weight.reshape(groups, -1, depth)
    cols = weight.shape[1]

    def kernel(where_ref, attended_ref, weight_ref, out_ref, held, sems):
        copies = [
            pltpu.make_async_copy(weight_ref.at[group], held.at[group], sems.at[group]) for group in range(groups)
        ]
        for copy in copies:
            copy.start()
        core = where_ref[3]
        for group in range(groups):
            copies[group].wait()
            sent = jnp.bitwise_xor(core, group % 2)
            out_ref[sent, group // 2] = lax.dot_general(
                attended_ref[...], held[group], (((1,), (1,)), ((), ())), preferred_element_type=jnp.float32
            ).astype(jnp.bfloat16)

    vmem = pl.BlockSpec(memory_space=pltpu.VMEM)
    return pl.pallas_call(
        kernel,
        out_shape=jax.ShapeDtypeStruct((2, groups // 2, tok, cols), jnp.bfloat16),
        in_specs=[pl.BlockSpec(memory_space=pltpu.SMEM), vmem, pl.BlockSpec(memory_space=pltpu.HBM)],
        out_specs=vmem,
        scratch_shapes=[pltpu.VMEM(weight.shape, jnp.bfloat16), pltpu.SemaphoreType.DMA((groups,))],
        compiler_params=pltpu.CompilerParams(vmem_limit_bytes=16 * 1024 * 1024),
        name="project",
    )(where, attended, pltpu.with_memory_space_constraint(weight, pltpu.HBM))


def down_column(array, steps):
    return lax.ppermute(
        array, "seq", [(8 * z + y, 8 * ((z + steps) % 8) + y) for z in range(8) for y in range(8)]
    )


def along_row(array, steps):
    return lax.ppermute(
        array, "seq", [(8 * z + y, 8 * z + (y + steps) % 8) for z in range(8) for y in range(8)]
    )


def layer(queries, keys, values, out_weight, doc_lengths):
    tok, _, width = queries.shape
    me = lax.axis_index("seq")
    core = lax.axis_index("head") % 2

    own = jnp.concatenate([keys.reshape(1, tok, width), values.reshape(1, tok, width)], axis=1)
    near = down_column(own, 1)
    far = down_column(own, 4)
    two = jnp.concatenate([own, near], axis=0)
    double = down_column(two, 2)
    column = jnp.concatenate([two, double, far], axis=0)
    turned = out_weight.T
    weight = lax.all_to_all(
        jnp.broadcast_to(turned[None], (8,) + turned.shape),
        "seq",
        0,
        0,
        axis_index_groups=[[8 * z + y for y in range(8)] for z in range(8)],
        tiled=True,
    ).reshape(8 * turned.shape[0], turned.shape[1])
    weight = lax.all_gather(
        weight,
        "seq",
        axis=0,
        axis_index_groups=[[8 * z + y for z in range(8)] for y in range(8)],
        tiled=True,
    )

    ends = jnp.cumsum(doc_lengths)
    position = me * tok + jnp.arange(tok, dtype=jnp.int32)
    starts = jnp.max(jnp.where(ends[None, :] <= position[:, None], ends[None, :], 0), axis=1)
    where = jnp.stack([me, starts[0] // tok, starts[-1], core, me % 8]).astype(jnp.int32)
    starts = jnp.broadcast_to(starts[:, None], (tok, 128))
    queries = jnp.transpose(queries, (1, 0, 2))


    def own_plan(where_ref, refs):
        me = where_ref[0]
        yield [(refs[0], a, me - 8 * a) for a in range(4)], 0, True

    def turn_plan(turn):
        def plan(where_ref, refs):
            me, place = where_ref[0], where_ref[4]
            skip = jnp.where(place >= turn, 0, 1)
            yield [(refs[0], skip + a, me - turn - 8 * a) for a in range(4)], -turn, False
            skip = jnp.where(place + turn < 8, 1, 0)
            yield [(refs[1], skip + a, me + turn - 8 - 8 * a) for a in range(4)], turn - 8, False

        return plan

    def last_plan(where_ref, refs):
        me, place = where_ref[0], where_ref[4]
        up, down, column, first_up, edge = refs
        shift = jnp.where(place >= 4, -4, 4)
        numbers = [me + shift - 8 * a for a in range(5)]
        numbers = [jnp.where(number > me, -1, number) for number in numbers]
        blocks = [(up, a, numbers[a]) for a in range(3)] + [(down, a, numbers[3 + a]) for a in range(2)]
        yield blocks, -4, False
        yield [(column, 4, me - 32)], -32, False
        beyond = jnp.where(place > 0, me - 33, -1)
        blocks = [(first_up, 4, beyond), (edge, 0, jnp.where(place > 0, -1, me - 33))]
        yield blocks, -33, False

    state, arrays, plan = None, [column], own_plan
    up = down = column
    for turn in range(1, 5):
        up = along_row(up if turn < 4 else up[:3], 1)
        down = along_row(down if turn < 4 else down[3:], -1)
        if turn == 1:
            first_up = up
        state = attend(where, queries, starts, arrays, plan, state)
        arrays, plan = [up, down], turn_plan(turn)
    edge = lax.ppermute(column[:1], "seq", [(8 * z + 7, 8 * ((z + 5) % 8)) for z in range(8)])
    arrays = [up, down, column, first_up, edge]
    (attended,) = attend(where, queries, starts, arrays, last_plan, state, True)
    partial = project(where, attended, weight)

    other = lax.ppermute(partial[1], "head", [(h, h ^ 1) for h in range(8)])
    both = (partial[0].astype(jnp.float32) + other.astype(jnp.float32)).astype(jnp.bfloat16)
    parts = lax.all_to_all(
        both, "head", 0, 0, axis_index_groups=[[0, 2, 4, 6], [1, 3, 5, 7]], tiled=True
    )
    return jnp.sum(parts.astype(jnp.float32), axis=0).astype(jnp.bfloat16)


def solution(mesh):
    placed = (
        P("seq", "head", None),
        P("seq", "head", None),
        P("seq", "head", None),
        P("head", "seq"),
        P(),
    )
    return jax.shard_map(layer, mesh=mesh, in_specs=placed, out_specs=P("seq", "head"), check_vma=False)
```

time: 167 us -> 188 us (1.13)
  the two profiles are of different devices: /device:TPU:1 before, /device:TPU:128 now
where the time goes in v3:
time: 188 us
  starting transfers between devices  49 us (26%)
  waiting for transfers between devices  48.2 us (26%)
  blocking collectives  44.1 us (23%)
  Pallas kernels  25.2 us (13%)
  between operations  16.2 us (9%)
  local copies, waits for them, and re-layouts  3.41 us (2%)
    ppermute x8, starting transfers between devices, along_row(): lax.ppermute(array, 'seq', [(8 * z + y, 8 * z + (y + steps) % 8) for z in...  28.2 us
    ppermute x3, waiting for transfers between devices, down_column(): lax.ppermute(array, 'seq', [(8 * z + y, 8 * ((z + steps) % 8) + y) for z...  25.4 us
    all_to_all x1, blocking collectives, layer(): lax.all_to_all(jnp.broadcast_to(turned[None], (8,) + turned.shape), 'seq'...  24.5 us
    pallas_call x5, Pallas kernels, attend(): pl.pallas_call(kernel, out_shape=out_shape, in_specs=[pl.BlockSpec(memory...  20.9 us
    ppermute x8, waiting for transfers between devices, along_row(): lax.ppermute(array, 'seq', [(8 * z + y, 8 * z + (y + steps) % 8) for z in...  20.1 us
    all_to_all x1, blocking collectives, layer(): lax.all_to_all(both, 'head', 0, 0, axis_index_groups=[[0, 2, 4, 6], [1, 3...  19.6 us
    ppermute x3, starting transfers between devices, down_column(): lax.ppermute(array, 'seq', [(8 * z + y, 8 * ((z + steps) % 8) + y) for z...  17.6 us
    pallas_call x1, Pallas kernels, project(): pl.pallas_call(kernel, out_shape=jax.ShapeDtypeStruct((2, groups // 2, to...  4.34 us
  transfers between devices with their start and end apart: 14, of which 6 were waited for; matrix products, arithmetic and copies ran while one was open for 1% of the time, Pallas kernels for 11%

profile of v3, /device:TPU:128, one launch (start us, length us, event | category | flops | bytes accessed | tf_op | source)
XLA Modules:
  0.0 187.7 jit_solution(14463326658398366183)
XLA Ops:
  7.5 24.5 %all_to_all.10 = bf16[8,64,512]{2,1,0:T(8,128)(2,1)} all-to-all(bf16[8,64,512]{2,1,0:T(8,128)(2,1)S(1)} %broadcast_in_dim.16), channel_id=1, replica_groups={{0,8,16,24,32,40,48,56},{64,72,80,88,96,104,112,120},{128,136,144,152,1..., dimensions={0} | all-to-all | bytes 1048576 | tf_op jit(solution)/shard_map/all_to_all | solution.py:148
  32.0 4.4 %collective-permute-start = (bf16[1,512,128]{2,1,0:T(8,128)(2,1)S(1)}, bf16[1,512,128]{2,1,0:T(8,128)(2,1)S(1)}, u32[]{:S(2)}, u32[]{:S(2)}) collective-permute-start(bf16[1,512,128]{2,1,0:T(8,128)(2,1)S(1)} %pad_maximum_fusion.2), channel_id=1, source_target_pairs={{0,64},{8,72},{16,80},{24,88},{32,96},{40,104},{48,112},{56,120},{... | collective-permute-start | bytes 393224 | tf_op jit(solution)/shard_map/ppermute | solution.py:125
  36.4 2.6 %collective-permute-done = bf16[1,512,128]{2,1,0:T(8,128)(2,1)S(1)} collective-permute-done((bf16[1,512,128]{2,1,0:T(8,128)(2,1)S(1)}, bf16[1,512,128]{2,1,0:T(8,128)(2,1)S(1)}, u32[]{:S(2)}, u32[]{:S(2)}) %collective-permute-start) | collective-permute-done | bytes 131104 | tf_op jit(solution)/shard_map/ppermute | solution.py:125
  39.0 8.5 %collective-permute-start.1 = (bf16[2,512,128]{2,1,0:T(8,128)(2,1)S(1)}, bf16[2,512,128]{2,1,0:T(8,128)(2,1)S(1)}, u32[]{:S(2)}, u32[]{:S(2)}) collective-permute-start(bf16[2,512,128]{2,1,0:T(8,128)(2,1)S(1)} %pad_maximum_fusion.1), channel_id=1, source_target_pairs={{0,128},{8,136},{16,144},{24,152},{32,160},{40,168},{48,176},{56,1... | collective-permute-start | bytes 786440 | tf_op jit(solution)/shard_map/ppermute | solution.py:125
  47.6 4.6 %collective-permute-start.2 = (bf16[1,512,128]{2,1,0:T(8,128)(2,1)S(1)}, bf16[1,512,128]{2,1,0:T(8,128)(2,1)S(1)}, u32[]{:S(2)}, u32[]{:S(2)}) collective-permute-start(bf16[1,512,128]{2,1,0:T(8,128)(2,1)S(1)} %pad_maximum_fusion.2), channel_id=1, source_target_pairs={{0,256},{8,264},{16,272},{24,280},{32,288},{40,296},{48,304},{56,3... | collective-permute-start | bytes 393224 | tf_op jit(solution)/shard_map/ppermute | solution.py:125
  52.2 22.8 %collective-permute-done.2 = bf16[1,512,128]{2,1,0:T(8,128)(2,1)S(1)} collective-permute-done((bf16[1,512,128]{2,1,0:T(8,128)(2,1)S(1)}, bf16[1,512,128]{2,1,0:T(8,128)(2,1)S(1)}, u32[]{:S(2)}, u32[]{:S(2)}) %collective-permute-start.2) | collective-permute-done | bytes 131104 | tf_op jit(solution)/shard_map/ppermute | solution.py:125
  75.1 1.9 %collective-permute-start.3 = (bf16[5,512,128]{2,1,0:T(8,128)(2,1)S(1)}, bf16[5,512,128]{2,1,0:T(8,128)(2,1)S(1)}, u32[]{:S(2)}, u32[]{:S(2)}) collective-permute-start(bf16[5,512,128]{2,1,0:T(8,128)(2,1)S(1)} %pad_maximum_fusion.refs_0_.refs_2_), channel_id=1, source_target_pairs={{0,8},{8,16},{16,24},{24,32},{32,40},{40,48},{48,56},{56,0},{64,72... | collective-permute-start | bytes 1966088 | tf_op jit(solution)/shard_map/ppermute | solution.py:131
  77.0 5.1 %collective-permute-start.7 = (bf16[5,512,128]{2,1,0:T(8,128)(2,1)S(1)}, bf16[5,512,128]{2,1,0:T(8,128)(2,1)S(1)}, u32[]{:S(2)}, u32[]{:S(2)}) collective-permute-start(bf16[5,512,128]{2,1,0:T(8,128)(2,1)S(1)} %pad_maximum_fusion.refs_0_.refs_2_), channel_id=1, source_target_pairs={{0,56},{8,0},{16,8},{24,16},{32,24},{40,32},{48,40},{56,48},{64,12... | collective-permute-start | bytes 1966088 | tf_op jit(solution)/shard_map/ppermute | solution.py:131
  82.1 8.1 %collective-permute-done.3.refs_0_.refs_3_ = bf16[5,512,128]{2,1,0:T(8,128)(2,1)S(1)} collective-permute-done((bf16[5,512,128]{2,1,0:T(8,128)(2,1)S(1)}, bf16[5,512,128]{2,1,0:T(8,128)(2,1)S(1)}, u32[]{:S(2)}, u32[]{:S(2)}) %collective-permute-start.3) | collective-permute-done | bytes 655392 | tf_op jit(solution)/shard_map/ppermute | solution.py:131
  92.1 5.1 %collective-permute-start.8 = (bf16[5,512,128]{2,1,0:T(8,128)(2,1)S(1)}, bf16[5,512,128]{2,1,0:T(8,128)(2,1)}, u32[]{:S(2)}, u32[]{:S(2)}) collective-permute-start(bf16[5,512,128]{2,1,0:T(8,128)(2,1)S(1)} %collective-permute-done.7.refs_1_), channel_id=1, source_target_pairs={{0,56},{8,0},{16,8},{24,16},{32,24},{40,32},{48,40},{56,48},{64,12... | collective-permute-start | bytes 1966088 | tf_op jit(solution)/shard_map/ppermute | solution.py:131
  98.1 6.8 %collective-permute-done.4.refs_0_ = bf16[5,512,128]{2,1,0:T(8,128)(2,1)} collective-permute-done((bf16[5,512,128]{2,1,0:T(8,128)(2,1)S(1)}, bf16[5,512,128]{2,1,0:T(8,128)(2,1)}, u32[]{:S(2)}, u32[]{:S(2)}) %collective-permute-start.4) | collective-permute-done | bytes 655392 | tf_op jit(solution)/shard_map/ppermute | solution.py:131
  106.8 5.1 %collective-permute-start.9 = (bf16[5,512,128]{2,1,0:T(8,128)(2,1)}, bf16[5,512,128]{2,1,0:T(8,128)(2,1)S(1)}, u32[]{:S(2)}, u32[]{:S(2)}) collective-permute-start(bf16[5,512,128]{2,1,0:T(8,128)(2,1)} %collective-permute-done.8.refs_1_), channel_id=1, source_target_pairs={{0,56},{8,0},{16,8},{24,16},{32,24},{40,32},{48,40},{56,48},{64,12... | collective-permute-start | bytes 1966088 | tf_op jit(solution)/shard_map/ppermute | solution.py:131
  117.5 5.3 %collective-permute-done.5.refs_0_ = bf16[5,512,128]{2,1,0:T(8,128)(2,1)S(1)} collective-permute-done((bf16[5,512,128]{2,1,0:T(8,128)(2,1)}, bf16[5,512,128]{2,1,0:T(8,128)(2,1)S(1)}, u32[]{:S(2)}, u32[]{:S(2)}) %collective-permute-start.5) | collective-permute-done | bytes 655392 | tf_op jit(solution)/shard_map/ppermute | solution.py:131
  122.8 1.9 %collective-permute-start.6 = (bf16[3,512,128]{2,1,0:T(8,128)(2,1)S(1)}, bf16[3,512,128]{2,1,0:T(8,128)(2,1)S(1)}, u32[]{:S(2)}, u32[]{:S(2)}) collective-permute-start(bf16[3,512,128]{2,1,0:T(8,128)(2,1)S(1)} %slice.24), channel_id=1, source_target_pairs={{0,8},{8,16},{16,24},{24,32},{32,40},{40,48},{48,56},{56,0},{64,72... | collective-permute-start | bytes 1179656 | tf_op jit(solution)/shard_map/ppermute | solution.py:131
  124.9 2.8 %attend.5 = (f32[4,256,256]{2,1,0:T(8,128)S(1)}, f32[4,256,128]{2,1,0:T(8,128)S(1)}) custom-call(s32[5]{0:T(128)S(1)} %stack.19.where_ref, bf16[4,256,128]{2,1,0:T(8,128)(2,1)S(1)} %bitcast.21, s32[256,128]{1,0:T(8,128)S(1)} %broadcast_in_dim.15.starts_ref, bf16[5,512,128]{2,1,0:T(8,128)(2,1)S(1)} %pad_maximum_fusion.refs_0_.refs_2_), custom_call_target="tpu_custom_call" | custom-call | flops 1073741824 | bytes 1048576 | tf_op jit(solution)/shard_map/attend/pallas_call | solution.py:75
  127.7 5.1 %collective-permute-start.10 = (bf16[2,512,128]{2,1,0:T(8,128)(2,1)S(1)}, bf16[2,512,128]{2,1,0:T(8,128)(2,1)S(1)}, u32[]{:S(2)}, u32[]{:S(2)}) collective-permute-start(bf16[2,512,128]{2,1,0:T(8,128)(2,1)S(1)} %slice.25), channel_id=1, source_target_pairs={{0,56},{8,0},{16,8},{24,16},{32,24},{40,32},{48,40},{56,48},{64,12... | collective-permute-start | bytes 786440 | tf_op jit(solution)/shard_map/ppermute | solution.py:131
  132.9 4.7 %attend.6 = (f32[4,256,256]{2,1,0:T(8,128)S(1)}, f32[4,256,128]{2,1,0:T(8,128)S(1)}) custom-call(s32[5]{0:T(128)S(1)} %stack.19.where_ref, bf16[4,256,128]{2,1,0:T(8,128)(2,1)S(1)} %bitcast.22, s32[256,128]{1,0:T(8,128)S(1)} %broadcast_in_dim.15.starts_ref, ...), custom_call_target="tpu_custom_call", output_to_operand_aliasing={{0}: (5, {}), {1}: (6, {})} | custom-call | flops 1073741824 | bytes 1048576 | tf_op jit(solution)/shard_map/attend/pallas_call | solution.py:75
  137.6 5.4 %attend.7 = (f32[4,256,256]{2,1,0:T(8,128)S(1)}, f32[4,256,128]{2,1,0:T(8,128)S(1)}) custom-call(s32[5]{0:T(128)S(1)} %stack.19.where_ref, bf16[4,256,128]{2,1,0:T(8,128)(2,1)S(1)} %bitcast.23, s32[256,128]{1,0:T(8,128)S(1)} %broadcast_in_dim.15.starts_ref, ...), custom_call_target="tpu_custom_call", output_to_operand_aliasing={{0}: (5, {}), {1}: (6, {})} | custom-call | flops 1073741824 | bytes 1048576 | tf_op jit(solution)/shard_map/attend/pallas_call | solution.py:75
  142.9 4.8 %attend.8 = (f32[4,256,256]{2,1,0:T(8,128)S(1)}, f32[4,256,128]{2,1,0:T(8,128)S(1)}) custom-call(s32[5]{0:T(128)S(1)} %stack.19.where_ref, bf16[4,256,128]{2,1,0:T(8,128)(2,1)S(1)} %bitcast.24, s32[256,128]{1,0:T(8,128)S(1)} %broadcast_in_dim.15.starts_ref, ...), custom_call_target="tpu_custom_call", output_to_operand_aliasing={{0}: (5, {}), {1}: (6, {})} | custom-call | flops 1073741824 | bytes 1048576 | tf_op jit(solution)/shard_map/attend/pallas_call | solution.py:75
  147.8 3.2 %attend.9.attended_ref = bf16[256,512]{1,0:T(8,128)(2,1)S(1)} custom-call(s32[5]{0:T(128)S(1)} %stack.19.where_ref, bf16[4,256,128]{2,1,0:T(8,128)(2,1)S(1)} %bitcast.25, s32[256,128]{1,0:T(8,128)S(1)} %broadcast_in_dim.15.starts_ref, bf16[3,512,128]{2,1,0:T(8,128)(2,1)S(1)} %collective-permute-done.6.refs_0_, ...), custom_call_target="tpu_custom_call" | custom-call | flops 1073741824 | bytes 1048576 | tf_op jit(solution)/shard_map/attend/pallas_call | solution.py:75
  151.0 4.3 %project.1 = bf16[2,4,256,512]{3,2,1,0:T(8,128)(2,1)S(1)} custom-call(s32[5]{0:T(128)S(1)} %stack.19.where_ref, bf16[256,512]{1,0:T(8,128)(2,1)S(1)} %attend.9.attended_ref, bf16[8,512,512]{2,1,0:T(8,128)(2,1)} %bitcast.26), custom_call_target="tpu_custom_call" | custom-call | tf_op jit(solution)/shard_map/project/pallas_call | solution.py:113
  155.4 1.9 %collective-permute-start.12 = (bf16[4,256,512]{2,1,0:T(8,128)(2,1)S(1)}, bf16[4,256,512]{2,1,0:T(8,128)(2,1)S(1)}, u32[]{:S(2)}, u32[]{:S(2)}) collective-permute-start(bf16[4,256,512]{2,1,0:T(8,128)(2,1)S(1)} %slice_bitcast_fusion), channel_id=1, source_target_pairs={{0,1},{1,0},{2,3},{3,2},{4,5},{5,4},{6,7},{7,6},{8,9},{9,8},{10,11... | collective-permute-start | bytes 3145736 | tf_op jit(solution)/shard_map/ppermute | solution.py:213
  157.4 2.6 %collective-permute-done.12 = bf16[4,256,512]{2,1,0:T(8,128)(2,1)S(1)} collective-permute-done((bf16[4,256,512]{2,1,0:T(8,128)(2,1)S(1)}, bf16[4,256,512]{2,1,0:T(8,128)(2,1)S(1)}, u32[]{:S(2)}, u32[]{:S(2)}) %collective-permute-start.12) | collective-permute-done | bytes 1048608 | tf_op jit(solution)/shard_map/ppermute | solution.py:213
  160.3 19.6 %all_to_all.11 = bf16[4,256,512]{2,1,0:T(8,128)(2,1)S(1)} all-to-all(bf16[4,256,512]{2,1,0:T(8,128)(2,1)S(1)} %fusion), channel_id=1, replica_groups={{0,2,4,6},{1,3,5,7},{8,10,12,14},{9,11,13,15},{16,18,20,22},{17,19,21,2..., dimensions={0} | all-to-all | bytes 2097152 | tf_op jit(solution)/shard_map/all_to_all | solution.py:215
  (43 shorter events, 10.2 us)
Async XLA Ops:
  6.5 25.5 %copy-start.3 = (bf16[256,1,128]{2,0,1:T(8,128)(2,1)S(1)}, bf16[256,1,128]{2,0,1:T(8,128)(2,1)}, u32[]{:S(2)}) copy-start(bf16[256,1,128]{2,0,1:T(8,128)(2,1)} %param.6) | copy-start | bytes 196612
  6.5 25.5 %copy-start.2 = (bf16[256,1,128]{2,0,1:T(8,128)(2,1)S(1)}, bf16[256,1,128]{2,0,1:T(8,128)(2,1)}, u32[]{:S(2)}) copy-start(bf16[256,1,128]{2,0,1:T(8,128)(2,1)} %param.7) | copy-start | bytes 196612
  6.5 144.5 %all-gather.2.cloned.1.call-start = ((), (), s32[]{:S(2)}) async-start(), calls=%async_computation.2 | async-start | bytes 4718592 | tf_op jit(solution)/shard_map/all_gather | solution.py:156
  32.0 81.3 %copy-start.5 = (s32[64]{0:T(128)S(1)}, s32[64]{0:T(128)}, u32[]{:S(2)}) copy-start(s32[64]{0:T(128)} %param.9) | copy-start | bytes 772
  32.0 84.8 %copy-start.4 = (bf16[256,4,128]{2,1,0:T(4,128)(2,1)S(1)}, bf16[256,4,128]{2,1,0:T(4,128)(2,1)}, u32[]{:S(2)}) copy-start(bf16[256,4,128]{2,1,0:T(4,128)(2,1)} %param.5) | copy-start | bytes 786436
  32.0 7.0 %collective-permute-start = (bf16[1,512,128]{2,1,0:T(8,128)(2,1)S(1)}, bf16[1,512,128]{2,1,0:T(8,128)(2,1)S(1)}, u32[]{:S(2)}, u32[]{:S(2)}) collective-permute-start(bf16[1,512,128]{2,1,0:T(8,128)(2,1)S(1)} %pad_maximum_fusion.2), channel_id=1, source_target_pairs={{0,64},{8,72},{16,80},{24,88},{32,96},{40,104},{48,112},{56,120},{... | collective-permute-start | bytes 393224 | tf_op jit(solution)/shard_map/ppermute | solution.py:125
  39.0 36.0 %collective-permute-start.1 = (bf16[2,512,128]{2,1,0:T(8,128)(2,1)S(1)}, bf16[2,512,128]{2,1,0:T(8,128)(2,1)S(1)}, u32[]{:S(2)}, u32[]{:S(2)}) collective-permute-start(bf16[2,512,128]{2,1,0:T(8,128)(2,1)S(1)} %pad_maximum_fusion.1), channel_id=1, source_target_pairs={{0,128},{8,136},{16,144},{24,152},{32,160},{40,168},{48,176},{56,1... | collective-permute-start | bytes 786440 | tf_op jit(solution)/shard_map/ppermute | solution.py:125
  47.6 27.4 %collective-permute-start.2 = (bf16[1,512,128]{2,1,0:T(8,128)(2,1)S(1)}, bf16[1,512,128]{2,1,0:T(8,128)(2,1)S(1)}, u32[]{:S(2)}, u32[]{:S(2)}) collective-permute-start(bf16[1,512,128]{2,1,0:T(8,128)(2,1)S(1)} %pad_maximum_fusion.2), channel_id=1, source_target_pairs={{0,256},{8,264},{16,272},{24,280},{32,288},{40,296},{48,304},{56,3... | collective-permute-start | bytes 393224 | tf_op jit(solution)/shard_map/ppermute | solution.py:125
  75.1 15.1 %collective-permute-start.3 = (bf16[5,512,128]{2,1,0:T(8,128)(2,1)S(1)}, bf16[5,512,128]{2,1,0:T(8,128)(2,1)S(1)}, u32[]{:S(2)}, u32[]{:S(2)}) collective-permute-start(bf16[5,512,128]{2,1,0:T(8,128)(2,1)S(1)} %pad_maximum_fusion.refs_0_.refs_2_), channel_id=1, source_target_pairs={{0,8},{8,16},{16,24},{24,32},{32,40},{40,48},{48,56},{56,0},{64,72... | collective-permute-start | bytes 1966088 | tf_op jit(solution)/shard_map/ppermute | solution.py:131
  77.0 15.1 %collective-permute-start.7 = (bf16[5,512,128]{2,1,0:T(8,128)(2,1)S(1)}, bf16[5,512,128]{2,1,0:T(8,128)(2,1)S(1)}, u32[]{:S(2)}, u32[]{:S(2)}) collective-permute-start(bf16[5,512,128]{2,1,0:T(8,128)(2,1)S(1)} %pad_maximum_fusion.refs_0_.refs_2_), channel_id=1, source_target_pairs={{0,56},{8,0},{16,8},{24,16},{32,24},{40,32},{48,40},{56,48},{64,12... | collective-permute-start | bytes 1966088 | tf_op jit(solution)/shard_map/ppermute | solution.py:131
  90.2 14.7 %collective-permute-start.4 = (bf16[5,512,128]{2,1,0:T(8,128)(2,1)S(1)}, bf16[5,512,128]{2,1,0:T(8,128)(2,1)}, u32[]{:S(2)}, u32[]{:S(2)}) collective-permute-start(bf16[5,512,128]{2,1,0:T(8,128)(2,1)S(1)} %collective-permute-done.3.refs_0_.refs_3_), channel_id=1, source_target_pairs={{0,8},{8,16},{16,24},{24,32},{32,40},{40,48},{48,56},{56,0},{64,72... | collective-permute-start | bytes 1966088 | tf_op jit(solution)/shard_map/ppermute | solution.py:131
  92.1 14.7 %collective-permute-start.8 = (bf16[5,512,128]{2,1,0:T(8,128)(2,1)S(1)}, bf16[5,512,128]{2,1,0:T(8,128)(2,1)}, u32[]{:S(2)}, u32[]{:S(2)}) collective-permute-start(bf16[5,512,128]{2,1,0:T(8,128)(2,1)S(1)} %collective-permute-done.7.refs_1_), channel_id=1, source_target_pairs={{0,56},{8,0},{16,8},{24,16},{32,24},{40,32},{48,40},{56,48},{64,12... | collective-permute-start | bytes 1966088 | tf_op jit(solution)/shard_map/ppermute | solution.py:131
  97.3 0.8 copy-start
  104.9 17.9 %collective-permute-start.5 = (bf16[5,512,128]{2,1,0:T(8,128)(2,1)}, bf16[5,512,128]{2,1,0:T(8,128)(2,1)S(1)}, u32[]{:S(2)}, u32[]{:S(2)}) collective-permute-start(bf16[5,512,128]{2,1,0:T(8,128)(2,1)} %collective-permute-done.4.refs_0_), channel_id=1, source_target_pairs={{0,8},{8,16},{16,24},{24,32},{32,40},{40,48},{48,56},{56,0},{64,72... | collective-permute-start | bytes 1966088 | tf_op jit(solution)/shard_map/ppermute | solution.py:131
  106.8 20.9 %collective-permute-start.9 = (bf16[5,512,128]{2,1,0:T(8,128)(2,1)}, bf16[5,512,128]{2,1,0:T(8,128)(2,1)S(1)}, u32[]{:S(2)}, u32[]{:S(2)}) collective-permute-start(bf16[5,512,128]{2,1,0:T(8,128)(2,1)} %collective-permute-done.8.refs_1_), channel_id=1, source_target_pairs={{0,56},{8,0},{16,8},{24,16},{32,24},{40,32},{48,40},{56,48},{64,12... | collective-permute-start | bytes 1966088 | tf_op jit(solution)/shard_map/ppermute | solution.py:131
  112.0 35.8 %collective-permute-start.11 = (bf16[1,512,128]{2,1,0:T(8,128)(2,1)S(1)}, bf16[1,512,128]{2,1,0:T(8,128)(2,1)S(1)}, u32[]{:S(2)}, u32[]{:S(2)}) collective-permute-start(bf16[1,512,128]{2,1,0:T(8,128)(2,1)S(1)} %pad_maximum_fusion.2), channel_id=1, source_target_pairs={{56,320},{120,384},{184,448},{248,0},{312,64},{376,128},{440,192},... | collective-permute-start | bytes 393224 | tf_op jit(solution)/shard_map/ppermute | solution.py:208
  122.8 24.9 %collective-permute-start.6 = (bf16[3,512,128]{2,1,0:T(8,128)(2,1)S(1)}, bf16[3,512,128]{2,1,0:T(8,128)(2,1)S(1)}, u32[]{:S(2)}, u32[]{:S(2)}) collective-permute-start(bf16[3,512,128]{2,1,0:T(8,128)(2,1)S(1)} %slice.24), channel_id=1, source_target_pairs={{0,8},{8,16},{16,24},{24,32},{32,40},{40,48},{48,56},{56,0},{64,72... | collective-permute-start | bytes 1179656 | tf_op jit(solution)/shard_map/ppermute | solution.py:131
  124.9 8.0 %copy-start.1 = (bf16[5,512,128]{2,1,0:T(8,128)(2,1)S(1)}, bf16[5,512,128]{2,1,0:T(8,128)(2,1)}, u32[]{:S(2)}) copy-start(bf16[5,512,128]{2,1,0:T(8,128)(2,1)} %copy-done) | copy-start | bytes 1966084
  127.7 20.0 %collective-permute-start.10 = (bf16[2,512,128]{2,1,0:T(8,128)(2,1)S(1)}, bf16[2,512,128]{2,1,0:T(8,128)(2,1)S(1)}, u32[]{:S(2)}, u32[]{:S(2)}) collective-permute-start(bf16[2,512,128]{2,1,0:T(8,128)(2,1)S(1)} %slice.25), channel_id=1, source_target_pairs={{0,56},{8,0},{16,8},{24,16},{32,24},{40,32},{48,40},{56,48},{64,12... | collective-permute-start | bytes 786440 | tf_op jit(solution)/shard_map/ppermute | solution.py:131
  155.4 4.6 %collective-permute-start.12 = (bf16[4,256,512]{2,1,0:T(8,128)(2,1)S(1)}, bf16[4,256,512]{2,1,0:T(8,128)(2,1)S(1)}, u32[]{:S(2)}, u32[]{:S(2)}) collective-permute-start(bf16[4,256,512]{2,1,0:T(8,128)(2,1)S(1)} %slice_bitcast_fusion), channel_id=1, source_target_pairs={{0,1},{1,0},{2,3},{3,2},{4,5},{5,4},{6,7},{7,6},{8,9},{9,8},{10,11... | collective-permute-start | bytes 3145736 | tf_op jit(solution)/shard_map/ppermute | solution.py:213
Sparse Core Ops, SparseCore 0:
  32.1 68.4 all-gather.1

commit v4 on v3

--- a/solution.py
+++ b/solution.py
@@ -89,36 +89,28 @@
     )(where, queries, starts, *arrays, *given)
 
 
-def project(where, attended, weight):
-    tok, depth = attended.shape
-    groups = 8
-    weight = weight.reshape(groups, -1, depth)
-    cols = weight.shape[1]
-
-    def kernel(where_ref, attended_ref, weight_ref, out_ref, held, sems):
-        copies = [
-            pltpu.make_async_copy(weight_ref.at[group], held.at[group], sems.at[group]) for group in range(groups)
-        ]
-        for copy in copies:
-            copy.start()
-        core = where_ref[3]
-        for group in range(groups):
-            copies[group].wait()
-            sent = jnp.bitwise_xor(core, group % 2)
-            out_ref[sent, group // 2] = lax.dot_general(
-                attended_ref[...], held[group], (((1,), (1,)), ((), ())), preferred_element_type=jnp.float32
+def project(where, attended, weights):
+    tok, _ = attended.shape
+    cols = weights[0][0].shape[0]
+
+    def kernel(where_ref, attended_ref, *refs):
+        *weight_refs, out_ref = refs
+        core, plane = where_ref[3], where_ref[0] // 8
+        for weight_ref, (_, distance) in zip(weight_refs, weights):
+            owner = lax.rem(plane + 8 - distance, 8)
+            out_ref[jnp.bitwise_xor(owner & 1, core), owner >> 1] = lax.dot_general(
+                attended_ref[...], weight_ref[...], (((1,), (1,)), ((), ())), preferred_element_type=jnp.float32
             ).astype(jnp.bfloat16)
 
     vmem = pl.BlockSpec(memory_space=pltpu.VMEM)
     return pl.pallas_call(
         kernel,
-        out_shape=jax.ShapeDtypeStruct((2, groups // 2, tok, cols), jnp.bfloat16),
-        in_specs=[pl.BlockSpec(memory_space=pltpu.SMEM), vmem, pl.BlockSpec(memory_space=pltpu.HBM)],
+        out_shape=jax.ShapeDtypeStruct((2, 4, tok, cols), jnp.bfloat16),
+        in_specs=[pl.BlockSpec(memory_space=pltpu.SMEM)] + [vmem] * (1 + len(weights)),
         out_specs=vmem,
-        scratch_shapes=[pltpu.VMEM(weight.shape, jnp.bfloat16), pltpu.SemaphoreType.DMA((groups,))],
         compiler_params=pltpu.CompilerParams(vmem_limit_bytes=16 * 1024 * 1024),
         name="project",
-    )(where, attended, pltpu.with_memory_space_constraint(weight, pltpu.HBM))
+    )(where, attended, *[weight for weight, _ in weights])
 
 
 def down_column(array, steps):
@@ -153,14 +145,6 @@
         axis_index_groups=[[8 * z + y for y in range(8)] for z in range(8)],
         tiled=True,
     ).reshape(8 * turned.shape[0], turned.shape[1])
-    weight = lax.all_gather(
-        weight,
-        "seq",
-        axis=0,
-        axis_index_groups=[[8 * z + y for z in range(8)] for y in range(8)],
-        tiled=True,
-    )
-
     ends = jnp.cumsum(doc_lengths)
     position = me * tok + jnp.arange(tok, dtype=jnp.int32)
     starts = jnp.max(jnp.where(ends[None, :] <= position[:, None], ends[None, :], 0), axis=1)
@@ -191,24 +175,30 @@
         numbers = [jnp.where(number > me, -1, number) for number in numbers]
         blocks = [(up, a, numbers[a]) for a in range(3)] + [(down, a, numbers[3 + a]) for a in range(2)]
         yield blocks, -4, False
-        yield [(column, 4, me - 32)], -32, False
         beyond = jnp.where(place > 0, me - 33, -1)
-        blocks = [(first_up, 4, beyond), (edge, 0, jnp.where(place > 0, -1, me - 33))]
-        yield blocks, -33, False
+        blocks = [(column, 4, me - 32), (first_up, 4, beyond), (edge, 0, jnp.where(place > 0, -1, me - 33))]
+        yield blocks, -32, False
 
     state, arrays, plan = None, [column], own_plan
     up = down = column
+    ahead = behind = weight
+    weights = [(weight, 0)]
     for turn in range(1, 5):
         up = along_row(up if turn < 4 else up[:3], 1)
         down = along_row(down if turn < 4 else down[3:], -1)
         if turn == 1:
             first_up = up
         state = attend(where, queries, starts, arrays, plan, state)
+        behind = down_column(behind, -1)
+        weights.append((behind, 8 - turn))
+        if turn < 4:
+            ahead = down_column(ahead, 1)
+            weights.append((ahead, turn))
         arrays, plan = [up, down], turn_plan(turn)
     edge = lax.ppermute(column[:1], "seq", [(8 * z + 7, 8 * ((z + 5) % 8)) for z in range(8)])
     arrays = [up, down, column, first_up, edge]
     (attended,) = attend(where, queries, starts, arrays, last_plan, state, True)
-    partial = project(where, attended, weight)
+    partial = project(where, attended, weights)
 
     other = lax.ppermute(partial[1], "head", [(h, h ^ 1) for h in range(8)])
     both = (partial[0].astype(jnp.float32) + other.astype(jnp.float32)).astype(jnp.bfloat16)

time: 188 us -> 172 us (0.915)
  the two profiles are of different devices: /device:TPU:128 before, /device:TPU:320 now
where the time goes in v4:
time: 172 us; the launch traced here: 171 us
  starting transfers between devices  79.4 us (46%)
  waiting for transfers between devices  34.4 us (20%)
  Pallas kernels  26 us (15%)
  blocking collectives  19.5 us (11%)
  local copies, waits for them, and re-layouts  5.36 us (3%)
  other arithmetic  3.14 us (2%)
  between operations  3 us (2%)
    ppermute x10, starting transfers between devices, down_column(): lax.ppermute(array, 'seq', [(8 * z + y, 8 * ((z + steps) % 8) + y) for z...  41.3 us
    ppermute x8, starting transfers between devices, along_row(): lax.ppermute(array, 'seq', [(8 * z + y, 8 * z + (y + steps) % 8) for z in...  27.6 us
    ppermute x10, waiting for transfers between devices, down_column(): lax.ppermute(array, 'seq', [(8 * z + y, 8 * ((z + steps) % 8) + y) for z...  26 us
    pallas_call x5, Pallas kernels, attend(): pl.pallas_call(kernel, out_shape=out_shape, in_specs=[pl.BlockSpec(memory...  23 us
    all_to_all x1, blocking collectives, layer(): lax.all_to_all(both, 'head', 0, 0, axis_index_groups=[[0, 2, 4, 6], [1, 3...  19.5 us
    all_to_all x1, starting transfers between devices, layer(): lax.all_to_all(jnp.broadcast_to(turned[None], (8,) + turned.shape), 'seq'...  7.23 us
    ppermute x8, waiting for transfers between devices, along_row(): lax.ppermute(array, 'seq', [(8 * z + y, 8 * z + (y + steps) % 8) for z in...  5.72 us
  transfers between devices with their start and end apart: 21, of which 7 were waited for; matrix products, arithmetic and copies ran while one was open for 3% of the time, Pallas kernels for 13%

profile of v4, /device:TPU:320, one launch (start us, length us, event | category | flops | bytes accessed | tf_op | source)
XLA Modules:
  0.0 170.7 jit_solution(332468604072664700)
XLA Ops:
  1.6 3.4 %collective-permute-start = (bf16[1,512,128]{2,1,0:T(8,128)(2,1)}, bf16[1,512,128]{2,1,0:T(8,128)(2,1)S(1)}, u32[]{:S(2)}, u32[]{:S(2)}) collective-permute-start(bf16[1,512,128]{2,1,0:T(8,128)(2,1)} %pad_maximum_fusion.2), channel_id=1, source_target_pairs={{0,64},{8,72},{16,80},{24,88},{32,96},{40,104},{48,112},{56,120},{... | collective-permute-start | bytes 393224 | tf_op jit(solution)/shard_map/ppermute | solution.py:117
  6.7 7.2 %all-to-all-start = ((bf16[8,64,512]{2,1,0:T(8,128)(2,1)}), bf16[8,64,512]{2,1,0:T(8,128)(2,1)S(1)}, u32[]{:S(2)}, u32[]{:S(2)}) async-start(bf16[8,64,512]{2,1,0:T(8,128)(2,1)} %broadcast_in_dim.16), calls=%async_computation | async-start | bytes 1048576 | tf_op jit(solution)/shard_map/all_to_all | solution.py:140
  13.9 2.8 %collective-permute-start.1 = (bf16[2,512,128]{2,1,0:T(8,128)(2,1)S(1)}, bf16[2,512,128]{2,1,0:T(8,128)(2,1)S(1)}, u32[]{:S(2)}, u32[]{:S(2)}) collective-permute-start(bf16[2,512,128]{2,1,0:T(8,128)(2,1)S(1)} %pad_maximum_fusion.1), channel_id=1, source_target_pairs={{0,128},{8,136},{16,144},{24,152},{32,160},{40,168},{48,176},{56,1... | collective-permute-start | bytes 786440 | tf_op jit(solution)/shard_map/ppermute | solution.py:117
  16.8 5.1 %collective-permute-start.2 = (bf16[1,512,128]{2,1,0:T(8,128)(2,1)}, bf16[1,512,128]{2,1,0:T(8,128)(2,1)S(1)}, u32[]{:S(2)}, u32[]{:S(2)}) collective-permute-start(bf16[1,512,128]{2,1,0:T(8,128)(2,1)} %pad_maximum_fusion.2), channel_id=1, source_target_pairs={{0,256},{8,264},{16,272},{24,280},{32,288},{40,296},{48,304},{56,3... | collective-permute-start | bytes 393224 | tf_op jit(solution)/shard_map/ppermute | solution.py:117
  21.9 8.2 %collective-permute-done.2 = bf16[1,512,128]{2,1,0:T(8,128)(2,1)S(1)} collective-permute-done((bf16[1,512,128]{2,1,0:T(8,128)(2,1)}, bf16[1,512,128]{2,1,0:T(8,128)(2,1)S(1)}, u32[]{:S(2)}, u32[]{:S(2)}) %collective-permute-start.2) | collective-permute-done | bytes 131104 | tf_op jit(solution)/shard_map/ppermute | solution.py:117
  31.4 3.6 %collective-permute-start.3 = (bf16[5,512,128]{2,1,0:T(8,128)(2,1)S(1)}, bf16[5,512,128]{2,1,0:T(8,128)(2,1)S(1)}, u32[]{:S(2)}, u32[]{:S(2)}) collective-permute-start(bf16[5,512,128]{2,1,0:T(8,128)(2,1)S(1)} %pad_maximum_fusion.refs_0_.refs_2_), channel_id=1, source_target_pairs={{0,8},{8,16},{16,24},{24,32},{32,40},{40,48},{48,56},{56,0},{64,72... | collective-permute-start | bytes 1966088 | tf_op jit(solution)/shard_map/ppermute | solution.py:123
  35.0 3.4 %collective-permute-start.7 = (bf16[5,512,128]{2,1,0:T(8,128)(2,1)S(1)}, bf16[5,512,128]{2,1,0:T(8,128)(2,1)}, u32[]{:S(2)}, u32[]{:S(2)}) collective-permute-start(bf16[5,512,128]{2,1,0:T(8,128)(2,1)S(1)} %pad_maximum_fusion.refs_0_.refs_2_), channel_id=1, source_target_pairs={{0,56},{8,0},{16,8},{24,16},{32,24},{40,32},{48,40},{56,48},{64,12... | collective-permute-start | bytes 1966088 | tf_op jit(solution)/shard_map/ppermute | solution.py:123
  38.5 5.7 %collective-permute-start.12 = (bf16[512,512]{1,0:T(8,128)(2,1)S(1)}, bf16[512,512]{1,0:T(8,128)(2,1)S(1)}, u32[]{:S(2)}, u32[]{:S(2)}) collective-permute-start(bf16[512,512]{1,0:T(8,128)(2,1)S(1)} %bitcast.20), channel_id=1, source_target_pairs={{0,448},{8,456},{16,464},{24,472},{32,480},{40,488},{48,496},{56,5... | collective-permute-start | bytes 1572872 | tf_op jit(solution)/shard_map/ppermute | solution.py:117
  44.1 5.7 %collective-permute-done.3.refs_0_.refs_3_ = bf16[5,512,128]{2,1,0:T(8,128)(2,1)S(1)} collective-permute-done((bf16[5,512,128]{2,1,0:T(8,128)(2,1)S(1)}, bf16[5,512,128]{2,1,0:T(8,128)(2,1)S(1)}, u32[]{:S(2)}, u32[]{:S(2)}) %collective-permute-start.3) | collective-permute-done | bytes 655392 | tf_op jit(solution)/shard_map/ppermute | solution.py:123
  52.1 4.8 %collective-permute-start.8 = (bf16[5,512,128]{2,1,0:T(8,128)(2,1)}, bf16[5,512,128]{2,1,0:T(8,128)(2,1)}, u32[]{:S(2)}, u32[]{:S(2)}) collective-permute-start(bf16[5,512,128]{2,1,0:T(8,128)(2,1)} %collective-permute-done.7.refs_1_), channel_id=1, source_target_pairs={{0,56},{8,0},{16,8},{24,16},{32,24},{40,32},{48,40},{56,48},{64,12... | collective-permute-start | bytes 1966088 | tf_op jit(solution)/shard_map/ppermute | solution.py:123
  56.9 9.6 %collective-permute-start.13 = (bf16[512,512]{1,0:T(8,128)(2,1)S(1)}, bf16[512,512]{1,0:T(8,128)(2,1)S(1)}, u32[]{:S(2)}, u32[]{:S(2)}) collective-permute-start(bf16[512,512]{1,0:T(8,128)(2,1)S(1)} %bitcast.21), channel_id=1, source_target_pairs={{0,64},{8,72},{16,80},{24,88},{32,96},{40,104},{48,112},{56,120},{... | collective-permute-start | bytes 1572872 | tf_op jit(solution)/shard_map/ppermute | solution.py:117
  70.4 5.6 %collective-permute-done.13.refs_2_ = bf16[512,512]{1,0:T(8,128)(2,1)S(1)} collective-permute-done((bf16[512,512]{1,0:T(8,128)(2,1)S(1)}, bf16[512,512]{1,0:T(8,128)(2,1)S(1)}, u32[]{:S(2)}, u32[]{:S(2)}) %collective-permute-start.13) | collective-permute-done | bytes 524320 | tf_op jit(solution)/shard_map/ppermute | solution.py:117
  76.0 4.4 %collective-permute-start.15 = (bf16[512,512]{1,0:T(8,128)(2,1)S(1)}, bf16[512,512]{1,0:T(8,128)(2,1)}, u32[]{:S(2)}, u32[]{:S(2)}) collective-permute-start(bf16[512,512]{1,0:T(8,128)(2,1)S(1)} %collective-permute-done.13.refs_2_), channel_id=1, source_target_pairs={{0,64},{8,72},{16,80},{24,88},{32,96},{40,104},{48,112},{56,120},{... | collective-permute-start | bytes 1572872 | tf_op jit(solution)/shard_map/ppermute | solution.py:117
  82.4 4.6 %collective-permute-start.9 = (bf16[5,512,128]{2,1,0:T(8,128)(2,1)}, bf16[5,512,128]{2,1,0:T(8,128)(2,1)}, u32[]{:S(2)}, u32[]{:S(2)}) collective-permute-start(bf16[5,512,128]{2,1,0:T(8,128)(2,1)} %collective-permute-done.8.refs_1_), channel_id=1, source_target_pairs={{0,56},{8,0},{16,8},{24,16},{32,24},{40,32},{48,40},{56,48},{64,12... | collective-permute-start | bytes 1966088 | tf_op jit(solution)/shard_map/ppermute | solution.py:123
  89.0 4.5 %collective-permute-start.17 = (bf16[512,512]{1,0:T(8,128)(2,1)}, bf16[512,512]{1,0:T(8,128)(2,1)}, u32[]{:S(2)}, u32[]{:S(2)}) collective-permute-start(bf16[512,512]{1,0:T(8,128)(2,1)} %collective-permute-done.15.refs_4_), channel_id=1, source_target_pairs={{0,64},{8,72},{16,80},{24,88},{32,96},{40,104},{48,112},{56,120},{... | collective-permute-start | bytes 1572872 | tf_op jit(solution)/shard_map/ppermute | solution.py:117
  93.5 10.7 %collective-permute-done.16.refs_5_ = bf16[512,512]{1,0:T(8,128)(2,1)} collective-permute-done((bf16[512,512]{1,0:T(8,128)(2,1)}, bf16[512,512]{1,0:T(8,128)(2,1)}, u32[]{:S(2)}, u32[]{:S(2)}) %collective-permute-start.16) | collective-permute-done | bytes 524320 | tf_op jit(solution)/shard_map/ppermute | solution.py:117
  113.2 2.7 %attend.5 = (f32[4,256,256]{2,1,0:T(8,128)S(1)}, f32[4,256,128]{2,1,0:T(8,128)S(1)}) custom-call(s32[5]{0:T(128)S(1)} %stack.19.where_ref, bf16[4,256,128]{2,1,0:T(8,128)(2,1)S(1)} %bitcast.23, s32[256,128]{1,0:T(8,128)S(1)} %broadcast_in_dim.15.starts_ref, bf16[5,512,128]{2,1,0:T(8,128)(2,1)S(1)} %pad_maximum_fusion.refs_0_.refs_2_), custom_call_target="tpu_custom_call" | custom-call | flops 1073741824 | bytes 1048576 | tf_op jit(solution)/shard_map/attend/pallas_call | solution.py:75
  116.9 5.1 %collective-permute-start.10 = (bf16[2,512,128]{2,1,0:T(8,128)(2,1)S(1)}, bf16[2,512,128]{2,1,0:T(8,128)(2,1)S(1)}, u32[]{:S(2)}, u32[]{:S(2)}) collective-permute-start(bf16[2,512,128]{2,1,0:T(8,128)(2,1)S(1)} %slice.25), channel_id=1, source_target_pairs={{0,56},{8,0},{16,8},{24,16},{32,24},{40,32},{48,40},{56,48},{64,12... | collective-permute-start | bytes 786440 | tf_op jit(solution)/shard_map/ppermute | solution.py:123
  122.1 5.0 %attend.6 = (f32[4,256,256]{2,1,0:T(8,128)S(1)}, f32[4,256,128]{2,1,0:T(8,128)S(1)}) custom-call(s32[5]{0:T(128)S(1)} %stack.19.where_ref, bf16[4,256,128]{2,1,0:T(8,128)(2,1)S(1)} %bitcast.24, s32[256,128]{1,0:T(8,128)S(1)} %broadcast_in_dim.15.starts_ref, ...), custom_call_target="tpu_custom_call", output_to_operand_aliasing={{0}: (5, {}), {1}: (6, {})} | custom-call | flops 1073741824 | bytes 1048576 | tf_op jit(solution)/shard_map/attend/pallas_call | solution.py:75
  127.1 5.4 %attend.7 = (f32[4,256,256]{2,1,0:T(8,128)S(1)}, f32[4,256,128]{2,1,0:T(8,128)S(1)}) custom-call(s32[5]{0:T(128)S(1)} %stack.19.where_ref, bf16[4,256,128]{2,1,0:T(8,128)(2,1)S(1)} %bitcast.25, s32[256,128]{1,0:T(8,128)S(1)} %broadcast_in_dim.15.starts_ref, ...), custom_call_target="tpu_custom_call", output_to_operand_aliasing={{0}: (5, {}), {1}: (6, {})} | custom-call | flops 1073741824 | bytes 1048576 | tf_op jit(solution)/shard_map/attend/pallas_call | solution.py:75
  132.5 5.2 %attend.8 = (f32[4,256,256]{2,1,0:T(8,128)S(1)}, f32[4,256,128]{2,1,0:T(8,128)S(1)}) custom-call(s32[5]{0:T(128)S(1)} %stack.19.where_ref, bf16[4,256,128]{2,1,0:T(8,128)(2,1)S(1)} %bitcast.26, s32[256,128]{1,0:T(8,128)S(1)} %broadcast_in_dim.15.starts_ref, ...), custom_call_target="tpu_custom_call", output_to_operand_aliasing={{0}: (5, {}), {1}: (6, {})} | custom-call | flops 1073741824 | bytes 1048576 | tf_op jit(solution)/shard_map/attend/pallas_call | solution.py:75
  137.8 4.6 %attend.9.attended_ref = bf16[256,512]{1,0:T(8,128)(2,1)S(1)} custom-call(s32[5]{0:T(128)S(1)} %stack.19.where_ref, bf16[4,256,128]{2,1,0:T(8,128)(2,1)S(1)} %bitcast.27, s32[256,128]{1,0:T(8,128)S(1)} %broadcast_in_dim.15.starts_ref, bf16[3,512,128]{2,1,0:T(8,128)(2,1)S(1)} %collective-permute-done.6.refs_0_, ...), custom_call_target="tpu_custom_call" | custom-call | flops 1073741824 | bytes 1048576 | tf_op jit(solution)/shard_map/attend/pallas_call | solution.py:75
  142.4 3.0 %project.1 = bf16[2,4,256,512]{3,2,1,0:T(8,128)(2,1)S(1)} custom-call(s32[5]{0:T(128)S(1)} %stack.19.where_ref, bf16[256,512]{1,0:T(8,128)(2,1)S(1)} %attend.9.attended_ref, bf16[512,512]{1,0:T(8,128)(2,1)S(1)} %bitcast.22, bf16[512,512]{1,0:T(8,128)(2,1)S(1)} %collective-permute-done.12.refs_1_, bf16[512,512]{1,0:T(8,128)(2,1)S(1)} %collective-permute-done.13.refs_2_, ...), custom_call_target="tpu_custom_call" | custom-call | tf_op jit(solution)/shard_map/project/pallas_call | solution.py:106
  150.4 19.5 %all_to_all.10 = bf16[4,256,512]{2,1,0:T(8,128)(2,1)S(1)} all-to-all(bf16[4,256,512]{2,1,0:T(8,128)(2,1)S(1)} %fusion), channel_id=1, replica_groups={{0,2,4,6},{1,3,5,7},{8,10,12,14},{9,11,13,15},{16,18,20,22},{17,19,21,2..., dimensions={0} | all-to-all | bytes 2097152 | tf_op jit(solution)/shard_map/all_to_all | solution.py:205
  (51 shorter events, 27.9 us)
Async XLA Ops:
  0.0 13.9 %copy-start = (bf16[256,1,128]{2,0,1:T(8,128)(2,1)S(1)}, bf16[256,1,128]{2,0,1:T(8,128)(2,1)}, u32[]{:S(2)}) copy-start(bf16[256,1,128]{2,0,1:T(8,128)(2,1)} %param.7) | copy-start | bytes 196612
  1.6 12.3 %collective-permute-start = (bf16[1,512,128]{2,1,0:T(8,128)(2,1)}, bf16[1,512,128]{2,1,0:T(8,128)(2,1)S(1)}, u32[]{:S(2)}, u32[]{:S(2)}) collective-permute-start(bf16[1,512,128]{2,1,0:T(8,128)(2,1)} %pad_maximum_fusion.2), channel_id=1, source_target_pairs={{0,64},{8,72},{16,80},{24,88},{32,96},{40,104},{48,112},{56,120},{... | collective-permute-start | bytes 393224 | tf_op jit(solution)/shard_map/ppermute | solution.py:117
  6.7 81.6 %copy-start.3 = (s32[64]{0:T(128)S(1)}, s32[64]{0:T(128)}, u32[]{:S(2)}) copy-start(s32[64]{0:T(128)} %param.9) | copy-start | bytes 772
  6.7 102.7 %copy-start.2 = (bf16[256,4,128]{2,1,0:T(4,128)(2,1)S(1)}, bf16[256,4,128]{2,1,0:T(4,128)(2,1)}, u32[]{:S(2)}) copy-start(bf16[256,4,128]{2,1,0:T(4,128)(2,1)} %param.5) | copy-start | bytes 786436
  6.7 31.8 %all-to-all-start = ((bf16[8,64,512]{2,1,0:T(8,128)(2,1)}), bf16[8,64,512]{2,1,0:T(8,128)(2,1)S(1)}, u32[]{:S(2)}, u32[]{:S(2)}) async-start(bf16[8,64,512]{2,1,0:T(8,128)(2,1)} %broadcast_in_dim.16), calls=%async_computation | async-start | bytes 1048576 | tf_op jit(solution)/shard_map/all_to_all | solution.py:140
  13.9 17.4 %collective-permute-start.1 = (bf16[2,512,128]{2,1,0:T(8,128)(2,1)S(1)}, bf16[2,512,128]{2,1,0:T(8,128)(2,1)S(1)}, u32[]{:S(2)}, u32[]{:S(2)}) collective-permute-start(bf16[2,512,128]{2,1,0:T(8,128)(2,1)S(1)} %pad_maximum_fusion.1), channel_id=1, source_target_pairs={{0,128},{8,136},{16,144},{24,152},{32,160},{40,168},{48,176},{56,1... | collective-permute-start | bytes 786440 | tf_op jit(solution)/shard_map/ppermute | solution.py:117
  16.8 13.3 %collective-permute-start.2 = (bf16[1,512,128]{2,1,0:T(8,128)(2,1)}, bf16[1,512,128]{2,1,0:T(8,128)(2,1)S(1)}, u32[]{:S(2)}, u32[]{:S(2)}) collective-permute-start(bf16[1,512,128]{2,1,0:T(8,128)(2,1)} %pad_maximum_fusion.2), channel_id=1, source_target_pairs={{0,256},{8,264},{16,272},{24,280},{32,288},{40,296},{48,304},{56,3... | collective-permute-start | bytes 393224 | tf_op jit(solution)/shard_map/ppermute | solution.py:117
  31.4 18.4 %collective-permute-start.3 = (bf16[5,512,128]{2,1,0:T(8,128)(2,1)S(1)}, bf16[5,512,128]{2,1,0:T(8,128)(2,1)S(1)}, u32[]{:S(2)}, u32[]{:S(2)}) collective-permute-start(bf16[5,512,128]{2,1,0:T(8,128)(2,1)S(1)} %pad_maximum_fusion.refs_0_.refs_2_), channel_id=1, source_target_pairs={{0,8},{8,16},{16,24},{24,32},{32,40},{40,48},{48,56},{56,0},{64,72... | collective-permute-start | bytes 1966088 | tf_op jit(solution)/shard_map/ppermute | solution.py:123
  35.0 17.0 %collective-permute-start.7 = (bf16[5,512,128]{2,1,0:T(8,128)(2,1)S(1)}, bf16[5,512,128]{2,1,0:T(8,128)(2,1)}, u32[]{:S(2)}, u32[]{:S(2)}) collective-permute-start(bf16[5,512,128]{2,1,0:T(8,128)(2,1)S(1)} %pad_maximum_fusion.refs_0_.refs_2_), channel_id=1, source_target_pairs={{0,56},{8,0},{16,8},{24,16},{32,24},{40,32},{48,40},{56,48},{64,12... | collective-permute-start | bytes 1966088 | tf_op jit(solution)/shard_map/ppermute | solution.py:123
  38.5 28.1 %collective-permute-start.12 = (bf16[512,512]{1,0:T(8,128)(2,1)S(1)}, bf16[512,512]{1,0:T(8,128)(2,1)S(1)}, u32[]{:S(2)}, u32[]{:S(2)}) collective-permute-start(bf16[512,512]{1,0:T(8,128)(2,1)S(1)} %bitcast.20), channel_id=1, source_target_pairs={{0,448},{8,456},{16,464},{24,472},{32,480},{40,488},{48,496},{56,5... | collective-permute-start | bytes 1572872 | tf_op jit(solution)/shard_map/ppermute | solution.py:117
  49.8 18.6 %collective-permute-start.4 = (bf16[5,512,128]{2,1,0:T(8,128)(2,1)S(1)}, bf16[5,512,128]{2,1,0:T(8,128)(2,1)}, u32[]{:S(2)}, u32[]{:S(2)}) collective-permute-start(bf16[5,512,128]{2,1,0:T(8,128)(2,1)S(1)} %collective-permute-done.3.refs_0_.refs_3_), channel_id=1, source_target_pairs={{0,8},{8,16},{16,24},{24,32},{32,40},{40,48},{48,56},{56,0},{64,72... | collective-permute-start | bytes 1966088 | tf_op jit(solution)/shard_map/ppermute | solution.py:123
  52.1 30.3 %collective-permute-start.8 = (bf16[5,512,128]{2,1,0:T(8,128)(2,1)}, bf16[5,512,128]{2,1,0:T(8,128)(2,1)}, u32[]{:S(2)}, u32[]{:S(2)}) collective-permute-start(bf16[5,512,128]{2,1,0:T(8,128)(2,1)} %collective-permute-done.7.refs_1_), channel_id=1, source_target_pairs={{0,56},{8,0},{16,8},{24,16},{32,24},{40,32},{48,40},{56,48},{64,12... | collective-permute-start | bytes 1966088 | tf_op jit(solution)/shard_map/ppermute | solution.py:123
  56.9 19.1 %collective-permute-start.13 = (bf16[512,512]{1,0:T(8,128)(2,1)S(1)}, bf16[512,512]{1,0:T(8,128)(2,1)S(1)}, u32[]{:S(2)}, u32[]{:S(2)}) collective-permute-start(bf16[512,512]{1,0:T(8,128)(2,1)S(1)} %bitcast.21), channel_id=1, source_target_pairs={{0,64},{8,72},{16,80},{24,88},{32,96},{40,104},{48,112},{56,120},{... | collective-permute-start | bytes 1572872 | tf_op jit(solution)/shard_map/ppermute | solution.py:117
  66.5 13.8 %collective-permute-start.14 = (bf16[512,512]{1,0:T(8,128)(2,1)S(1)}, bf16[512,512]{1,0:T(8,128)(2,1)}, u32[]{:S(2)}, u32[]{:S(2)}) collective-permute-start(bf16[512,512]{1,0:T(8,128)(2,1)S(1)} %collective-permute-done.12.refs_1_), channel_id=1, source_target_pairs={{0,448},{8,456},{16,464},{24,472},{32,480},{40,488},{48,496},{56,5... | collective-permute-start | bytes 1572872 | tf_op jit(solution)/shard_map/ppermute | solution.py:117
  68.5 41.7 %collective-permute-start.5 = (bf16[5,512,128]{2,1,0:T(8,128)(2,1)}, bf16[5,512,128]{2,1,0:T(8,128)(2,1)}, u32[]{:S(2)}, u32[]{:S(2)}) collective-permute-start(bf16[5,512,128]{2,1,0:T(8,128)(2,1)} %collective-permute-done.4.refs_0_), channel_id=1, source_target_pairs={{0,8},{8,16},{16,24},{24,32},{32,40},{40,48},{48,56},{56,0},{64,72... | collective-permute-start | bytes 1966088 | tf_op jit(solution)/shard_map/ppermute | solution.py:123
  76.0 13.1 %collective-permute-start.15 = (bf16[512,512]{1,0:T(8,128)(2,1)S(1)}, bf16[512,512]{1,0:T(8,128)(2,1)}, u32[]{:S(2)}, u32[]{:S(2)}) collective-permute-start(bf16[512,512]{1,0:T(8,128)(2,1)S(1)} %collective-permute-done.13.refs_2_), channel_id=1, source_target_pairs={{0,64},{8,72},{16,80},{24,88},{32,96},{40,104},{48,112},{56,120},{... | collective-permute-start | bytes 1572872 | tf_op jit(solution)/shard_map/ppermute | solution.py:117
  80.4 23.9 %collective-permute-start.16 = (bf16[512,512]{1,0:T(8,128)(2,1)}, bf16[512,512]{1,0:T(8,128)(2,1)}, u32[]{:S(2)}, u32[]{:S(2)}) collective-permute-start(bf16[512,512]{1,0:T(8,128)(2,1)} %collective-permute-done.14.refs_3_), channel_id=1, source_target_pairs={{0,448},{8,456},{16,464},{24,472},{32,480},{40,488},{48,496},{56,5... | collective-permute-start | bytes 1572872 | tf_op jit(solution)/shard_map/ppermute | solution.py:117
  82.4 33.6 %collective-permute-start.9 = (bf16[5,512,128]{2,1,0:T(8,128)(2,1)}, bf16[5,512,128]{2,1,0:T(8,128)(2,1)}, u32[]{:S(2)}, u32[]{:S(2)}) collective-permute-start(bf16[5,512,128]{2,1,0:T(8,128)(2,1)} %collective-permute-done.8.refs_1_), channel_id=1, source_target_pairs={{0,56},{8,0},{16,8},{24,16},{32,24},{40,32},{48,40},{56,48},{64,12... | collective-permute-start | bytes 1966088 | tf_op jit(solution)/shard_map/ppermute | solution.py:123
  87.0 50.7 %collective-permute-start.11 = (bf16[1,512,128]{2,1,0:T(8,128)(2,1)}, bf16[1,512,128]{2,1,0:T(8,128)(2,1)S(1)}, u32[]{:S(2)}, u32[]{:S(2)}) collective-permute-start(bf16[1,512,128]{2,1,0:T(8,128)(2,1)} %pad_maximum_fusion.2), channel_id=1, source_target_pairs={{56,320},{120,384},{184,448},{248,0},{312,64},{376,128},{440,192},... | collective-permute-start | bytes 393224 | tf_op jit(solution)/shard_map/ppermute | solution.py:198
  89.0 53.4 %collective-permute-start.17 = (bf16[512,512]{1,0:T(8,128)(2,1)}, bf16[512,512]{1,0:T(8,128)(2,1)}, u32[]{:S(2)}, u32[]{:S(2)}) collective-permute-start(bf16[512,512]{1,0:T(8,128)(2,1)} %collective-permute-done.15.refs_4_), channel_id=1, source_target_pairs={{0,64},{8,72},{16,80},{24,88},{32,96},{40,104},{48,112},{56,120},{... | collective-permute-start | bytes 1572872 | tf_op jit(solution)/shard_map/ppermute | solution.py:117
  104.2 38.2 %collective-permute-start.18 = (bf16[512,512]{1,0:T(8,128)(2,1)}, bf16[512,512]{1,0:T(8,128)(2,1)}, u32[]{:S(2)}, u32[]{:S(2)}) collective-permute-start(bf16[512,512]{1,0:T(8,128)(2,1)} %collective-permute-done.16.refs_5_), channel_id=1, source_target_pairs={{0,448},{8,456},{16,464},{24,472},{32,480},{40,488},{48,496},{56,5... | collective-permute-start | bytes 1572872 | tf_op jit(solution)/shard_map/ppermute | solution.py:117
  111.2 26.5 %collective-permute-start.6 = (bf16[3,512,128]{2,1,0:T(8,128)(2,1)S(1)}, bf16[3,512,128]{2,1,0:T(8,128)(2,1)S(1)}, u32[]{:S(2)}, u32[]{:S(2)}) collective-permute-start(bf16[3,512,128]{2,1,0:T(8,128)(2,1)S(1)} %slice.24), channel_id=1, source_target_pairs={{0,8},{8,16},{16,24},{24,32},{32,40},{40,48},{48,56},{56,0},{64,72... | collective-permute-start | bytes 1179656 | tf_op jit(solution)/shard_map/ppermute | solution.py:123
  116.9 20.8 %collective-permute-start.10 = (bf16[2,512,128]{2,1,0:T(8,128)(2,1)S(1)}, bf16[2,512,128]{2,1,0:T(8,128)(2,1)S(1)}, u32[]{:S(2)}, u32[]{:S(2)}) collective-permute-start(bf16[2,512,128]{2,1,0:T(8,128)(2,1)S(1)} %slice.25), channel_id=1, source_target_pairs={{0,56},{8,0},{16,8},{24,16},{32,24},{40,32},{48,40},{56,48},{64,12... | collective-permute-start | bytes 786440 | tf_op jit(solution)/shard_map/ppermute | solution.py:123
  145.5 4.6 %collective-permute-start.19 = (bf16[4,256,512]{2,1,0:T(8,128)(2,1)S(1)}, bf16[4,256,512]{2,1,0:T(8,128)(2,1)S(1)}, u32[]{:S(2)}, u32[]{:S(2)}) collective-permute-start(bf16[4,256,512]{2,1,0:T(8,128)(2,1)S(1)} %slice_bitcast_fusion), channel_id=1, source_target_pairs={{0,1},{1,0},{2,3},{3,2},{4,5},{5,4},{6,7},{7,6},{8,9},{9,8},{10,11... | collective-permute-start | bytes 3145736 | tf_op jit(solution)/shard_map/ppermute | solution.py:203
  (1 other events, 13.9 us)

commit v5 on v4

--- a/solution.py
+++ b/solution.py
@@ -89,12 +89,13 @@
     )(where, queries, starts, *arrays, *given)
 
 
-def project(where, attended, weights):
+def project(where, attended, weights, partial=None):
     tok, _ = attended.shape
     cols = weights[0][0].shape[0]
+    given = [] if partial is None else [partial]
 
     def kernel(where_ref, attended_ref, *refs):
-        *weight_refs, out_ref = refs
+        weight_refs, out_ref = refs[: len(weights)], refs[-1]
         core, plane = where_ref[3], where_ref[0] // 8
         for weight_ref, (_, distance) in zip(weight_refs, weights):
             owner = lax.rem(plane + 8 - distance, 8)
@@ -106,11 +107,12 @@
     return pl.pallas_call(
         kernel,
         out_shape=jax.ShapeDtypeStruct((2, 4, tok, cols), jnp.bfloat16),
-        in_specs=[pl.BlockSpec(memory_space=pltpu.SMEM)] + [vmem] * (1 + len(weights)),
+        in_specs=[pl.BlockSpec(memory_space=pltpu.SMEM)] + [vmem] * (1 + len(weights) + len(given)),
         out_specs=vmem,
+        input_output_aliases={2 + len(weights): 0} if given else {},
         compiler_params=pltpu.CompilerParams(vmem_limit_bytes=16 * 1024 * 1024),
         name="project",
-    )(where, attended, *[weight for weight, _ in weights])
+    )(where, attended, *[weight for weight, _ in weights], *given)
 
 
 def down_column(array, steps):
@@ -148,7 +150,7 @@
     ends = jnp.cumsum(doc_lengths)
     position = me * tok + jnp.arange(tok, dtype=jnp.int32)
     starts = jnp.max(jnp.where(ends[None, :] <= position[:, None], ends[None, :], 0), axis=1)
-    where = jnp.stack([me, starts[0] // tok, starts[-1], core, me % 8]).astype(jnp.int32)
+    where = jnp.stack([me, starts[0] // tok, starts[-1], core]).astype(jnp.int32)
     starts = jnp.broadcast_to(starts[:, None], (tok, 128))
     queries = jnp.transpose(queries, (1, 0, 2))
 
@@ -159,7 +161,8 @@
 
     def turn_plan(turn):
         def plan(where_ref, refs):
-            me, place = where_ref[0], where_ref[4]
+            me = where_ref[0]
+            place = lax.rem(me, 8)
             skip = jnp.where(place >= turn, 0, 1)
             yield [(refs[0], skip + a, me - turn - 8 * a) for a in range(4)], -turn, False
             skip = jnp.where(place + turn < 8, 1, 0)
@@ -168,7 +171,8 @@
         return plan
 
     def last_plan(where_ref, refs):
-        me, place = where_ref[0], where_ref[4]
+        me = where_ref[0]
+        place = lax.rem(me, 8)
         up, down, column, first_up, edge = refs
         shift = jnp.where(place >= 4, -4, 4)
         numbers = [me + shift - 8 * a for a in range(5)]
@@ -198,7 +202,8 @@
     edge = lax.ppermute(column[:1], "seq", [(8 * z + 7, 8 * ((z + 5) % 8)) for z in range(8)])
     arrays = [up, down, column, first_up, edge]
     (attended,) = attend(where, queries, starts, arrays, last_plan, state, True)
-    partial = project(where, attended, weights)
+    partial = project(where, attended, weights[:6])
+    partial = project(where, attended, weights[6:], partial)
 
     other = lax.ppermute(partial[1], "head", [(h, h ^ 1) for h in range(8)])
     both = (partial[0].astype(jnp.float32) + other.astype(jnp.float32)).astype(jnp.bfloat16)

time: 172 us -> 170 us (0.988)
  the two profiles are of different devices: /device:TPU:320 before, /device:TPU:120 now
where the time goes in v5:
time: 170 us; the launch traced here: 169 us
  starting transfers between devices  96.8 us (57%)
  Pallas kernels  25.5 us (15%)
  blocking collectives  19.5 us (11%)
  waiting for transfers between devices  12.7 us (7%)
  local copies, waits for them, and re-layouts  6.19 us (4%)
  other arithmetic  5.3 us (3%)
  between operations  2.99 us (2%)
    ppermute x10, starting transfers between devices, down_column(): lax.ppermute(array, 'seq', [(8 * z + y, 8 * ((z + steps) % 8) + y) for z...  51.3 us
    ppermute x8, starting transfers between devices, along_row(): lax.ppermute(array, 'seq', [(8 * z + y, 8 * z + (y + steps) % 8) for z in...  24.1 us
    pallas_call x5, Pallas kernels, attend(): pl.pallas_call(kernel, out_shape=out_shape, in_specs=[pl.BlockSpec(memory...  22.2 us
    all_to_all x1, blocking collectives, layer(): lax.all_to_all(both, 'head', 0, 0, axis_index_groups=[[0, 2, 4, 6], [1, 3...  19.5 us
    ppermute x1, starting transfers between devices, layer(): lax.ppermute(column[:1], 'seq', [(8 * z + 7, 8 * ((z + 5) % 8)) for z in...  12.5 us
    ppermute x10, waiting for transfers between devices, down_column(): lax.ppermute(array, 'seq', [(8 * z + y, 8 * ((z + steps) % 8) + y) for z...  9.09 us
    all_to_all x1, starting transfers between devices, layer(): lax.all_to_all(jnp.broadcast_to(turned[None], (8,) + turned.shape), 'seq'...  7 us
  transfers between devices with their start and end apart: 21, of which 4 were waited for; matrix products, arithmetic and copies ran while one was open for 5% of the time, Pallas kernels for 14%

profile of v5, /device:TPU:120, one launch (start us, length us, event | category | flops | bytes accessed | tf_op | source)
XLA Modules:
  0.0 169.0 jit_solution(8621919269166762617)
XLA Ops:
  0.9 4.3 %collective-permute-start = (bf16[1,512,128]{2,1,0:T(8,128)(2,1)S(1)}, bf16[1,512,128]{2,1,0:T(8,128)(2,1)S(1)}, u32[]{:S(2)}, u32[]{:S(2)}) collective-permute-start(bf16[1,512,128]{2,1,0:T(8,128)(2,1)S(1)} %pad_maximum_fusion.2), channel_id=1, source_target_pairs={{0,64},{8,72},{16,80},{24,88},{32,96},{40,104},{48,112},{56,120},{... | collective-permute-start | bytes 393224 | tf_op jit(solution)/shard_map/ppermute | solution.py:119
  6.9 7.0 %all-to-all-start = ((bf16[8,64,512]{2,1,0:T(8,128)(2,1)}), bf16[8,64,512]{2,1,0:T(8,128)(2,1)S(1)}, u32[]{:S(2)}, u32[]{:S(2)}) async-start(bf16[8,64,512]{2,1,0:T(8,128)(2,1)} %broadcast_in_dim.16), calls=%async_computation | async-start | bytes 1048576 | tf_op jit(solution)/shard_map/all_to_all | solution.py:142
  14.0 7.3 %collective-permute-start.1 = (bf16[2,512,128]{2,1,0:T(8,128)(2,1)S(1)}, bf16[2,512,128]{2,1,0:T(8,128)(2,1)S(1)}, u32[]{:S(2)}, u32[]{:S(2)}) collective-permute-start(bf16[2,512,128]{2,1,0:T(8,128)(2,1)S(1)} %pad_maximum_fusion.1), channel_id=1, source_target_pairs={{0,128},{8,136},{16,144},{24,152},{32,160},{40,168},{48,176},{56,1... | collective-permute-start | bytes 786440 | tf_op jit(solution)/shard_map/ppermute | solution.py:119
  21.3 4.6 %collective-permute-start.2 = (bf16[1,512,128]{2,1,0:T(8,128)(2,1)S(1)}, bf16[1,512,128]{2,1,0:T(8,128)(2,1)S(1)}, u32[]{:S(2)}, u32[]{:S(2)}) collective-permute-start(bf16[1,512,128]{2,1,0:T(8,128)(2,1)S(1)} %pad_maximum_fusion.2), channel_id=1, source_target_pairs={{0,256},{8,264},{16,272},{24,280},{32,288},{40,296},{48,304},{56,3... | collective-permute-start | bytes 393224 | tf_op jit(solution)/shard_map/ppermute | solution.py:119
  25.9 7.9 %collective-permute-done.2 = bf16[1,512,128]{2,1,0:T(8,128)(2,1)S(1)} collective-permute-done((bf16[1,512,128]{2,1,0:T(8,128)(2,1)S(1)}, bf16[1,512,128]{2,1,0:T(8,128)(2,1)S(1)}, u32[]{:S(2)}, u32[]{:S(2)}) %collective-permute-start.2) | collective-permute-done | bytes 131104 | tf_op jit(solution)/shard_map/ppermute | solution.py:119
  33.9 2.7 %collective-permute-start.3 = (bf16[5,512,128]{2,1,0:T(8,128)(2,1)S(1)}, bf16[5,512,128]{2,1,0:T(8,128)(2,1)S(1)}, u32[]{:S(2)}, u32[]{:S(2)}) collective-permute-start(bf16[5,512,128]{2,1,0:T(8,128)(2,1)S(1)} %pad_maximum_fusion.refs_0_.refs_2_), channel_id=1, source_target_pairs={{0,8},{8,16},{16,24},{24,32},{32,40},{40,48},{48,56},{56,0},{64,72... | collective-permute-start | bytes 1966088 | tf_op jit(solution)/shard_map/ppermute | solution.py:125
  36.6 3.2 %collective-permute-start.7 = (bf16[5,512,128]{2,1,0:T(8,128)(2,1)S(1)}, bf16[5,512,128]{2,1,0:T(8,128)(2,1)}, u32[]{:S(2)}, u32[]{:S(2)}) collective-permute-start(bf16[5,512,128]{2,1,0:T(8,128)(2,1)S(1)} %pad_maximum_fusion.refs_0_.refs_2_), channel_id=1, source_target_pairs={{0,56},{8,0},{16,8},{24,16},{32,24},{40,32},{48,40},{56,48},{64,12... | collective-permute-start | bytes 1966088 | tf_op jit(solution)/shard_map/ppermute | solution.py:125
  39.8 7.9 %collective-permute-start.15 = (bf16[512,512]{1,0:T(8,128)(2,1)S(1)}, bf16[512,512]{1,0:T(8,128)(2,1)S(1)}, u32[]{:S(2)}, u32[]{:S(2)}) collective-permute-start(bf16[512,512]{1,0:T(8,128)(2,1)S(1)} %bitcast.19), channel_id=1, source_target_pairs={{0,448},{8,456},{16,464},{24,472},{32,480},{40,488},{48,496},{56,5... | collective-permute-start | bytes 1572872 | tf_op jit(solution)/shard_map/ppermute | solution.py:119
  48.6 3.7 %collective-permute-start.4 = (bf16[5,512,128]{2,1,0:T(8,128)(2,1)S(1)}, bf16[5,512,128]{2,1,0:T(8,128)(2,1)}, u32[]{:S(2)}, u32[]{:S(2)}) collective-permute-start(bf16[5,512,128]{2,1,0:T(8,128)(2,1)S(1)} %collective-permute-done.3.refs_0_.refs_3_), channel_id=1, source_target_pairs={{0,8},{8,16},{16,24},{24,32},{32,40},{40,48},{48,56},{56,0},{64,72... | collective-permute-start | bytes 1966088 | tf_op jit(solution)/shard_map/ppermute | solution.py:125
  52.4 2.1 %collective-permute-start.8 = (bf16[5,512,128]{2,1,0:T(8,128)(2,1)}, bf16[5,512,128]{2,1,0:T(8,128)(2,1)}, u32[]{:S(2)}, u32[]{:S(2)}) collective-permute-start(bf16[5,512,128]{2,1,0:T(8,128)(2,1)} %collective-permute-done.7.refs_1_), channel_id=1, source_target_pairs={{0,56},{8,0},{16,8},{24,16},{32,24},{40,32},{48,40},{56,48},{64,12... | collective-permute-start | bytes 1966088 | tf_op jit(solution)/shard_map/ppermute | solution.py:125
  54.5 11.0 %collective-permute-start.12 = (bf16[512,512]{1,0:T(8,128)(2,1)S(1)}, bf16[512,512]{1,0:T(8,128)(2,1)S(1)}, u32[]{:S(2)}, u32[]{:S(2)}) collective-permute-start(bf16[512,512]{1,0:T(8,128)(2,1)S(1)} %bitcast.20), channel_id=1, source_target_pairs={{0,64},{8,72},{16,80},{24,88},{32,96},{40,104},{48,112},{56,120},{... | collective-permute-start | bytes 1572872 | tf_op jit(solution)/shard_map/ppermute | solution.py:119
  67.4 4.6 %collective-permute-start.5 = (bf16[5,512,128]{2,1,0:T(8,128)(2,1)}, bf16[5,512,128]{2,1,0:T(8,128)(2,1)}, u32[]{:S(2)}, u32[]{:S(2)}) collective-permute-start(bf16[5,512,128]{2,1,0:T(8,128)(2,1)} %collective-permute-done.4.refs_0_), channel_id=1, source_target_pairs={{0,8},{8,16},{16,24},{24,32},{32,40},{40,48},{48,56},{56,0},{64,72... | collective-permute-start | bytes 1966088 | tf_op jit(solution)/shard_map/ppermute | solution.py:125
  73.2 6.5 %collective-permute-start.13 = (bf16[512,512]{1,0:T(8,128)(2,1)S(1)}, bf16[512,512]{1,0:T(8,128)(2,1)}, u32[]{:S(2)}, u32[]{:S(2)}) collective-permute-start(bf16[512,512]{1,0:T(8,128)(2,1)S(1)} %collective-permute-done.12.refs_2_), channel_id=1, source_target_pairs={{0,64},{8,72},{16,80},{24,88},{32,96},{40,104},{48,112},{56,120},{... | collective-permute-start | bytes 1572872 | tf_op jit(solution)/shard_map/ppermute | solution.py:119
  83.6 12.5 %collective-permute-start.11 = (bf16[1,512,128]{2,1,0:T(8,128)(2,1)}, bf16[1,512,128]{2,1,0:T(8,128)(2,1)S(1)}, u32[]{:S(2)}, u32[]{:S(2)}) collective-permute-start(bf16[1,512,128]{2,1,0:T(8,128)(2,1)} %copy-done.2), channel_id=1, source_target_pairs={{56,320},{120,384},{184,448},{248,0},{312,64},{376,128},{440,192},... | collective-permute-start | bytes 393224 | tf_op jit(solution)/shard_map/ppermute | solution.py:202
  104.4 3.9 %collective-permute-start.18 = (bf16[512,512]{1,0:T(8,128)(2,1)}, bf16[512,512]{1,0:T(8,128)(2,1)S(1)}, u32[]{:S(2)}, u32[]{:S(2)}) collective-permute-start(bf16[512,512]{1,0:T(8,128)(2,1)} %collective-permute-done.17.refs_5_), channel_id=1, source_target_pairs={{0,448},{8,456},{16,464},{24,472},{32,480},{40,488},{48,496},{56,5... | collective-permute-start | bytes 1572872 | tf_op jit(solution)/shard_map/ppermute | solution.py:119
  113.1 2.8 %attend.5 = (f32[4,256,256]{2,1,0:T(8,128)S(1)}, f32[4,256,128]{2,1,0:T(8,128)S(1)}) custom-call(s32[4]{0:T(128)S(1)} %pad_add_fusion.where_ref, bf16[4,256,128]{2,1,0:T(8,128)(2,1)S(1)} %bitcast.22, s32[256,128]{1,0:T(8,128)S(1)} %broadcast_in_dim.15.starts_ref, bf16[5,512,128]{2,1,0:T(8,128)(2,1)S(1)} %pad_maximum_fusion.refs_0_.refs_2_), custom_call_target="tpu_custom_call" | custom-call | flops 1073741824 | bytes 1048576 | tf_op jit(solution)/shard_map/attend/pallas_call | solution.py:75
  116.9 3.9 %collective-permute-start.10 = (bf16[2,512,128]{2,1,0:T(8,128)(2,1)S(1)}, bf16[2,512,128]{2,1,0:T(8,128)(2,1)S(1)}, u32[]{:S(2)}, u32[]{:S(2)}) collective-permute-start(bf16[2,512,128]{2,1,0:T(8,128)(2,1)S(1)} %slice.25), channel_id=1, source_target_pairs={{0,56},{8,0},{16,8},{24,16},{32,24},{40,32},{48,40},{56,48},{64,12... | collective-permute-start | bytes 786440 | tf_op jit(solution)/shard_map/ppermute | solution.py:125
  120.9 5.2 %attend.6 = (f32[4,256,256]{2,1,0:T(8,128)S(1)}, f32[4,256,128]{2,1,0:T(8,128)S(1)}) custom-call(s32[4]{0:T(128)S(1)} %pad_add_fusion.where_ref, bf16[4,256,128]{2,1,0:T(8,128)(2,1)S(1)} %bitcast.23, s32[256,128]{1,0:T(8,128)S(1)} %broadcast_in_dim.15.starts_ref, ...), custom_call_target="tpu_custom_call", output_to_operand_aliasing={{0}: (5, {}), {1}: (6, {})} | custom-call | flops 1073741824 | bytes 1048576 | tf_op jit(solution)/shard_map/attend/pallas_call | solution.py:75
  126.1 5.6 %attend.7 = (f32[4,256,256]{2,1,0:T(8,128)S(1)}, f32[4,256,128]{2,1,0:T(8,128)S(1)}) custom-call(s32[4]{0:T(128)S(1)} %pad_add_fusion.where_ref, bf16[4,256,128]{2,1,0:T(8,128)(2,1)S(1)} %bitcast.24, s32[256,128]{1,0:T(8,128)S(1)} %broadcast_in_dim.15.starts_ref, ...), custom_call_target="tpu_custom_call", output_to_operand_aliasing={{0}: (5, {}), {1}: (6, {})} | custom-call | flops 1073741824 | bytes 1048576 | tf_op jit(solution)/shard_map/attend/pallas_call | solution.py:75
  131.7 5.4 %attend.8 = (f32[4,256,256]{2,1,0:T(8,128)S(1)}, f32[4,256,128]{2,1,0:T(8,128)S(1)}) custom-call(s32[4]{0:T(128)S(1)} %pad_add_fusion.where_ref, bf16[4,256,128]{2,1,0:T(8,128)(2,1)S(1)} %bitcast.25, s32[256,128]{1,0:T(8,128)S(1)} %broadcast_in_dim.15.starts_ref, ...), custom_call_target="tpu_custom_call", output_to_operand_aliasing={{0}: (5, {}), {1}: (6, {})} | custom-call | flops 1073741824 | bytes 1048576 | tf_op jit(solution)/shard_map/attend/pallas_call | solution.py:75
  137.1 3.2 %attend.9.attended_ref = bf16[256,512]{1,0:T(8,128)(2,1)S(1)} custom-call(s32[4]{0:T(128)S(1)} %pad_add_fusion.where_ref, bf16[4,256,128]{2,1,0:T(8,128)(2,1)S(1)} %bitcast.26, s32[256,128]{1,0:T(8,128)S(1)} %broadcast_in_dim.15.starts_ref, bf16[3,512,128]{2,1,0:T(8,128)(2,1)S(1)} %collective-permute-done.6.refs_0_, ...), custom_call_target="tpu_custom_call" | custom-call | flops 1073741824 | bytes 1048576 | tf_op jit(solution)/shard_map/attend/pallas_call | solution.py:75
  140.3 2.3 %project.2.refs_2_ = bf16[2,4,256,512]{3,2,1,0:T(8,128)(2,1)S(1)} custom-call(s32[4]{0:T(128)S(1)} %pad_add_fusion.where_ref, bf16[256,512]{1,0:T(8,128)(2,1)S(1)} %attend.9.attended_ref, bf16[512,512]{1,0:T(8,128)(2,1)S(1)} %bitcast.21, bf16[512,512]{1,0:T(8,128)(2,1)S(1)} %collective-permute-done.15.refs_1_, ...), custom_call_target="tpu_custom_call" | custom-call | tf_op jit(solution)/shard_map/project/pallas_call | solution.py:107
  145.6 2.6 %collective-permute-done.19 = bf16[4,256,512]{2,1,0:T(8,128)(2,1)S(1)} collective-permute-done((bf16[4,256,512]{2,1,0:T(8,128)(2,1)S(1)}, bf16[4,256,512]{2,1,0:T(8,128)(2,1)S(1)}, u32[]{:S(2)}, u32[]{:S(2)}) %collective-permute-start.19) | collective-permute-done | bytes 1048608 | tf_op jit(solution)/shard_map/ppermute | solution.py:208
  148.6 19.5 %all_to_all.10 = bf16[4,256,512]{2,1,0:T(8,128)(2,1)S(1)} all-to-all(bf16[4,256,512]{2,1,0:T(8,128)(2,1)S(1)} %fusion), channel_id=1, replica_groups={{0,2,4,6},{1,3,5,7},{8,10,12,14},{9,11,13,15},{16,18,20,22},{17,19,21,2..., dimensions={0} | all-to-all | bytes 2097152 | tf_op jit(solution)/shard_map/all_to_all | solution.py:210
  (52 shorter events, 26.2 us)
Async XLA Ops:
  0.0 13.9 %copy-start = (bf16[256,1,128]{2,0,1:T(8,128)(2,1)S(1)}, bf16[256,1,128]{2,0,1:T(8,128)(2,1)}, u32[]{:S(2)}) copy-start(bf16[256,1,128]{2,0,1:T(8,128)(2,1)} %param.7) | copy-start | bytes 196612
  0.9 32.9 %copy-start.2 = (bf16[1,512,128]{2,1,0:T(8,128)(2,1)}, bf16[1,512,128]{2,1,0:T(8,128)(2,1)S(1)}, u32[]{:S(2)}) copy-start(bf16[1,512,128]{2,1,0:T(8,128)(2,1)S(1)} %pad_maximum_fusion.2) | copy-start | bytes 393220
  0.9 13.0 %collective-permute-start = (bf16[1,512,128]{2,1,0:T(8,128)(2,1)S(1)}, bf16[1,512,128]{2,1,0:T(8,128)(2,1)S(1)}, u32[]{:S(2)}, u32[]{:S(2)}) collective-permute-start(bf16[1,512,128]{2,1,0:T(8,128)(2,1)S(1)} %pad_maximum_fusion.2), channel_id=1, source_target_pairs={{0,64},{8,72},{16,80},{24,88},{32,96},{40,104},{48,112},{56,120},{... | collective-permute-start | bytes 393224 | tf_op jit(solution)/shard_map/ppermute | solution.py:119
  6.9 89.2 %copy-start.3 = (s32[64]{0:T(128)S(1)}, s32[64]{0:T(128)}, u32[]{:S(2)}) copy-start(s32[64]{0:T(128)} %param.9) | copy-start | bytes 772
  6.9 32.8 %all-to-all-start = ((bf16[8,64,512]{2,1,0:T(8,128)(2,1)}), bf16[8,64,512]{2,1,0:T(8,128)(2,1)S(1)}, u32[]{:S(2)}, u32[]{:S(2)}) async-start(bf16[8,64,512]{2,1,0:T(8,128)(2,1)} %broadcast_in_dim.16), calls=%async_computation | async-start | bytes 1048576 | tf_op jit(solution)/shard_map/all_to_all | solution.py:142
  14.0 19.9 %collective-permute-start.1 = (bf16[2,512,128]{2,1,0:T(8,128)(2,1)S(1)}, bf16[2,512,128]{2,1,0:T(8,128)(2,1)S(1)}, u32[]{:S(2)}, u32[]{:S(2)}) collective-permute-start(bf16[2,512,128]{2,1,0:T(8,128)(2,1)S(1)} %pad_maximum_fusion.1), channel_id=1, source_target_pairs={{0,128},{8,136},{16,144},{24,152},{32,160},{40,168},{48,176},{56,1... | collective-permute-start | bytes 786440 | tf_op jit(solution)/shard_map/ppermute | solution.py:119
  21.3 12.6 %collective-permute-start.2 = (bf16[1,512,128]{2,1,0:T(8,128)(2,1)S(1)}, bf16[1,512,128]{2,1,0:T(8,128)(2,1)S(1)}, u32[]{:S(2)}, u32[]{:S(2)}) collective-permute-start(bf16[1,512,128]{2,1,0:T(8,128)(2,1)S(1)} %pad_maximum_fusion.2), channel_id=1, source_target_pairs={{0,256},{8,264},{16,272},{24,280},{32,288},{40,296},{48,304},{56,3... | collective-permute-start | bytes 393224 | tf_op jit(solution)/shard_map/ppermute | solution.py:119
  33.9 14.7 %collective-permute-start.3 = (bf16[5,512,128]{2,1,0:T(8,128)(2,1)S(1)}, bf16[5,512,128]{2,1,0:T(8,128)(2,1)S(1)}, u32[]{:S(2)}, u32[]{:S(2)}) collective-permute-start(bf16[5,512,128]{2,1,0:T(8,128)(2,1)S(1)} %pad_maximum_fusion.refs_0_.refs_2_), channel_id=1, source_target_pairs={{0,8},{8,16},{16,24},{24,32},{32,40},{40,48},{48,56},{56,0},{64,72... | collective-permute-start | bytes 1966088 | tf_op jit(solution)/shard_map/ppermute | solution.py:125
  36.6 15.8 %collective-permute-start.7 = (bf16[5,512,128]{2,1,0:T(8,128)(2,1)S(1)}, bf16[5,512,128]{2,1,0:T(8,128)(2,1)}, u32[]{:S(2)}, u32[]{:S(2)}) collective-permute-start(bf16[5,512,128]{2,1,0:T(8,128)(2,1)S(1)} %pad_maximum_fusion.refs_0_.refs_2_), channel_id=1, source_target_pairs={{0,56},{8,0},{16,8},{24,16},{32,24},{40,32},{48,40},{56,48},{64,12... | collective-permute-start | bytes 1966088 | tf_op jit(solution)/shard_map/ppermute | solution.py:125
  39.8 25.7 %collective-permute-start.15 = (bf16[512,512]{1,0:T(8,128)(2,1)S(1)}, bf16[512,512]{1,0:T(8,128)(2,1)S(1)}, u32[]{:S(2)}, u32[]{:S(2)}) collective-permute-start(bf16[512,512]{1,0:T(8,128)(2,1)S(1)} %bitcast.19), channel_id=1, source_target_pairs={{0,448},{8,456},{16,464},{24,472},{32,480},{40,488},{48,496},{56,5... | collective-permute-start | bytes 1572872 | tf_op jit(solution)/shard_map/ppermute | solution.py:119
  48.6 18.8 %collective-permute-start.4 = (bf16[5,512,128]{2,1,0:T(8,128)(2,1)S(1)}, bf16[5,512,128]{2,1,0:T(8,128)(2,1)}, u32[]{:S(2)}, u32[]{:S(2)}) collective-permute-start(bf16[5,512,128]{2,1,0:T(8,128)(2,1)S(1)} %collective-permute-done.3.refs_0_.refs_3_), channel_id=1, source_target_pairs={{0,8},{8,16},{16,24},{24,32},{32,40},{40,48},{48,56},{56,0},{64,72... | collective-permute-start | bytes 1966088 | tf_op jit(solution)/shard_map/ppermute | solution.py:125
  52.4 29.3 %collective-permute-start.8 = (bf16[5,512,128]{2,1,0:T(8,128)(2,1)}, bf16[5,512,128]{2,1,0:T(8,128)(2,1)}, u32[]{:S(2)}, u32[]{:S(2)}) collective-permute-start(bf16[5,512,128]{2,1,0:T(8,128)(2,1)} %collective-permute-done.7.refs_1_), channel_id=1, source_target_pairs={{0,56},{8,0},{16,8},{24,16},{32,24},{40,32},{48,40},{56,48},{64,12... | collective-permute-start | bytes 1966088 | tf_op jit(solution)/shard_map/ppermute | solution.py:125
  54.5 18.7 %collective-permute-start.12 = (bf16[512,512]{1,0:T(8,128)(2,1)S(1)}, bf16[512,512]{1,0:T(8,128)(2,1)S(1)}, u32[]{:S(2)}, u32[]{:S(2)}) collective-permute-start(bf16[512,512]{1,0:T(8,128)(2,1)S(1)} %bitcast.20), channel_id=1, source_target_pairs={{0,64},{8,72},{16,80},{24,88},{32,96},{40,104},{48,112},{56,120},{... | collective-permute-start | bytes 1572872 | tf_op jit(solution)/shard_map/ppermute | solution.py:119
  65.5 14.2 %collective-permute-start.16 = (bf16[512,512]{1,0:T(8,128)(2,1)S(1)}, bf16[512,512]{1,0:T(8,128)(2,1)S(1)}, u32[]{:S(2)}, u32[]{:S(2)}) collective-permute-start(bf16[512,512]{1,0:T(8,128)(2,1)S(1)} %collective-permute-done.15.refs_1_), channel_id=1, source_target_pairs={{0,448},{8,456},{16,464},{24,472},{32,480},{40,488},{48,496},{56,5... | collective-permute-start | bytes 1572872 | tf_op jit(solution)/shard_map/ppermute | solution.py:119
  67.4 42.7 %collective-permute-start.5 = (bf16[5,512,128]{2,1,0:T(8,128)(2,1)}, bf16[5,512,128]{2,1,0:T(8,128)(2,1)}, u32[]{:S(2)}, u32[]{:S(2)}) collective-permute-start(bf16[5,512,128]{2,1,0:T(8,128)(2,1)} %collective-permute-done.4.refs_0_), channel_id=1, source_target_pairs={{0,8},{8,16},{16,24},{24,32},{32,40},{40,48},{48,56},{56,0},{64,72... | collective-permute-start | bytes 1966088 | tf_op jit(solution)/shard_map/ppermute | solution.py:125
  73.2 29.3 %collective-permute-start.13 = (bf16[512,512]{1,0:T(8,128)(2,1)S(1)}, bf16[512,512]{1,0:T(8,128)(2,1)}, u32[]{:S(2)}, u32[]{:S(2)}) collective-permute-start(bf16[512,512]{1,0:T(8,128)(2,1)S(1)} %collective-permute-done.12.refs_2_), channel_id=1, source_target_pairs={{0,64},{8,72},{16,80},{24,88},{32,96},{40,104},{48,112},{56,120},{... | collective-permute-start | bytes 1572872 | tf_op jit(solution)/shard_map/ppermute | solution.py:119
  79.7 24.7 %collective-permute-start.17 = (bf16[512,512]{1,0:T(8,128)(2,1)S(1)}, bf16[512,512]{1,0:T(8,128)(2,1)}, u32[]{:S(2)}, u32[]{:S(2)}) collective-permute-start(bf16[512,512]{1,0:T(8,128)(2,1)S(1)} %collective-permute-done.16.refs_3_), channel_id=1, source_target_pairs={{0,448},{8,456},{16,464},{24,472},{32,480},{40,488},{48,496},{56,5... | collective-permute-start | bytes 1572872 | tf_op jit(solution)/shard_map/ppermute | solution.py:119
  81.7 34.3 %collective-permute-start.9 = (bf16[5,512,128]{2,1,0:T(8,128)(2,1)}, bf16[5,512,128]{2,1,0:T(8,128)(2,1)}, u32[]{:S(2)}, u32[]{:S(2)}) collective-permute-start(bf16[5,512,128]{2,1,0:T(8,128)(2,1)} %collective-permute-done.8.refs_1_), channel_id=1, source_target_pairs={{0,56},{8,0},{16,8},{24,16},{32,24},{40,32},{48,40},{56,48},{64,12... | collective-permute-start | bytes 1966088 | tf_op jit(solution)/shard_map/ppermute | solution.py:125
  83.6 53.5 %collective-permute-start.11 = (bf16[1,512,128]{2,1,0:T(8,128)(2,1)}, bf16[1,512,128]{2,1,0:T(8,128)(2,1)S(1)}, u32[]{:S(2)}, u32[]{:S(2)}) collective-permute-start(bf16[1,512,128]{2,1,0:T(8,128)(2,1)} %copy-done.2), channel_id=1, source_target_pairs={{56,320},{120,384},{184,448},{248,0},{312,64},{376,128},{440,192},... | collective-permute-start | bytes 393224 | tf_op jit(solution)/shard_map/ppermute | solution.py:202
  102.5 40.1 %collective-permute-start.14 = (bf16[512,512]{1,0:T(8,128)(2,1)}, bf16[512,512]{1,0:T(8,128)(2,1)S(1)}, u32[]{:S(2)}, u32[]{:S(2)}) collective-permute-start(bf16[512,512]{1,0:T(8,128)(2,1)} %collective-permute-done.13.refs_4_), channel_id=1, source_target_pairs={{0,64},{8,72},{16,80},{24,88},{32,96},{40,104},{48,112},{56,120},{... | collective-permute-start | bytes 1572872 | tf_op jit(solution)/shard_map/ppermute | solution.py:119
  104.4 38.2 %collective-permute-start.18 = (bf16[512,512]{1,0:T(8,128)(2,1)}, bf16[512,512]{1,0:T(8,128)(2,1)S(1)}, u32[]{:S(2)}, u32[]{:S(2)}) collective-permute-start(bf16[512,512]{1,0:T(8,128)(2,1)} %collective-permute-done.17.refs_5_), channel_id=1, source_target_pairs={{0,448},{8,456},{16,464},{24,472},{32,480},{40,488},{48,496},{56,5... | collective-permute-start | bytes 1572872 | tf_op jit(solution)/shard_map/ppermute | solution.py:119
  111.1 26.0 %collective-permute-start.6 = (bf16[3,512,128]{2,1,0:T(8,128)(2,1)S(1)}, bf16[3,512,128]{2,1,0:T(8,128)(2,1)S(1)}, u32[]{:S(2)}, u32[]{:S(2)}) collective-permute-start(bf16[3,512,128]{2,1,0:T(8,128)(2,1)S(1)} %slice.24), channel_id=1, source_target_pairs={{0,8},{8,16},{16,24},{24,32},{32,40},{40,48},{48,56},{56,0},{64,72... | collective-permute-start | bytes 1179656 | tf_op jit(solution)/shard_map/ppermute | solution.py:125
  116.9 20.2 %collective-permute-start.10 = (bf16[2,512,128]{2,1,0:T(8,128)(2,1)S(1)}, bf16[2,512,128]{2,1,0:T(8,128)(2,1)S(1)}, u32[]{:S(2)}, u32[]{:S(2)}) collective-permute-start(bf16[2,512,128]{2,1,0:T(8,128)(2,1)S(1)} %slice.25), channel_id=1, source_target_pairs={{0,56},{8,0},{16,8},{24,16},{32,24},{40,32},{48,40},{56,48},{64,12... | collective-permute-start | bytes 786440 | tf_op jit(solution)/shard_map/ppermute | solution.py:125
  143.7 4.6 %collective-permute-start.19 = (bf16[4,256,512]{2,1,0:T(8,128)(2,1)S(1)}, bf16[4,256,512]{2,1,0:T(8,128)(2,1)S(1)}, u32[]{:S(2)}, u32[]{:S(2)}) collective-permute-start(bf16[4,256,512]{2,1,0:T(8,128)(2,1)S(1)} %slice_bitcast_fusion), channel_id=1, source_target_pairs={{0,1},{1,0},{2,3},{3,2},{4,5},{5,4},{6,7},{7,6},{8,9},{9,8},{10,11... | collective-permute-start | bytes 3145736 | tf_op jit(solution)/shard_map/ppermute | solution.py:208
  (1 other events, 13.9 us)
